TPU v7x, 8 devices: a whole 2x2x1 slice. The times are simulated.
8 devices in a mesh: model: 2 (over z, y), data: 2 (over x), stage: 2 (over core).
Axes of the slice: x: 2, y: 2, z: 1, core: 2. Of those that a mesh axis runs over, the one named last changes fastest.
Arguments:
- w_up: float32 [2, 1280, 5120], P('stage', None, 'model')
- w_down: float32 [2, 5120, 1280], P('stage', 'model')
- m_up: float32 [2, 1280, 5120], P('stage', None, 'model')
- m_down: float32 [2, 5120, 1280], P('stage', 'model')
- v_up: float32 [2, 1280, 5120], P('stage', None, 'model')
- v_down: float32 [2, 5120, 1280], P('stage', 'model')
- g_up: float32 [2, 2, 1280, 5120], P('data', 'stage', None, 'model')
- g_down: float32 [2, 2, 5120, 1280], P('data', 'stage', 'model')
- acts_last: bfloat16 [2, 512, 1280], P('stage', 'data')
- grad_out: bfloat16 [512, 1280], P('data')
- x_next: bfloat16 [3, 512, 1280], P(None, 'data')
- learn_rate: float32 [1], replicated
- max_norm: float32 [1], replicated
Outputs:
- output 1: float32 [2, 1280, 5120], P('stage', None, 'model')
- output 2: float32 [2, 5120, 1280], P('stage', 'model')
- output 3: float32 [2, 1280, 5120], P('stage', None, 'model')
- output 4: float32 [2, 5120, 1280], P('stage', 'model')
- output 5: float32 [2, 1280, 5120], P('stage', None, 'model')
- output 6: float32 [2, 5120, 1280], P('stage', 'model')
- output 7: bfloat16 [3, 512, 1280], P(None, 'data')
All inputs are finite; a program needn't handle non-finite values.
Results may differ from a plain program's by a relative error of at most 0.00703998.
Values are sent between devices in bfloat16 or wider.
A program may use at most 1 GiB of HBM per device.

v0:
```python
import jax
import jax.numpy as jnp
from jax import lax
from jax.sharding import PartitionSpec as P

ADAM_STEP = 10
BETA_ONE = 0.9
BETA_TWO = 0.95
ADAM_EPS = 1e-8
WEIGHT_DECAY = 0.1
NORM_EPS = 1e-6
CONTRACT_LAST = (((1,), (1,)), ((), ()))
CONTRACT_FIRST = (((0,), (0,)), ((), ()))


def gelu_vjp(pre_act, upstream):
    pull_back = jax.vjp(jax.nn.gelu, pre_act)[1]
    return pull_back(upstream)[0]


def adamw_update(weight, moment_one, moment_two, grad_step, step_rate):
    mom_new = BETA_ONE * moment_one + (1.0 - BETA_ONE) * grad_step
    sec_new = BETA_TWO * moment_two + (1.0 - BETA_TWO) * grad_step * grad_step
    one_corr = 1.0 - BETA_ONE ** ADAM_STEP
    two_corr = 1.0 - BETA_TWO ** ADAM_STEP
    direction = (mom_new / one_corr) / (jnp.sqrt(sec_new / two_corr) + ADAM_EPS)
    weight_new = weight - step_rate * (direction + WEIGHT_DECAY * weight)
    return weight_new, mom_new, sec_new


def solution(mesh):
    n_stage = mesh.shape['stage']
    n_data = mesh.shape['data']
    down_perm = [(sender, sender - 1) for sender in range(1, n_stage)]
    up_perm = [(sender, sender + 1) for sender in range(n_stage - 1)]
    up_spec = P('stage', None, 'model')
    down_spec = P('stage', 'model', None)
    row_spec = P(None, 'data', None)
    in_specs = (up_spec, down_spec, up_spec, down_spec, up_spec, down_spec, P('data', 'stage', None, 'model'), P('data', 'stage', 'model', None), P('stage', 'data', None), P('data', None), row_spec, P(None), P(None))
    out_specs = (up_spec, down_spec, up_spec, down_spec, up_spec, down_spec, row_spec)

    def device_step(w_up, w_down, m_up, m_down, v_up, v_down, g_up, g_down, acts_last, grad_out, x_next, learn_rate, max_norm):
        stage_id = lax.axis_index('stage')
        acts_in = acts_last[0]
        up_bf = w_up[0].astype(jnp.bfloat16)
        down_bf = w_down[0].astype(jnp.bfloat16)
        row_count, d_model = acts_in.shape
        ff_local = up_bf.shape[1]
        n_micro = x_next.shape[0]

        def back_core(upstream):
            pre_act = jnp.dot(acts_in, up_bf, preferred_element_type=jnp.float32)
            hidden = jax.nn.gelu(pre_act).astype(jnp.bfloat16)
            grad_hid = lax.dot_general(upstream, down_bf, CONTRACT_LAST, preferred_element_type=jnp.float32)
            grad_pre = gelu_vjp(pre_act, grad_hid).astype(jnp.bfloat16)
            return hidden, grad_pre

        def back_send(state_in):
            hidden, grad_pre = back_core(state_in[0])
            part_sum = lax.dot_general(grad_pre, up_bf, CONTRACT_LAST, preferred_element_type=jnp.float32)
            return hidden, grad_pre, state_in[0], part_sum

        def hold_send(state_in):
            return state_in[1], state_in[2], state_in[3], jnp.zeros((row_count, d_model), jnp.float32)

        def back_keep(state_in):
            hidden, grad_pre = back_core(state_in[0])
            return hidden, grad_pre, state_in[0]

        def hold_keep(state_in):
            return state_in[1], state_in[2], state_in[3]

        upstream = grad_out
        keep_hid = jnp.zeros((row_count, ff_local), jnp.bfloat16)
        keep_pre = jnp.zeros((row_count, ff_local), jnp.bfloat16)
        keep_up = grad_out
        for step_idx in range(n_stage - 1):
            active = stage_id == n_stage - 1 - step_idx
            keep_hid, keep_pre, keep_up, part_sum = lax.cond(active, back_send, hold_send, (upstream, keep_hid, keep_pre, keep_up))
            summed = lax.psum(part_sum, 'model')
            grad_in = (upstream.astype(jnp.float32) + summed).astype(jnp.bfloat16)
            upstream = lax.ppermute(grad_in, 'stage', down_perm)
        keep_hid, keep_pre, keep_up = lax.cond(stage_id == 0, back_keep, hold_keep, (upstream, keep_hid, keep_pre, keep_up))

        grad_down = lax.dot_general(keep_hid, keep_up, CONTRACT_FIRST, preferred_element_type=jnp.float32)
        grad_up = lax.dot_general(acts_in, keep_pre, CONTRACT_FIRST, preferred_element_type=jnp.float32)
        mean_up = lax.psum(g_up[0, 0] + grad_up, 'data') / n_data
        mean_down = lax.psum(g_down[0, 0] + grad_down, 'data') / n_data
        local_sq = lax.psum(jnp.sum(mean_up * mean_up) + jnp.sum(mean_down * mean_down), 'model')
        norm_acc = local_sq
        for step_idx in range(n_stage - 1):
            incoming = lax.ppermute(norm_acc, 'stage', down_perm)
            norm_acc = jnp.where(stage_id == n_stage - 2 - step_idx, local_sq + incoming, norm_acc)
        clip_cur = jnp.minimum(1.0, max_norm[0] / (jnp.sqrt(norm_acc) + NORM_EPS))
        step_rate = learn_rate[0]

        def apply_update(state_in):
            clip_now = state_in[1]
            up_w, up_m, up_v = adamw_update(w_up[0], m_up[0], v_up[0], clip_now * mean_up, step_rate)
            down_w, down_m, down_v = adamw_update(w_down[0], m_down[0], v_down[0], clip_now * mean_down, step_rate)
            return (up_w, down_w, up_m, down_m, up_v, down_v, up_w.astype(jnp.bfloat16), down_w.astype(jnp.bfloat16))

        def keep_state(state_in):
            return state_in[0]

        def fwd_local(state_in):
            acts_cur, up_new_bf, down_new_bf = state_in
            pre_act = jnp.dot(acts_cur, up_new_bf, preferred_element_type=jnp.float32)
            hidden = jax.nn.gelu(pre_act).astype(jnp.bfloat16)
            return jnp.dot(hidden, down_new_bf, preferred_element_type=jnp.float32)

        def fwd_idle(state_in):
            return jnp.zeros((row_count, d_model), jnp.float32)

        opt_state = (w_up[0], w_down[0], m_up[0], m_down[0], v_up[0], v_down[0], up_bf, down_bf)
        acts_cur = x_next[0]
        finished = []
        for step_idx in range(n_micro + n_stage - 1):
            if step_idx < n_stage:
                opt_state = lax.cond(stage_id == step_idx, apply_update, keep_state, (opt_state, clip_cur))
            if 0 < step_idx < n_micro:
                acts_cur = jnp.where(stage_id == 0, x_next[step_idx], acts_cur)
            micro_idx = step_idx - stage_id
            is_busy = (micro_idx >= 0) & (micro_idx < n_micro)
            branch = lax.cond(is_busy, fwd_local, fwd_idle, (acts_cur, opt_state[6], opt_state[7]))
            summed = lax.psum(branch, 'model')
            acts_out = (acts_cur.astype(jnp.float32) + summed).astype(jnp.bfloat16)
            if step_idx >= n_stage - 1:
                finished.append(acts_out)
            if step_idx < n_micro + n_stage - 2:
                acts_cur = lax.ppermute(acts_out, 'stage', up_perm)
            if step_idx < n_stage - 1:
                clip_cur = lax.ppermute(clip_cur, 'stage', up_perm)
        y_local = jnp.stack(finished)
        y_next = lax.psum(jnp.where(stage_id == n_stage - 1, y_local, jnp.zeros_like(y_local)), 'stage')
        return (opt_state[0][None], opt_state[1][None], opt_state[2][None], opt_state[3][None], opt_state[4][None], opt_state[5][None], y_next)

    return jax.shard_map(device_step, mesh=mesh, in_specs=in_specs, out_specs=out_specs, check_vma=False)
```

profile of v0, /device:TPU:0, one launch (start us, length us, event | category | flops | bytes accessed | tf_op | source)
XLA Modules:
  0.0 1160.2 jit_solution(15392673278272666804)
XLA Ops:
  7.2 8.2 bitcast_convert_fusion.1
  15.4 8.1 bitcast_convert_fusion
  23.5 1.3 conditional.8
  23.5 0.1 broadcast.148
  23.6 1.1 broadcast.148.clone
  24.7 0.1 broadcast.149
  24.8 1.0 copy-done.3
  25.9 0.0 all-reduce.21.cloned.1.call-start
  25.9 53.6 %all-reduce.9.cloned.1.call-done = f32[256,1280]{1,0:T(8,128)} async-done(((f32[256,1280]{1,0:T(8,128)}), f32[256,1280]{1,0:T(8,128)}) %all-reduce.9.cloned.1.call-update) | async-done | bytes 1310736 | tf_op jit(solution)/shard_map/psum | solution.py:80
  79.5 1.4 add_convert_fusion.4
  80.9 1.3 collective-permute-start
  82.2 13.9 %copy.20 = f32[1,1,1280,2560]{2,3,1,0:T(8,128)} copy(f32[1,1,1280,2560]{3,2,1,0:T(8,128)} %param.35) | data formatting | bytes 26214400 | tf_op args[6]
  96.1 9.5 conditional.9
  96.1 4.9 fusion.120
  101.1 4.4 fusion.13
  105.7 12.5 %bitcast_add_fusion.4 = f32[1280,2560]{0,1:T(8,128)} fusion(f32[1,1,1280,2560]{2,3,1,0:T(8,128)} %copy.20, bf16[256,2560]{1,0:T(8,128)(2,1)} %get-tuple-element.227, bf16[1,256,1280]{2,1,0:T(8,128)(2,1)} %param.37), kind=kOutput, calls=%fused_computation.125 | convolution fusion | flops 1680998400 | bytes 28180480 | tf_op jit(solution)/shard_map/dot_general | solution.py:86
  118.3 6.9 convolution_add_fusion
  125.2 0.0 all-reduce.11.cloned.1.call-start
  126.0 0.7 copy-done.8
  126.7 0.9 slice_bitcast_fusion
  127.6 572.3 %all-reduce.21.cloned.1.call-done = (f32[1280,2560]{0,1:T(8,128)}, f32[2560,1280]{1,0:T(8,128)}) async-done(((f32[1280,2560]{0,1:T(8,128)}, f32[2560,1280]{1,0:T(8,128)}), (f32[1280,2560]{0,1:T(8,128)}, f32[2560,1280]{1,0:T(8,128)})) %all-reduce.21.cloned.1.call-update) | async-done | bytes 26214416 | tf_op jit(solution)/shard_map/psum | solution.py:87
  699.8 13.5 %broadcast_multiply_fusion.1 = (f32[1280,2560]{0,1:T(8,128)}, f32[]{:T(128)}) fusion(f32[1280,2560]{0,1:T(8,128)} %get-tuple-element.292), kind=kLoop, calls=%fused_computation.129 | loop fusion | flops 9830399 | bytes 26214404 | tf_op jit(solution)/shard_map/div | solution.py:87
  713.3 13.4 %broadcast_multiply_fusion = (f32[2560,1280]{1,0:T(8,128)}, f32[]{:T(128)}) fusion(f32[2560,1280]{1,0:T(8,128)} %get-tuple-element.293), kind=kLoop, calls=%fused_computation.128 | loop fusion | flops 9830399 | bytes 26214404 | tf_op jit(solution)/shard_map/div | solution.py:88
  728.0 5.4 psum.66
  733.5 1.3 collective-permute-start.1
  734.7 1.7 collective-permute-done.1
  738.5 90.8 %conditional.10 = (f32[1280,2560]{1,0:T(8,128)}, f32[2560,1280]{1,0:T(8,128)}, f32[1280,2560]{1,0:T(8,128)}, f32[2560,1280]{1,0:T(8,128)}, f32[1280,2560]{1,0:T(...) conditional(s32[]{:T(128)} %convert_element_type.93, ...), branch_computations={%region_10.11_spmd, %region_11.12_spmd} | conditional | flops 111411200 | bytes 222822480 | solution.py:120
  746.1 13.9 %copy.21 = f32[1280,2560]{1,0:T(8,128)} copy(f32[1280,2560]{0,1:T(8,128)} %get-tuple-element.276) | data formatting | bytes 26214400 | tf_op jit(solution)/shard_map
  760.0 34.4 %fusion.106 = (bf16[1280,2560]{1,0:T(8,128)(2,1)}, f32[1280,2560]{1,0:T(8,128)}, f32[1280,2560]{1,0:T(8,128)}, f32[1280,2560]{1,0:T(8,128)}) fusion(f32[]{:T(128)} %get-tuple-element.162, f32[1,1280,2560]{2,1,0:T(8,128)} %get-tuple-element.161, f32[1280,2560]{1,0:T(8,128)} %copy.21, f32[]{:T(128)} %get-tuple-element.164, ...), kind=kLoop, calls=%fused_computation.144 | loop fusion | flops 55705600 | bytes 98304008 | tf_op jit(solution)/shard_map/cond/branch_1_fun/convert_element_type | solution.py:101
  794.4 34.9 %fusion.104 = (bf16[2560,1280]{1,0:T(8,128)(2,1)}, f32[2560,1280]{1,0:T(8,128)}, f32[2560,1280]{1,0:T(8,128)}, f32[2560,1280]{1,0:T(8,128)}) fusion(f32[]{:T(128)} %get-tuple-element.162, f32[1,2560,1280]{2,1,0:T(8,128)} %get-tuple-element.167, f32[2560,1280]{1,0:T(8,128)} %get-tuple-element.169, f32[]{:T(128)} %get-tuple-element.164, ...), kind=kLoop, calls=%fused_computation.143 | loop fusion | flops 55705600 | bytes 98304008 | tf_op jit(solution)/shard_map/cond/branch_1_fun/convert_element_type | solution.py:101
  829.3 8.6 conditional.12
  829.3 8.6 fusion.38
  838.0 1.0 copy-done.4
  839.1 41.1 %all-reduce.11.cloned.1.call-done = f32[256,1280]{1,0:T(8,128)} async-done(((f32[256,1280]{1,0:T(8,128)}), f32[256,1280]{1,0:T(8,128)}) %all-reduce.11.cloned.1.call-update) | async-done | bytes 1310736 | tf_op jit(solution)/shard_map/psum | solution.py:126
  880.2 1.4 add_convert_fusion.3
  881.7 1.5 collective-permute-start.3
  883.2 2.1 collective-permute-start.2
  885.3 0.2 conditional.11
  885.5 0.9 bitcast_select_fusion.1
  886.4 8.6 conditional.13
  886.4 8.6 fusion.56
  895.0 1.0 copy-done.5
  896.1 0.3 all-reduce.15.cloned.1.call-start
  896.4 125.7 %all-reduce.13.cloned.1.call-done = f32[256,1280]{1,0:T(8,128)} async-done(((f32[256,1280]{1,0:T(8,128)}), f32[256,1280]{1,0:T(8,128)}) %all-reduce.13.cloned.1.call-update) | async-done | bytes 1310736 | tf_op jit(solution)/shard_map/psum | solution.py:126
  1022.1 1.6 add_convert_fusion.2
  1023.7 1.5 collective-permute-start.4
  1025.2 1.7 collective-permute-done.4
  1026.9 0.9 bitcast_select_fusion
  1027.8 8.6 conditional.14
  1027.8 8.6 fusion.74
  1036.5 1.0 copy-done.6
  1037.6 40.1 %all-reduce.15.cloned.1.call-done = f32[256,1280]{1,0:T(8,128)} async-done(((f32[256,1280]{1,0:T(8,128)}), f32[256,1280]{1,0:T(8,128)}) %all-reduce.15.cloned.1.call-update) | async-done | bytes 1310736 | tf_op jit(solution)/shard_map/psum | solution.py:126
  1077.7 1.6 add_convert_fusion.1
  1079.3 1.5 collective-permute-start.5
  1080.8 1.7 collective-permute-done.5
  1082.5 0.1 conditional.15
  1082.5 0.1 broadcast.203
  1082.6 1.0 copy-done.7
  1083.7 0.0 all-reduce.19.cloned.1.call-start
  1083.7 48.5 %all-reduce.17.cloned.1.call-done = f32[256,1280]{1,0:T(8,128)} async-done(((f32[256,1280]{1,0:T(8,128)}), f32[256,1280]{1,0:T(8,128)}) %all-reduce.17.cloned.1.call-update) | async-done | bytes 1310736 | tf_op jit(solution)/shard_map/psum | solution.py:126
  1132.3 1.4 fusion.102
  1133.7 1.5 maximum_select_fusion
  1135.3 14.9 %all-reduce.19.cloned.1.call-done = bf16[3,256,1280]{2,1,0:T(8,128)(2,1)} async-done(((bf16[3,256,1280]{2,1,0:T(8,128)(2,1)}), bf16[3,256,1280]{2,1,0:T(8,128)(2,1)}) %all-reduce.19.cloned.1.call-update) | async-done | bytes 1966096 | tf_op jit(solution)/shard_map/psum | solution.py:135
  1150.2 2.9 copy.92
  (39 shorter events, 0.3 us)
Async XLA Ops:
  7.2 72.3 %all-reduce.9.cloned.1.call-start = ((), (), s32[]{:S(2)}) async-start(), calls=%async_computation | async-start | bytes 2621440 | tf_op jit(solution)/shard_map/psum | solution.py:80
  15.4 8.1 copy-start.2
  24.8 1.1 copy-start.3
  25.9 674.0 %all-reduce.21.cloned.1.call-start = ((), (), s32[]{:S(2)}) async-start(), calls=%async_computation.6 | async-start | bytes 52428800 | tf_op jit(solution)/shard_map/psum | solution.py:87
  80.9 15.2 %collective-permute-start = (bf16[256,1280]{1,0:T(8,128)(2,1)S(1)}, bf16[256,1280]{1,0:T(8,128)(2,1)S(1)}, u32[]{:S(2)}, u32[]{:S(2)}) collective-permute-start(bf16[256,1280]{1,0:T(8,128)(2,1)S(1)} %add_convert_fusion.4), channel_id=1, source_target_pairs={{1,0},{3,2},{5,4},{7,6}} | collective-permute-start | bytes 1966088 | tf_op jit(solution)/shard_map/ppermute | solution.py:82
  96.1 4.9 copy-start.1
  96.1 4.9 copy-start.12
  105.6 12.6 %slice-start = ((s8[13107200]{0:T(1024)(128)(4,1)}), s8[4194304]{0:T(1024)(128)(4,1)S(1)}, s32[]{:S(2)}) async-start(s8[13107200]{0:T(1024)(128)(4,1)} %bitcast.159), calls=%async_computation.7 | async-start | bytes 8388608
  105.7 12.6 %slice-start.1 = ((s8[13107200]{0:T(1024)(128)(4,1)}), s8[4194304]{0:T(1024)(128)(4,1)S(1)}, s32[]{:S(2)}) async-start(s8[13107200]{0:T(1024)(128)(4,1)} %bitcast.159), calls=%async_computation.8 | async-start | bytes 8388608
  105.7 12.6 %slice-start.2 = ((s8[13107200]{0:T(1024)(128)(4,1)}), s8[4194304]{0:T(1024)(128)(4,1)S(1)}, s32[]{:S(2)}) async-start(s8[13107200]{0:T(1024)(128)(4,1)} %bitcast.159), calls=%async_computation.9 | async-start | bytes 8388608
  105.7 12.6 %slice-start.3 = ((s8[13107200]{0:T(1024)(128)(4,1)}), s8[524288]{0:T(1024)(128)(4,1)S(1)}, s32[]{:S(2)}) async-start(s8[13107200]{0:T(1024)(128)(4,1)} %bitcast.159), calls=%async_computation.10 | async-start | bytes 1048576
  125.1 1.6 copy-start.8
  125.2 755.1 %all-reduce.11.cloned.1.call-start = ((), (), s32[]{:S(2)}) async-start(), calls=%async_computation.1 | async-start | bytes 2621440 | tf_op jit(solution)/shard_map/psum | solution.py:126
  733.5 3.0 collective-permute-start.1
  837.9 1.1 copy-start.4
  839.0 183.1 %all-reduce.13.cloned.1.call-start = ((), (), s32[]{:S(2)}) async-start(), calls=%async_computation.2 | async-start | bytes 2621440 | tf_op jit(solution)/shard_map/psum | solution.py:126
  881.7 3.8 collective-permute-start.3
  883.2 2.1 collective-permute-start.2
  895.0 1.1 copy-start.5
  896.1 181.6 %all-reduce.15.cloned.1.call-start = ((), (), s32[]{:S(2)}) async-start(), calls=%async_computation.3 | async-start | bytes 2621440 | tf_op jit(solution)/shard_map/psum | solution.py:126
  1023.7 4.1 copy-start.9
  1023.7 3.2 collective-permute-start.4
  1036.5 1.1 copy-start.6
  1037.5 94.7 %all-reduce.17.cloned.1.call-start = ((), (), s32[]{:S(2)}) async-start(), calls=%async_computation.4 | async-start | bytes 2621440 | tf_op jit(solution)/shard_map/psum | solution.py:126
  1079.3 3.2 collective-permute-start.5
  1082.5 51.2 %copy-start.10 = (bf16[256,1280]{1,0:T(8,128)(2,1)S(1)}, bf16[256,1280]{1,0:T(8,128)(2,1)}, u32[]{:S(2)}) copy-start(bf16[256,1280]{1,0:T(8,128)(2,1)} %copy-done.9) | copy-start | bytes 1966084
  1082.6 1.1 copy-start.7
  1083.7 66.5 %all-reduce.19.cloned.1.call-start = ((), (), s32[]{:S(2)}) async-start(), calls=%async_computation.5 | async-start | bytes 3932160 | tf_op jit(solution)/shard_map/psum | solution.py:135
Sparse Core Ops, SparseCore 0:
  26.0 53.4 all-reduce.8
  125.3 574.5 all-reduce.20
  839.1 41.0 all-reduce.10
  896.2 125.8 all-reduce.12
  1037.7 39.9 all-reduce.14
  1083.8 48.4 all-reduce.16
  1135.4 14.7 all-reduce.18
where the time goes:
time: 1170 us; the launch traced here: 1160 us
  waiting for transfers between devices  901 us (77%)
  other arithmetic  123 us (11%)
  matrix products  54.6 us (5%)
  local copies, waits for them, and re-layouts  39.1 us (3%)
  between operations  18.7 us (2%)
    psum x1, waiting for transfers between devices, device_step(): mean_up = lax.psum(g_up[0, 0] + grad_up, 'data') / n_data  572 us
    psum x4, waiting for transfers between devices, device_step(): summed = lax.psum(branch, 'model')  256 us
    psum x1, waiting for transfers between devices, device_step(): summed = lax.psum(part_sum, 'model')  53.6 us
    convert_element_type x1, other arithmetic, apply_update(): down_w.astype(jnp.bfloat16)  34.9 us
    convert_element_type x1, other arithmetic, apply_update(): up_w.astype(jnp.bfloat16)  34.4 us
    dot_general x3, matrix products, fwd_local(): return jnp.dot(hidden, down_new_bf, preferred_element_type=jnp.float32)  25.9 us
  transfers between devices with their start and end apart: 13, of which 10 were waited for; matrix products, arithmetic and copies ran while one was open for 1% of the time, Pallas kernels for 0%

commit v1 on v0

v1 whole, which is shorter than its diff:
```python
import functools

import jax
import jax.numpy as jnp
from jax import lax
from jax.experimental import pallas as pl
from jax.experimental.pallas import tpu as pltpu
from jax.sharding import PartitionSpec as P

ADAM_STEP = 10
BETA_ONE = 0.9
BETA_TWO = 0.95
ADAM_EPS = 1e-8
WEIGHT_DECAY = 0.1
NORM_EPS = 1e-6
ONE_CORR = 1.0 - BETA_ONE ** ADAM_STEP
TWO_CORR = 1.0 - BETA_TWO ** ADAM_STEP
GELU_A = 0.7978845608028654
GELU_B = 0.044715
NT = (((1,), (1,)), ((), ()))
TN = (((0,), (0,)), ((), ()))
MESH = pl.DeviceIdType.MESH
VMEM_MAX = 67_043_328
CHUNK = 256
F32 = jnp.float32
BF16 = jnp.bfloat16


def gelu_parts(z):
    t = jnp.tanh(GELU_A * (z + GELU_B * (z * z * z)))
    return t, z * (0.5 * (1.0 + t))


def gelu_slope(z, t):
    return 0.5 * (1.0 + t) + 0.5 * z * (1.0 - t * t) * (GELU_A * (1.0 + 3.0 * GELU_B * z * z))


def dot(a, b, dims=(((1,), (0,)), ((), ()))):
    return lax.dot_general(a, b, dims, preferred_element_type=F32)


def positions():
    return lax.axis_index("model"), lax.axis_index("data"), lax.axis_index("stage")


def entry_barrier(peers):
    barrier = pltpu.get_barrier_semaphore()
    for peer in peers:
        pl.semaphore_signal(barrier, inc=1, device_id=peer, device_id_type=MESH)
    pl.semaphore_wait(barrier, len(peers))


def remote(src, dst, send, recv, peer):
    return pltpu.make_async_remote_copy(src_ref=src, dst_ref=dst, send_sem=send, recv_sem=recv, device_id=peer, device_id_type=MESH)


def grad_kernel(n_chunk, width, w1, w2, g1, g2, acts, dy, max_norm, gb1, gb2, clip,
                gs1, gs2, gr1, gr2, w1b, w2b, gvec, gout, part, part_in, sq1, sq2, sq_out, sq_in,
                w_sem, g_sem, send1, send2, recv1, recv2, out1, out2, part_sem, gvec_sem, sq_send, sq_recv):
    m, d, s = positions()
    peer_x = (m, 1 - d, s)
    peer_y = (1 - m, d, s)
    peer_c = (m, d, 1 - s)
    peer_d = (1 - m, d, 1 - s)

    def loads(j):
        slot = lax.rem(j, 2)
        cols = pl.ds(pl.multiple_of(j * width, width), width)
        return (pltpu.make_async_copy(w1.at[:, cols], w1b.at[slot], w_sem.at[0, slot]),
                pltpu.make_async_copy(w2.at[cols, :], w2b.at[slot], w_sem.at[1, slot]),
                pltpu.make_async_copy(g2.at[cols, :], gs2.at[j], g_sem.at[0, slot]),
                pltpu.make_async_copy(g1.at[:, cols], gs1.at[j], g_sem.at[1, slot]))

    for first in (0, 1):
        for copy in loads(first):
            copy.start()
    entry_barrier((peer_x, peer_y, peer_c, peer_d))

    is_last = s == 1
    hand_over = remote(gout, gvec, gvec_sem.at[0], gvec_sem.at[1], peer_c)
    swap_part = remote(part, part_in, part_sem.at[0], part_sem.at[1], peer_y)

    @pl.when(is_last)
    def _():
        gvec[...] = dy[...]
        part[...] = jnp.zeros_like(part)

    @pl.when(jnp.logical_not(is_last))
    def _():
        hand_over.wait_recv()

    def send_two(j):
        return remote(gs2.at[j], gr2.at[j], send2.at[j], recv2.at[j], peer_x)

    def send_one(j):
        return remote(gs1.at[j], gr1.at[j], send1.at[j], recv1.at[j], peer_x)

    @pl.loop(0, n_chunk)
    def _(j):
        slot = lax.rem(j, 2)
        copies = loads(j)
        copies[0].wait()
        up = w1b[slot].astype(BF16)
        rows = acts[...]
        grad = gvec[...]
        z = dot(rows, up)
        t, act = gelu_parts(z)
        hid = act.astype(BF16)
        copies[2].wait()
        gs2[j] += dot(hid, grad, TN)
        send_two(j).start()
        copies[1].wait()
        grad_hid = dot(grad, w2b[slot].astype(BF16), NT)
        grad_pre = (gelu_slope(z, t) * grad_hid).astype(BF16)
        copies[3].wait()
        gs1[j] += dot(rows, grad_pre, TN)
        send_one(j).start()

        @pl.when(is_last)
        def _():
            part[...] += dot(grad_pre, up, NT)

        @pl.when(j + 2 < n_chunk)
        def _():
            for copy in loads(j + 2):
                copy.start()

    @pl.when(is_last)
    def _():
        swap_part.start()
        swap_part.wait()
        gout[...] = (gvec[...].astype(F32) + (part[...] + part_in[...])).astype(BF16)
        hand_over.start()

    sq1[...] = jnp.zeros_like(sq1)
    sq2[...] = jnp.zeros_like(sq2)

    def write_two(j):
        return pltpu.make_async_copy(gr2.at[j], gb2.at[j], out2.at[j])

    def write_one(j):
        return pltpu.make_async_copy(gr1.at[j], gb1.at[j], out1.at[j])

    @pl.loop(0, n_chunk)
    def _(j):
        send_two(j).wait_recv()
        mean = (gs2[j] + gr2[j]) * 0.5
        gr2[j] = mean
        sq2[...] += jnp.sum((mean * mean).reshape(-1, 8, mean.shape[1]), axis=0)
        write_two(j).start()
        send_one(j).wait_recv()
        mean = (gs1[j] + gr1[j]) * 0.5
        gr1[j] = mean
        sq1[...] += jnp.sum((mean * mean).reshape(-1, 8, mean.shape[1]), axis=0)
        write_one(j).start()

    sq_out[...] = jnp.full(sq_out.shape, jnp.sum(sq1[...]) + jnp.sum(sq2[...]), F32)
    mine = 2 * m + s
    others = ((peer_y, 2 * (1 - m) + s), (peer_c, 2 * m + 1 - s), (peer_d, 2 * (1 - m) + 1 - s))
    shares = [remote(sq_out, sq_in.at[mine], sq_send.at[k], sq_recv.at[mine], peer) for k, (peer, _) in enumerate(others)]
    for copy in shares:
        copy.start()
    sq_in[mine] = sq_out[...]
    for peer, index in others:
        remote(sq_out, sq_in.at[index], sq_send.at[0], sq_recv.at[index], peer).wait_recv()
    total = (sq_in[0] + sq_in[1]) + (sq_in[2] + sq_in[3])
    clip[...] = jnp.minimum(1.0, max_norm[0] / (jnp.sqrt(total) + NORM_EPS))

    for copy in shares:
        copy.wait_send()

    @pl.when(is_last)
    def _():
        hand_over.wait_send()

    @pl.loop(0, n_chunk)
    def _(j):
        send_two(j).wait_send()
        send_one(j).wait_send()
        write_two(j).wait()
        write_one(j).wait()


def update_kernel(clip, rate, w1, m1, v1, gb1, w2, m2, v2, gb2, x,
                  nw1, nw2, nm1, nm2, nv1, nv2, wb1, wb2, acc):
    s = lax.axis_index("stage")
    j = pl.program_id(0)
    scale = clip[0, 0]
    step_rate = rate[0]

    def adamw(w, mom, sec, mean):
        grad = scale * mean
        mom_new = BETA_ONE * mom + (1.0 - BETA_ONE) * grad
        sec_new = BETA_TWO * sec + (1.0 - BETA_TWO) * grad * grad
        direction = (mom_new / ONE_CORR) / (jnp.sqrt(sec_new / TWO_CORR) + ADAM_EPS)
        return w - step_rate * (direction + WEIGHT_DECAY * w), mom_new, sec_new

    a, b, c = adamw(w1[...], m1[...], v1[...], gb1[...])
    nw1[...] = a
    nm1[...] = b
    nv1[...] = c
    wb1[...] = a.astype(BF16)
    a, b, c = adamw(w2[...], m2[...], v2[...], gb2[...])
    nw2[...] = a
    nm2[...] = b
    nv2[...] = c
    wb2[...] = a.astype(BF16)

    @pl.when(j == 0)
    def _():
        acc[...] = jnp.zeros_like(acc)

    @pl.when(s == 0)
    def _():
        hid = gelu_parts(dot(x[...], wb1[...]))[1].astype(BF16)
        acc[...] += dot(hid, wb2[...])


def forward_kernel(n_chunk, n_micro, half, acc, x, wb1, wb2, y,
                   w1, w2, first_in, own_half, act, peer_half, part, part_in,
                   w_sem, a_send, a_recv, o_send, o_recv, p_send, p_recv, y_send, y_recv, f_send, f_recv):
    m, d, s = positions()
    peer_y = (1 - m, d, s)
    peer_c = (m, d, 1 - s)
    peer_d = (1 - m, d, 1 - s)
    entry_barrier((peer_y, peer_c, peer_d))
    mine = pl.ds(pl.multiple_of(m * half, half), half)
    theirs = pl.ds(pl.multiple_of((1 - m) * half, half), half)

    def send_first(k):
        return remote(acc.at[k, theirs, :], first_in.at[k], a_send.at[k], a_recv.at[k], peer_y)

    def give_core(k):
        return remote(own_half.at[k], act.at[k, mine, :], o_send.at[0, k], o_recv.at[0, k], peer_c)

    def give_diag(k):
        return remote(own_half.at[k], act.at[k, mine, :], o_send.at[1, k], o_recv.at[1, k], peer_d)

    def send_part(k):
        return remote(part.at[k, theirs, :], part_in.at[k], p_send.at[k], p_recv.at[k], peer_y)

    def swap_y(k):
        return remote(own_half.at[k], peer_half.at[k], y_send.at[0, k], y_recv.at[0, k], peer_y)

    def give_own(k):
        return remote(own_half.at[k], y.at[k, mine, :], y_send.at[1, k], y_recv.at[1, k], peer_c)

    def pass_on(k):
        return remote(peer_half.at[k], y.at[k, theirs, :], f_send.at[k], f_recv.at[k], peer_c)

    @pl.when(s == 0)
    def _():
        send_first(0).start()
        for k in range(n_micro):
            if k + 1 < n_micro:
                send_first(k + 1).start()
            send_first(k).wait_recv()
            out = x[k, mine, :].astype(F32) + (acc[k, mine, :] + first_in[k])
            own_half[k] = out.astype(BF16)
            give_core(k).start()
            give_diag(k).start()
        for k in range(n_micro):
            give_own(k).wait_recv()
            pass_on(k).wait_recv()
        for k in range(n_micro):
            send_first(k).wait_send()
            give_core(k).wait_send()
            give_diag(k).wait_send()

    @pl.when(s == 1)
    def _():
        cp1 = pltpu.make_async_copy(wb1, w1, w_sem.at[0])
        cp2 = pltpu.make_async_copy(wb2, w2, w_sem.at[1])
        cp1.start()
        cp2.start()
        cp1.wait()
        cp2.wait()

        def finish(k):
            send_part(k).wait_recv()
            out = act[k, mine, :].astype(F32) + (part[k, mine, :] + part_in[k])
            own_half[k] = out.astype(BF16)
            swap_y(k).start()
            give_own(k).start()
            y[k, mine, :] = own_half[k]

        for k in range(n_micro):
            give_core(k).wait_recv()
            give_diag(k).wait_recv()
            part[k] = jnp.zeros_like(part[k])

            @pl.loop(0, n_chunk)
            def _(j):
                hid = gelu_parts(dot(act[k], w1[j]))[1].astype(BF16)
                part[k] += dot(hid, w2[j])

            send_part(k).start()
            if k > 0:
                finish(k - 1)
        finish(n_micro - 1)
        for k in range(n_micro):
            swap_y(k).wait_recv()
            pass_on(k).start()
            y[k, theirs, :] = peer_half[k]
        for k in range(n_micro):
            send_part(k).wait_send()
            swap_y(k).wait_send()
            give_own(k).wait_send()
            pass_on(k).wait_send()


def solution(mesh):
    up_spec = P('stage', None, 'model')
    down_spec = P('stage', 'model', None)
    row_spec = P(None, 'data', None)
    in_specs = (up_spec, down_spec, up_spec, down_spec, up_spec, down_spec, P('data', 'stage', None, 'model'), P('data', 'stage', 'model', None), P('stage', 'data', None), P('data', None), row_spec, P(None), P(None))
    out_specs = (up_spec, down_spec, up_spec, down_spec, up_spec, down_spec, row_spec)

    def device_step(w_up, w_down, m_up, m_down, v_up, v_down, g_up, g_down, acts_last, grad_out, x_next, learn_rate, max_norm):
        d_model, ff = w_up.shape[1:]
        rows = grad_out.shape[0]
        n_micro = x_next.shape[0]
        width = CHUNK
        n_chunk = ff // width
        half = rows // 2
        hbm = pl.BlockSpec(memory_space=pl.ANY)
        vmem = pl.BlockSpec(memory_space=pltpu.VMEM)
        smem = pl.BlockSpec(memory_space=pltpu.SMEM)
        dma = pltpu.SemaphoreType.DMA

        mean_up, mean_down, clip = pl.pallas_call(
            functools.partial(grad_kernel, n_chunk, width),
            out_shape=(jax.ShapeDtypeStruct((n_chunk, d_model, width), F32),
                       jax.ShapeDtypeStruct((n_chunk, width, d_model), F32),
                       jax.ShapeDtypeStruct((8, 128), F32)),
            in_specs=[hbm, hbm, hbm, hbm, vmem, vmem, smem],
            out_specs=(hbm, hbm, vmem),
            scratch_shapes=[
                pltpu.VMEM((n_chunk, d_model, width), F32),
                pltpu.VMEM((n_chunk, width, d_model), F32),
                pltpu.VMEM((n_chunk, d_model, width), F32),
                pltpu.VMEM((n_chunk, width, d_model), F32),
                pltpu.VMEM((2, d_model, width), F32),
                pltpu.VMEM((2, width, d_model), F32),
                pltpu.VMEM((rows, d_model), BF16),
                pltpu.VMEM((rows, d_model), BF16),
                pltpu.VMEM((rows, d_model), F32),
                pltpu.VMEM((rows, d_model), F32),
                pltpu.VMEM((8, width), F32),
                pltpu.VMEM((8, d_model), F32),
                pltpu.VMEM((8, 128), F32),
                pltpu.VMEM((4, 8, 128), F32),
                dma((2, 2)), dma((2, 2)),
                dma((n_chunk,)), dma((n_chunk,)), dma((n_chunk,)), dma((n_chunk,)),
                dma((n_chunk,)), dma((n_chunk,)),
                dma((2,)), dma((2,)), dma((3,)), dma((4,)),
            ],
            compiler_params=pltpu.CompilerParams(collective_id=0, has_side_effects=True, vmem_limit_bytes=VMEM_MAX),
            name="grad_exchange",
        )(w_up[0], w_down[0], g_up[0, 0], g_down[0, 0], acts_last[0], grad_out, max_norm)

        x_all = x_next.reshape(n_micro * rows, d_model)
        up_block = pl.BlockSpec((None, d_model, width), lambda j: (0, 0, j))
        down_block = pl.BlockSpec((None, width, d_model), lambda j: (0, j, 0))
        up_chunk = pl.BlockSpec((None, d_model, width), lambda j: (j, 0, 0))
        down_chunk = pl.BlockSpec((None, width, d_model), lambda j: (j, 0, 0))
        whole = pl.BlockSpec((n_micro * rows, d_model), lambda j: (0, 0))
        up_out = jax.ShapeDtypeStruct(w_up.shape, F32)
        down_out = jax.ShapeDtypeStruct(w_down.shape, F32)
        nw1, nw2, nm1, nm2, nv1, nv2, wb1, wb2, acc = pl.pallas_call(
            update_kernel,
            grid=(n_chunk,),
            out_shape=(up_out, down_out, up_out, down_out, up_out, down_out,
                       jax.ShapeDtypeStruct((n_chunk, d_model, width), BF16),
                       jax.ShapeDtypeStruct((n_chunk, width, d_model), BF16),
                       jax.ShapeDtypeStruct((n_micro * rows, d_model), F32)),
            in_specs=[smem, smem, up_block, up_block, up_block, up_chunk,
                      down_block, down_block, down_block, down_chunk, whole],
            out_specs=(up_block, down_block, up_block, down_block, up_block, down_block, up_chunk, down_chunk, whole),
            compiler_params=pltpu.CompilerParams(vmem_limit_bytes=VMEM_MAX),
            name="update",
        )(clip, learn_rate, w_up, m_up, v_up, mean_up, w_down, m_down, v_down, mean_down, x_all)

        y_next = pl.pallas_call(
            functools.partial(forward_kernel, n_chunk, n_micro, half),
            out_shape=jax.ShapeDtypeStruct(x_next.shape, BF16),
            in_specs=[vmem, vmem, hbm, hbm],
            out_specs=vmem,
            scratch_shapes=[
                pltpu.VMEM((n_chunk, d_model, width), BF16),
                pltpu.VMEM((n_chunk, width, d_model), BF16),
                pltpu.VMEM((n_micro, half, d_model), F32),
                pltpu.VMEM((n_micro, half, d_model), BF16),
                pltpu.VMEM((n_micro, rows, d_model), BF16),
                pltpu.VMEM((n_micro, half, d_model), BF16),
                pltpu.VMEM((n_micro, rows, d_model), F32),
                pltpu.VMEM((n_micro, half, d_model), F32),
                dma((2,)), dma((n_micro,)), dma((n_micro,)), dma((2, n_micro)), dma((2, n_micro)),
                dma((n_micro,)), dma((n_micro,)), dma((2, n_micro)), dma((2, n_micro)), dma((n_micro,)), dma((n_micro,)),
            ],
            compiler_params=pltpu.CompilerParams(collective_id=1, has_side_effects=True, vmem_limit_bytes=VMEM_MAX),
            name="forward_exchange",
        )(acc.reshape(n_micro, rows, d_model), x_next, wb1, wb2)
        return nw1, nw2, nm1, nm2, nv1, nv2, y_next

    return jax.shard_map(device_step, mesh=mesh, in_specs=in_specs, out_specs=out_specs, check_vma=False)
```

time: 1170 us -> 733 us (0.63)
  waiting for transfers between devices: 901 us -> 0 us
  Pallas kernels: 0 us -> 728 us
  other arithmetic: 123 us -> 0 us
  matrix products: 54.6 us -> 0 us
  local copies, waits for them, and re-layouts: 39.1 us -> 2.94 us
  between operations: 18.7 us -> 1.95 us
    psum x7 -> x0, waiting for transfers between devices: 896 us -> none  [the longest x1 572 us: device_step(): mean_up = lax.psum(g_up[0, 0] + grad_up, 'data') / n_data]
    pallas_call x0 -> x3, Pallas kernels: none -> 728 us  [the longest x1 574 us: device_step(): pl.pallas_call(functools.partial(grad_kernel, n_chunk, width), out_shape=...]
    convert_element_type x8 -> x0, other arithmetic: 91.6 us -> none  [the longest x1 34.9 us: apply_update(): down_w.astype(jnp.bfloat16)]
    dot_general x7 -> x0, matrix products: 54.6 us -> none  [the longest x3 25.9 us: fwd_local(): return jnp.dot(hidden, down_new_bf, preferred_element_type=jnp.float32)]
    div x2 -> x0, other arithmetic: 26.9 us -> none  [the longest x1 13.5 us: device_step(): mean_up = lax.psum(g_up[0, 0] + grad_up, 'data') / n_data]
    unnamed x28 -> x1, local copies, waits for them, and re-layouts: 22.8 us -> 2.94 us
    another operation x5 -> x0, local copies, waits for them, and re-layouts: 15.3 us -> none
  transfers between devices with their start and end apart: 13 -> 0, of which waited for: 10 -> 0; matrix products, arithmetic and copies ran while one was open for 1% -> 0% of each run, Pallas kernels for 0% -> 0%
where the time goes in v1:
time: 733 us
  Pallas kernels  728 us (99%)
    pallas_call x1, Pallas kernels, device_step(): pl.pallas_call(functools.partial(grad_kernel, n_chunk, width), out_shape=...  574 us
    pallas_call x1, Pallas kernels, device_step(): pl.pallas_call(update_kernel, grid=(n_chunk,), out_shape=(up_out, down_ou...  81.4 us
    pallas_call x1, Pallas kernels, device_step(): pl.pallas_call(functools.partial(forward_kernel, n_chunk, n_micro, half),...  72.6 us

profile of v1, /device:TPU:0, one launch (start us, length us, event | category | flops | bytes accessed | tf_op | source)
XLA Modules:
  0.0 733.2 jit_solution(10189076217640801020)
XLA Ops:
  1.9 574.3 %grad_exchange.1 = (f32[10,1280,256]{2,1,0:T(8,128)}, f32[10,256,1280]{2,1,0:T(8,128)}, f32[8,128]{1,0:T(8,128)}) custom-call(f32[1280,2560]{1,0:T(8,128)} %bitcast.7, f32[2560,1280]{1,0:T(8,128)} %bitcast.8, f32[1280,2560]{1,0:T(8,128)} %bitcast.9, f32[2560,1280]{1,0:T(8,128)} %bitcast.10, bf16[256,1280]{1,0:T(8,128)(2,1)} %bitcast.13, ...), custom_call_target="tpu_custom_call" | custom-call | tf_op jit(solution)/shard_map/grad_exchange/pallas_call | solution.py:331
  576.2 81.4 %update.1 = (f32[1,1280,2560]{2,1,0:T(8,128)}, f32[1,2560,1280]{2,1,0:T(8,128)}, f32[1,1280,2560]{2,1,0:T(8,128)}, f32[1,2560,1280]{2,1,0:T(8,128)}, f32[1,1280,...) custom-call(f32[8,128]{1,0:T(8,128)} %get-tuple-element.19.clip, ...), custom_call_target="tpu_custom_call" | custom-call | tf_op jit(solution)/shard_map/update/pallas_call | solution.py:370
  657.6 72.6 %forward_exchange.1 = bf16[3,256,1280]{2,1,0:T(8,128)(2,1)} custom-call(f32[3,256,1280]{2,1,0:T(8,128)} %bitcast.12, bf16[3,256,1280]{2,1,0:T(8,128)(2,1)} %x.1, bf16[10,1280,256]{2,1,0:T(8,128)(2,1)} %get-tuple-element.29.wb1, bf16[10,256,1280]{2,1,0:T(8,128)(2,1)} %get-tuple-element.30.wb2), custom_call_target="tpu_custom_call" | custom-call | tf_op jit(solution)/shard_map/forward_exchange/pallas_call | solution.py:384
  730.2 2.9 copy.23

commit v2 on v1

--- a/solution.py
+++ b/solution.py
@@ -22,6 +22,7 @@
 MESH = pl.DeviceIdType.MESH
 VMEM_MAX = 67_043_328
 CHUNK = 256
+COLS = 128
 F32 = jnp.float32
 BF16 = jnp.bfloat16
 
@@ -181,54 +182,81 @@
         write_one(j).wait()
 
 
-def update_kernel(clip, rate, w1, m1, v1, gb1, w2, m2, v2, gb2, x,
-                  nw1, nw2, nm1, nm2, nv1, nv2, wb1, wb2, acc):
-    s = lax.axis_index("stage")
+def adamw(scale, step_rate, w, mom, sec, mean):
+    grad = scale * mean
+    mom_new = BETA_ONE * mom + (1.0 - BETA_ONE) * grad
+    sec_new = BETA_TWO * sec + ((1.0 - BETA_TWO) * grad) * grad
+    direction = (mom_new * (1.0 / ONE_CORR)) / (jnp.sqrt(sec_new * (1.0 / TWO_CORR)) + ADAM_EPS)
+    return w - step_rate * (direction + WEIGHT_DECAY * w), mom_new, sec_new
+
+
+def update_down(clip, rate, w2, m2, v2, gb2, hid, nw2, nm2, nv2, mine, theirs, prod):
+    n_micro, half = mine.shape[0], mine.shape[1]
+    new, mom, sec = adamw(clip[0, 0], rate[0], w2[...], m2[...], v2[...], gb2[...])
+    nw2[...] = new
+    nm2[...] = mom
+    nv2[...] = sec
+
+    @pl.when(lax.axis_index("stage") == 0)
+    def _():
+        m = lax.axis_index("model")
+        prod[...] = dot(hid[...], nw2[...].astype(BF16)).reshape(prod.shape)
+        for k in range(n_micro):
+            mine[k] = prod[k, pl.ds(pl.multiple_of(m * half, half), half), :]
+            theirs[k] = prod[k, pl.ds(pl.multiple_of((1 - m) * half, half), half), :]
+
+
+def update_first(n_chunk, width, clip, rate, w1, m1, v1, gb1, w2, m2, v2, gb2, x,
+                 nw1, nm1, nv1, nw2, nm2, nv2, hid, mine, theirs, prod):
     j = pl.program_id(0)
-    scale = clip[0, 0]
-    step_rate = rate[0]
-
-    def adamw(w, mom, sec, mean):
-        grad = scale * mean
-        mom_new = BETA_ONE * mom + (1.0 - BETA_ONE) * grad
-        sec_new = BETA_TWO * sec + (1.0 - BETA_TWO) * grad * grad
-        direction = (mom_new / ONE_CORR) / (jnp.sqrt(sec_new / TWO_CORR) + ADAM_EPS)
-        return w - step_rate * (direction + WEIGHT_DECAY * w), mom_new, sec_new
-
-    a, b, c = adamw(w1[...], m1[...], v1[...], gb1[...])
-    nw1[...] = a
-    nm1[...] = b
-    nv1[...] = c
-    wb1[...] = a.astype(BF16)
-    a, b, c = adamw(w2[...], m2[...], v2[...], gb2[...])
-    nw2[...] = a
-    nm2[...] = b
-    nv2[...] = c
-    wb2[...] = a.astype(BF16)
-
-    @pl.when(j == 0)
-    def _():
-        acc[...] = jnp.zeros_like(acc)
-
-    @pl.when(s == 0)
-    def _():
-        hid = gelu_parts(dot(x[...], wb1[...]))[1].astype(BF16)
-        acc[...] += dot(hid, wb2[...])
-
-
-def forward_kernel(n_chunk, n_micro, half, acc, x, wb1, wb2, y,
-                   w1, w2, first_in, own_half, act, peer_half, part, part_in,
+
+    @pl.when(j < n_chunk)
+    def _():
+        new, mom, sec = adamw(clip[0, 0], rate[0], w1[...], m1[...], v1[...], gb1[...])
+        nw1[...] = new
+        nm1[...] = mom
+        nv1[...] = sec
+
+        @pl.when(lax.axis_index("stage") == 0)
+        def _():
+            cols = pl.ds(pl.multiple_of(j * width, width), width)
+            hid[:, cols] = gelu_parts(dot(x[...], nw1[...].astype(BF16)))[1].astype(BF16)
+
+    @pl.when(j >= n_chunk)
+    def _():
+        update_down(clip, rate, w2, m2, v2, gb2, hid, nw2, nm2, nv2, mine, theirs, prod)
+
+
+def update_second(clip, rate, w2, m2, v2, gb2, hid, _w, _m, _v, nw2, nm2, nv2, mine, theirs, prod):
+    update_down(clip, rate, w2, m2, v2, gb2, hid, nw2, nm2, nv2, mine, theirs, prod)
+
+
+def forward_kernel(n_chunk, n_micro, half, width, cut, mine_a, got_a, mine_b, theirs_b, x, nw1, nw2, y,
+                   w1, w2, w1f, w2f, got_b, own_half, act, peer_half, part, part_in,
                    w_sem, a_send, a_recv, o_send, o_recv, p_send, p_recv, y_send, y_recv, f_send, f_recv):
     m, d, s = positions()
     peer_y = (1 - m, d, s)
     peer_c = (m, d, 1 - s)
     peer_d = (1 - m, d, 1 - s)
+
+    def loads(j):
+        slot = lax.rem(j, 2)
+        cols = pl.ds(pl.multiple_of(j * width, width), width)
+        return (pltpu.make_async_copy(nw1.at[0, :, cols], w1f.at[slot], w_sem.at[0, slot]),
+                pltpu.make_async_copy(nw2.at[0, cols, :], w2f.at[slot], w_sem.at[1, slot]))
+
+    @pl.when(s == 1)
+    def _():
+        for first in (0, 1):
+            for copy in loads(first):
+                copy.start()
+
     entry_barrier((peer_y, peer_c, peer_d))
     mine = pl.ds(pl.multiple_of(m * half, half), half)
     theirs = pl.ds(pl.multiple_of((1 - m) * half, half), half)
 
     def send_first(k):
-        return remote(acc.at[k, theirs, :], first_in.at[k], a_send.at[k], a_recv.at[k], peer_y)
+        return remote(theirs_b.at[k], got_b.at[k], a_send.at[k], a_recv.at[k], peer_y)
 
     def give_core(k):
         return remote(own_half.at[k], act.at[k, mine, :], o_send.at[0, k], o_recv.at[0, k], peer_c)
@@ -254,11 +282,12 @@
         for k in range(n_micro):
             if k + 1 < n_micro:
                 send_first(k + 1).start()
+            rows = x[k, mine, :].astype(F32)
+            own_half[k, :, :cut] = (rows[:, :cut] + (mine_a[k] + got_a[k])).astype(BF16)
             send_first(k).wait_recv()
-            out = x[k, mine, :].astype(F32) + (acc[k, mine, :] + first_in[k])
-            own_half[k] = out.astype(BF16)
+            own_half[k, :, cut:] = (rows[:, cut:] + (mine_b[k] + got_b[k])).astype(BF16)
+            give_diag(k).start()
             give_core(k).start()
-            give_diag(k).start()
         for k in range(n_micro):
             give_own(k).wait_recv()
             pass_on(k).wait_recv()
@@ -269,12 +298,19 @@
 
     @pl.when(s == 1)
     def _():
-        cp1 = pltpu.make_async_copy(wb1, w1, w_sem.at[0])
-        cp2 = pltpu.make_async_copy(wb2, w2, w_sem.at[1])
-        cp1.start()
-        cp2.start()
-        cp1.wait()
-        cp2.wait()
+        @pl.loop(0, n_chunk)
+        def _(j):
+            slot = lax.rem(j, 2)
+            copies = loads(j)
+            copies[0].wait()
+            w1[j] = w1f[slot].astype(BF16)
+            copies[1].wait()
+            w2[j] = w2f[slot].astype(BF16)
+
+            @pl.when(j + 2 < n_chunk)
+            def _():
+                for copy in loads(j + 2):
+                    copy.start()
 
         def finish(k):
             send_part(k).wait_recv()
@@ -360,47 +396,77 @@
         )(w_up[0], w_down[0], g_up[0, 0], g_down[0, 0], acts_last[0], grad_out, max_norm)
 
         x_all = x_next.reshape(n_micro * rows, d_model)
-        up_block = pl.BlockSpec((None, d_model, width), lambda j: (0, 0, j))
-        down_block = pl.BlockSpec((None, width, d_model), lambda j: (0, j, 0))
-        up_chunk = pl.BlockSpec((None, d_model, width), lambda j: (j, 0, 0))
-        down_chunk = pl.BlockSpec((None, width, d_model), lambda j: (j, 0, 0))
-        whole = pl.BlockSpec((n_micro * rows, d_model), lambda j: (0, 0))
+        n_col = d_model // COLS
+        n_first = n_col * 3 // 5
+        cut = n_first * COLS
+        mean_down = mean_down.reshape(1, ff, d_model)
+        up_block = pl.BlockSpec((None, d_model, width), lambda j: (0, 0, jnp.minimum(j, n_chunk - 1)))
+        up_chunk = pl.BlockSpec((None, d_model, width), lambda j: (jnp.minimum(j, n_chunk - 1), 0, 0))
+        col_a = pl.BlockSpec((None, ff, COLS), lambda j: (0, 0, jnp.maximum(j - n_chunk, 0)))
+        col_b = pl.BlockSpec((None, ff, COLS), lambda j: (0, 0, j + n_first))
+        piece_a = pl.BlockSpec((n_micro, half, COLS), lambda j: (0, 0, jnp.maximum(j - n_chunk, 0)))
+        piece_b = pl.BlockSpec((n_micro, half, COLS), lambda j: (0, 0, j))
+        x_block = pl.BlockSpec((n_micro * rows, d_model), lambda j: (0, 0))
+        hid_block = pl.BlockSpec((n_micro * rows, ff), lambda j: (0, 0))
         up_out = jax.ShapeDtypeStruct(w_up.shape, F32)
         down_out = jax.ShapeDtypeStruct(w_down.shape, F32)
-        nw1, nw2, nm1, nm2, nv1, nv2, wb1, wb2, acc = pl.pallas_call(
-            update_kernel,
-            grid=(n_chunk,),
-            out_shape=(up_out, down_out, up_out, down_out, up_out, down_out,
-                       jax.ShapeDtypeStruct((n_chunk, d_model, width), BF16),
-                       jax.ShapeDtypeStruct((n_chunk, width, d_model), BF16),
-                       jax.ShapeDtypeStruct((n_micro * rows, d_model), F32)),
-            in_specs=[smem, smem, up_block, up_block, up_block, up_chunk,
-                      down_block, down_block, down_block, down_chunk, whole],
-            out_specs=(up_block, down_block, up_block, down_block, up_block, down_block, up_chunk, down_chunk, whole),
+        part_a = jax.ShapeDtypeStruct((n_micro, half, cut), F32)
+        part_b = jax.ShapeDtypeStruct((n_micro, half, d_model - cut), F32)
+        prod = [pltpu.VMEM((n_micro, rows, COLS), F32)]
+
+        def cost(units):
+            return pl.CostEstimate(flops=2 * n_micro * rows * units, bytes_accessed=28 * units, transcendentals=2 * units)
+
+        nw1, nm1, nv1, nw2, nm2, nv2, hid, mine_a, theirs_a = pl.pallas_call(
+            functools.partial(update_first, n_chunk, width),
+            grid=(n_chunk + n_first,),
+            out_shape=(up_out, up_out, up_out, down_out, down_out, down_out,
+                       jax.ShapeDtypeStruct((n_micro * rows, ff), BF16), part_a, part_a),
+            in_specs=[smem, smem, up_block, up_block, up_block, up_chunk, col_a, col_a, col_a, col_a, x_block],
+            out_specs=(up_block, up_block, up_block, col_a, col_a, col_a, hid_block, piece_a, piece_a),
+            scratch_shapes=prod,
             compiler_params=pltpu.CompilerParams(vmem_limit_bytes=VMEM_MAX),
-            name="update",
+            cost_estimate=cost(d_model * ff + cut * ff),
+            name="update_first",
         )(clip, learn_rate, w_up, m_up, v_up, mean_up, w_down, m_down, v_down, mean_down, x_all)
 
+        got_a = lax.ppermute(theirs_a, ('model', 'stage'), [(0, 2), (2, 0)])
+
+        nw2, nm2, nv2, mine_b, theirs_b = pl.pallas_call(
+            update_second,
+            grid=(n_col - n_first,),
+            out_shape=(down_out, down_out, down_out, part_b, part_b),
+            in_specs=[smem, smem, col_b, col_b, col_b, col_b, hid_block, hbm, hbm, hbm],
+            out_specs=(col_b, col_b, col_b, piece_b, piece_b),
+            scratch_shapes=prod,
+            input_output_aliases={7: 0, 8: 1, 9: 2},
+            compiler_params=pltpu.CompilerParams(vmem_limit_bytes=VMEM_MAX),
+            cost_estimate=cost((d_model - cut) * ff),
+            name="update_second",
+        )(clip, learn_rate, w_down, m_down, v_down, mean_down, hid, nw2, nm2, nv2)
+
         y_next = pl.pallas_call(
-            functools.partial(forward_kernel, n_chunk, n_micro, half),
+            functools.partial(forward_kernel, n_chunk, n_micro, half, width, cut),
             out_shape=jax.ShapeDtypeStruct(x_next.shape, BF16),
-            in_specs=[vmem, vmem, hbm, hbm],
+            in_specs=[vmem, vmem, vmem, vmem, vmem, hbm, hbm],
             out_specs=vmem,
             scratch_shapes=[
                 pltpu.VMEM((n_chunk, d_model, width), BF16),
                 pltpu.VMEM((n_chunk, width, d_model), BF16),
-                pltpu.VMEM((n_micro, half, d_model), F32),
+                pltpu.VMEM((2, d_model, width), F32),
+                pltpu.VMEM((2, width, d_model), F32),
+                pltpu.VMEM((n_micro, half, d_model - cut), F32),
                 pltpu.VMEM((n_micro, half, d_model), BF16),
                 pltpu.VMEM((n_micro, rows, d_model), BF16),
                 pltpu.VMEM((n_micro, half, d_model), BF16),
                 pltpu.VMEM((n_micro, rows, d_model), F32),
                 pltpu.VMEM((n_micro, half, d_model), F32),
-                dma((2,)), dma((n_micro,)), dma((n_micro,)), dma((2, n_micro)), dma((2, n_micro)),
+                dma((2, 2)), dma((n_micro,)), dma((n_micro,)), dma((2, n_micro)), dma((2, n_micro)),
                 dma((n_micro,)), dma((n_micro,)), dma((2, n_micro)), dma((2, n_micro)), dma((n_micro,)), dma((n_micro,)),
             ],
             compiler_params=pltpu.CompilerParams(collective_id=1, has_side_effects=True, vmem_limit_bytes=VMEM_MAX),
             name="forward_exchange",
-        )(acc.reshape(n_micro, rows, d_model), x_next, wb1, wb2)
+        )(mine_a, got_a, mine_b, theirs_b, x_next, nw1, nw2)
         return nw1, nw2, nm1, nm2, nv1, nv2, y_next
 
     return jax.shard_map(device_step, mesh=mesh, in_specs=in_specs, out_specs=out_specs, check_vma=False)

time: 733 us -> 729 us (level)
  Pallas kernels: 728 us -> 720 us
    pallas_call x2 -> x3, Pallas kernels: 154 us -> 146 us  [the longest x1 63.4 us: device_step(): pl.pallas_call(functools.partial(update_first, n_chunk, width), grid=(n_c...]
  transfers between devices with their start and end apart: 0 -> 1, of which waited for: 0 -> 0; matrix products, arithmetic and copies ran while one was open for 0% -> 0% of each run, Pallas kernels for 0% -> 3%
where the time goes in v2:
time: 729 us; the launch traced here: 728 us
  Pallas kernels  720 us (99%)
    pallas_call x1, Pallas kernels, device_step(): pl.pallas_call(functools.partial(grad_kernel, n_chunk, width), out_shape=...  574 us
    pallas_call x1, Pallas kernels, device_step(): pl.pallas_call(functools.partial(update_first, n_chunk, width), grid=(n_c...  63.4 us
    pallas_call x1, Pallas kernels, device_step(): pl.pallas_call(functools.partial(forward_kernel, n_chunk, n_micro, half,...  62.7 us
    pallas_call x1, Pallas kernels, device_step(): pl.pallas_call(update_second, grid=(n_col - n_first,), out_shape=(down_ou...  20.1 us
  transfers between devices with their start and end apart: 1, of which 0 were waited for; matrix products, arithmetic and copies ran while one was open for 0% of the time, Pallas kernels for 3%

profile of v2, /device:TPU:0, one launch (start us, length us, event | category | flops | bytes accessed | tf_op | source)
XLA Modules:
  0.0 728.4 jit_solution(16429140675586296081)
XLA Ops:
  1.9 574.3 %grad_exchange.1 = (f32[10,1280,256]{2,1,0:T(8,128)}, f32[10,256,1280]{2,1,0:T(8,128)}, f32[8,128]{1,0:T(8,128)}) custom-call(f32[1280,2560]{1,0:T(8,128)} %bitcast.8, f32[2560,1280]{1,0:T(8,128)} %bitcast.7, f32[1280,2560]{1,0:T(8,128)} %bitcast.11, f32[2560,1280]{1,0:T(8,128)} %bitcast.12, bf16[256,1280]{1,0:T(8,128)(2,1)} %bitcast.14, ...), custom_call_target="tpu_custom_call" | custom-call | tf_op jit(solution)/shard_map/grad_exchange/pallas_call | solution.py:367
  576.2 63.4 %update_first.1 = (f32[1,1280,2560]{2,1,0:T(8,128)}, f32[1,1280,2560]{2,1,0:T(8,128)}, f32[1,1280,2560]{2,1,0:T(8,128)}, f32[1,2560,1280]{2,1,0:T(8,128)}, f32[1...) custom-call(f32[8,128]{1,0:T(8,128)} %get-tuple-element.24.clip, ...), custom_call_target="tpu_custom_call" | custom-call | flops 8053063680 | bytes 146800640 | tf_op jit(solution)/shard_map/update_first/pallas_call | solution.py:420
  639.6 3.1 collective-permute-start
  642.7 20.1 %update_second.1 = (f32[1,2560,1280]{2,1,0:T(8,128)}, f32[1,2560,1280]{2,1,0:T(8,128)}, f32[1,2560,1280]{2,1,0:T(8,128)}, f32[3,128,512]{2,1,0:T(8,128)}, f32[3,128,512]{2,1,0:T(8,128)}) custom-call(f32[8,128]{1,0:T(8,128)} %get-tuple-element.24.clip, f32[1]{0:T(128)S(6)} %copy.27.rate, ...), custom_call_target="tpu_custom_call", output_to_operand_aliasing={{0}: (7, {}), {1}: (8, {}), {2}: (9, {})} | custom-call | flops 2013265920 | bytes 36700160 | tf_op jit(solution)/shard_map/update_second/pallas_call | solution.py:435
  662.8 0.0 collective-permute-done.got_a
  662.8 62.7 %forward_exchange.1 = bf16[3,256,1280]{2,1,0:T(8,128)(2,1)} custom-call(f32[3,128,768]{2,1,0:T(8,128)} %get-tuple-element.37.mine_a, f32[3,128,768]{2,1,0:T(8,128)} %collective-permute-done.got_a, f32[3,128,512]{2,1,0:T(8,128)} %get-tuple-element.39.mine_b, f32[3,128,512]{2,1,0:T(8,128)} %get-tuple-element.40.theirs_b, bf16[3,256,1280]{2,1,0:T(8,128)(2,1)} %x.1, ...), custom_call_target="tpu_custom_call" | custom-call | tf_op jit(solution)/shard_map/forward_exchange/pallas_call | solution.py:448
  725.5 2.9 copy.29
Async XLA Ops:
  639.6 23.2 %collective-permute-start = (f32[3,128,768]{2,1,0:T(8,128)}, f32[3,128,768]{2,1,0:T(8,128)}, u32[]{:S(2)}, u32[]{:S(2)}) collective-permute-start(f32[3,128,768]{2,1,0:T(8,128)} %get-tuple-element.38), channel_id=1, source_target_pairs={{0,4},{4,0},{2,6},{6,2}} | collective-permute-start | bytes 3538952 | tf_op jit(solution)/shard_map/ppermute | solution.py:433

commit v3 on v2

--- a/solution.py
+++ b/solution.py
@@ -23,6 +23,9 @@
 VMEM_MAX = 67_043_328
 CHUNK = 256
 COLS = 128
+SLOTS = 8
+AHEAD = 5
+SPARE = 1 << 20
 F32 = jnp.float32
 BF16 = jnp.bfloat16
 
@@ -55,9 +58,9 @@
     return pltpu.make_async_remote_copy(src_ref=src, dst_ref=dst, send_sem=send, recv_sem=recv, device_id=peer, device_id_type=MESH)
 
 
-def grad_kernel(n_chunk, width, w1, w2, g1, g2, acts, dy, max_norm, gb1, gb2, clip,
-                gs1, gs2, gr1, gr2, w1b, w2b, gvec, gout, part, part_in, sq1, sq2, sq_out, sq_in,
-                w_sem, g_sem, send1, send2, recv1, recv2, out1, out2, part_sem, gvec_sem, sq_send, sq_recv):
+def grad_kernel(n_chunk, width, w1, w2, g1, g2, acts, dy, max_norm, gr1, gr2, clip,
+                gs1, gs2, w1b, w2b, gvec, gout, part, part_in, sq1, sq2, sq_out, sq_in,
+                w_sem, g_sem, send1, send2, recv1, recv2, part_sem, gvec_sem, sq_send, sq_recv):
     m, d, s = positions()
     peer_x = (m, 1 - d, s)
     peer_y = (1 - m, d, s)
@@ -136,24 +139,16 @@
     sq1[...] = jnp.zeros_like(sq1)
     sq2[...] = jnp.zeros_like(sq2)
 
-    def write_two(j):
-        return pltpu.make_async_copy(gr2.at[j], gb2.at[j], out2.at[j])
-
-    def write_one(j):
-        return pltpu.make_async_copy(gr1.at[j], gb1.at[j], out1.at[j])
-
     @pl.loop(0, n_chunk)
     def _(j):
         send_two(j).wait_recv()
         mean = (gs2[j] + gr2[j]) * 0.5
         gr2[j] = mean
         sq2[...] += jnp.sum((mean * mean).reshape(-1, 8, mean.shape[1]), axis=0)
-        write_two(j).start()
         send_one(j).wait_recv()
         mean = (gs1[j] + gr1[j]) * 0.5
         gr1[j] = mean
         sq1[...] += jnp.sum((mean * mean).reshape(-1, 8, mean.shape[1]), axis=0)
-        write_one(j).start()
 
     sq_out[...] = jnp.full(sq_out.shape, jnp.sum(sq1[...]) + jnp.sum(sq2[...]), F32)
     mine = 2 * m + s
@@ -178,8 +173,6 @@
     def _(j):
         send_two(j).wait_send()
         send_one(j).wait_send()
-        write_two(j).wait()
-        write_one(j).wait()
 
 
 def adamw(scale, step_rate, w, mom, sec, mean):
@@ -190,45 +183,131 @@
     return w - step_rate * (direction + WEIGHT_DECAY * w), mom_new, sec_new
 
 
-def update_down(clip, rate, w2, m2, v2, gb2, hid, nw2, nm2, nv2, mine, theirs, prod):
-    n_micro, half = mine.shape[0], mine.shape[1]
-    new, mom, sec = adamw(clip[0, 0], rate[0], w2[...], m2[...], v2[...], gb2[...])
-    nw2[...] = new
-    nm2[...] = mom
-    nv2[...] = sec
-
-    @pl.when(lax.axis_index("stage") == 0)
-    def _():
-        m = lax.axis_index("model")
-        prod[...] = dot(hid[...], nw2[...].astype(BF16)).reshape(prod.shape)
-        for k in range(n_micro):
-            mine[k] = prod[k, pl.ds(pl.multiple_of(m * half, half), half), :]
-            theirs[k] = prod[k, pl.ds(pl.multiple_of((1 - m) * half, half), half), :]
-
-
-def update_first(n_chunk, width, clip, rate, w1, m1, v1, gb1, w2, m2, v2, gb2, x,
-                 nw1, nm1, nv1, nw2, nm2, nv2, hid, mine, theirs, prod):
-    j = pl.program_id(0)
-
-    @pl.when(j < n_chunk)
-    def _():
-        new, mom, sec = adamw(clip[0, 0], rate[0], w1[...], m1[...], v1[...], gb1[...])
-        nw1[...] = new
-        nm1[...] = mom
-        nv1[...] = sec
-
-        @pl.when(lax.axis_index("stage") == 0)
-        def _():
-            cols = pl.ds(pl.multiple_of(j * width, width), width)
-            hid[:, cols] = gelu_parts(dot(x[...], nw1[...].astype(BF16)))[1].astype(BF16)
-
-    @pl.when(j >= n_chunk)
-    def _():
-        update_down(clip, rate, w2, m2, v2, gb2, hid, nw2, nm2, nv2, mine, theirs, prod)
-
-
-def update_second(clip, rate, w2, m2, v2, gb2, hid, _w, _m, _v, nw2, nm2, nv2, mine, theirs, prod):
-    update_down(clip, rate, w2, m2, v2, gb2, hid, nw2, nm2, nv2, mine, theirs, prod)
+def update_kernel(first, last, n_up, width, clip, rate, w1, m1, v1, gb1, w2, m2, v2, gb2, x, hid_in,
+                  nw1, nm1, nv1, nw2, nm2, nv2, hid, mine, theirs,
+                  ring, x_buf, prod, in_sem, out_sem, x_sem):
+    m, _, s = positions()
+    n_slot = ring.shape[1]
+    deep, wide = ring.shape[2:]
+    n_micro, half = mine.shape[:2]
+    first_col = (first - n_up) // 2 if first > n_up else 0
+    scale = clip[0, 0]
+    step_rate = rate[0]
+    hid_now = hid if first < n_up else hid_in
+    load_x = pltpu.make_async_copy(x, x_buf, x_sem)
+
+    def place(i):
+        col = pl.multiple_of(((i - n_up) // 2) * wide, wide)
+        row = pl.multiple_of(lax.rem(i - n_up, 2) * deep, deep)
+        return pl.ds(row, deep), pl.ds(col, wide)
+
+    def start(i, fetch):
+        slot = lax.rem(i, n_slot)
+        sem = in_sem if fetch else out_sem
+
+        def go(k, far):
+            near = ring.at[k, slot]
+            pair = (far, near) if fetch else (near, far)
+            pltpu.make_async_copy(*pair, sem.at[k, slot]).start()
+
+        if first < n_up:
+            @pl.when(i < n_up)
+            def _():
+                cols = pl.ds(pl.multiple_of(i * wide, wide), wide)
+                for k, ref in enumerate((w1, m1, v1) if fetch else (nw1, nm1, nv1)):
+                    go(k, ref.at[0, :, cols])
+
+        @pl.when(i >= n_up)
+        def _():
+            rows, cols = place(i)
+            for k, ref in enumerate((w2, m2, v2) if fetch else (nw2, nm2, nv2)):
+                go(k, ref.at[0, rows, cols])
+
+    def finish(i, fetch):
+        slot = lax.rem(i, n_slot)
+        for k, ref in enumerate((w2, m2, v2) if fetch else (nw2, nm2, nv2)):
+            far, near = ref.at[0, :deep, :wide], ring.at[k, slot]
+            sem = (in_sem if fetch else out_sem).at[k, slot]
+            (pltpu.make_async_copy(far, near, sem) if fetch else pltpu.make_async_copy(near, far, sem)).wait()
+
+    for i in range(first, first + AHEAD):
+        start(jnp.int32(i), True)
+    if first < n_up:
+        load_x.start()
+        load_x.wait()
+
+    def step(slot, mean):
+        new, mom, sec = adamw(scale, step_rate, ring[0, slot], ring[1, slot], ring[2, slot], mean)
+        ring[0, slot] = new
+        ring[1, slot] = mom
+        ring[2, slot] = sec
+
+    def up_chunk(i, slot):
+        part = pl.ds(pl.multiple_of(lax.rem(i, width // wide) * wide, wide), wide)
+        step(slot, gb1[i // (width // wide), :, part])
+
+        @pl.when(s == 0)
+        def _():
+            cols = pl.ds(pl.multiple_of(i * wide, wide), wide)
+            rows = x_buf[...].reshape(-1, x_buf.shape[2])
+            hid[:, cols] = gelu_parts(dot(rows, ring[0, slot].astype(BF16)))[1].astype(BF16)
+
+    def down_chunk(i, slot):
+        rows, cols = place(i)
+        upper = lax.rem(i - n_up, 2)
+        block = deep // gb2.shape[1]
+        mean = gb2[pl.ds(upper * block, block), :, cols].reshape(deep, wide)
+        step(slot, mean)
+
+        @pl.when(s == 0)
+        def _():
+            new = dot(hid_now[:, rows], ring[0, slot].astype(BF16)).reshape(prod.shape)
+
+            @pl.when(upper == 0)
+            def _():
+                prod[...] = new
+
+            @pl.when(upper == 1)
+            def _():
+                prod[...] += new
+                out = pl.ds(pl.multiple_of(((i - n_up) // 2 - first_col) * wide, wide), wide)
+                for k in range(n_micro):
+                    mine[k, :, out] = prod[k, pl.ds(pl.multiple_of(m * half, half), half), :]
+                    theirs[k, :, out] = prod[k, pl.ds(pl.multiple_of((1 - m) * half, half), half), :]
+
+    @pl.loop(first, last)
+    def _(i):
+        slot = lax.rem(i, n_slot)
+        finish(i, True)
+        if first < n_up:
+            @pl.when(i < n_up)
+            def _():
+                up_chunk(i, slot)
+
+        @pl.when(i >= n_up)
+        def _():
+            down_chunk(i, slot)
+
+        start(i, False)
+
+        @pl.when(i + AHEAD < last)
+        def _():
+            @pl.when(i + AHEAD - n_slot >= first)
+            def _():
+                finish(i + AHEAD - n_slot, False)
+            start(i + AHEAD, True)
+
+    for i in range(last - n_slot, last):
+        finish(jnp.int32(i), False)
+
+
+def update_first(n_up, width, last, clip, rate, w1, m1, v1, gb1, w2, m2, v2, gb2, x, *rest):
+    update_kernel(0, last, n_up, width, clip, rate, w1, m1, v1, gb1, w2, m2, v2, gb2, x, None, *rest)
+
+
+def update_second(n_up, width, first, last, clip, rate, w2, m2, v2, gb2, hid, _w, _m, _v, nw2, nm2, nv2, mine, theirs, *scratch):
+    update_kernel(first, last, n_up, width, clip, rate, None, None, None, None, w2, m2, v2, gb2, None, hid,
+                  None, None, None, nw2, nm2, nv2, None, mine, theirs, *scratch)
 
 
 def forward_kernel(n_chunk, n_micro, half, width, cut, mine_a, got_a, mine_b, theirs_b, x, nw1, nw2, y,
@@ -364,16 +443,15 @@
         smem = pl.BlockSpec(memory_space=pltpu.SMEM)
         dma = pltpu.SemaphoreType.DMA
 
+        resident = 4 * 2 * d_model * ff
         mean_up, mean_down, clip = pl.pallas_call(
             functools.partial(grad_kernel, n_chunk, width),
-            out_shape=(jax.ShapeDtypeStruct((n_chunk, d_model, width), F32),
-                       jax.ShapeDtypeStruct((n_chunk, width, d_model), F32),
+            out_shape=(pltpu.VMEM((n_chunk, d_model, width), F32),
+                       pltpu.VMEM((n_chunk, width, d_model), F32),
                        jax.ShapeDtypeStruct((8, 128), F32)),
             in_specs=[hbm, hbm, hbm, hbm, vmem, vmem, smem],
-            out_specs=(hbm, hbm, vmem),
+            out_specs=(vmem, vmem, vmem),
             scratch_shapes=[
-                pltpu.VMEM((n_chunk, d_model, width), F32),
-                pltpu.VMEM((n_chunk, width, d_model), F32),
                 pltpu.VMEM((n_chunk, d_model, width), F32),
                 pltpu.VMEM((n_chunk, width, d_model), F32),
                 pltpu.VMEM((2, d_model, width), F32),
@@ -388,62 +466,60 @@
                 pltpu.VMEM((4, 8, 128), F32),
                 dma((2, 2)), dma((2, 2)),
                 dma((n_chunk,)), dma((n_chunk,)), dma((n_chunk,)), dma((n_chunk,)),
-                dma((n_chunk,)), dma((n_chunk,)),
                 dma((2,)), dma((2,)), dma((3,)), dma((4,)),
             ],
-            compiler_params=pltpu.CompilerParams(collective_id=0, has_side_effects=True, vmem_limit_bytes=VMEM_MAX),
+            compiler_params=pltpu.CompilerParams(collective_id=0, has_side_effects=True, vmem_limit_bytes=VMEM_MAX - resident - SPARE),
             name="grad_exchange",
         )(w_up[0], w_down[0], g_up[0, 0], g_down[0, 0], acts_last[0], grad_out, max_norm)
 
-        x_all = x_next.reshape(n_micro * rows, d_model)
-        n_col = d_model // COLS
-        n_first = n_col * 3 // 5
+        n_up = ff // COLS
+        n_first = d_model // COLS // 2
         cut = n_first * COLS
-        mean_down = mean_down.reshape(1, ff, d_model)
-        up_block = pl.BlockSpec((None, d_model, width), lambda j: (0, 0, jnp.minimum(j, n_chunk - 1)))
-        up_chunk = pl.BlockSpec((None, d_model, width), lambda j: (jnp.minimum(j, n_chunk - 1), 0, 0))
-        col_a = pl.BlockSpec((None, ff, COLS), lambda j: (0, 0, jnp.maximum(j - n_chunk, 0)))
-        col_b = pl.BlockSpec((None, ff, COLS), lambda j: (0, 0, j + n_first))
-        piece_a = pl.BlockSpec((n_micro, half, COLS), lambda j: (0, 0, jnp.maximum(j - n_chunk, 0)))
-        piece_b = pl.BlockSpec((n_micro, half, COLS), lambda j: (0, 0, j))
-        x_block = pl.BlockSpec((n_micro * rows, d_model), lambda j: (0, 0))
-        hid_block = pl.BlockSpec((n_micro * rows, ff), lambda j: (0, 0))
+        last = n_up + 2 * (d_model // COLS)
+        middle = n_up + 2 * n_first
         up_out = jax.ShapeDtypeStruct(w_up.shape, F32)
         down_out = jax.ShapeDtypeStruct(w_down.shape, F32)
         part_a = jax.ShapeDtypeStruct((n_micro, half, cut), F32)
         part_b = jax.ShapeDtypeStruct((n_micro, half, d_model - cut), F32)
-        prod = [pltpu.VMEM((n_micro, rows, COLS), F32)]
+
+        def scratch(x_shape):
+            return [pltpu.VMEM((3, SLOTS, d_model, COLS), F32),
+                    pltpu.VMEM(x_shape, BF16),
+                    pltpu.VMEM((n_micro, rows, COLS), F32),
+                    dma((3, SLOTS)), dma((3, SLOTS)), dma(())]
 
         def cost(units):
-            return pl.CostEstimate(flops=2 * n_micro * rows * units, bytes_accessed=28 * units, transcendentals=2 * units)
-
+            return pl.CostEstimate(flops=2 * n_micro * rows * units, bytes_accessed=24 * units, transcendentals=2 * units)
+
+        def stay(array):
+            return pltpu.with_memory_space_constraint(array, pltpu.VMEM)
+
+        params = pltpu.CompilerParams(vmem_limit_bytes=VMEM_MAX - resident - 2 * SPARE)
         nw1, nm1, nv1, nw2, nm2, nv2, hid, mine_a, theirs_a = pl.pallas_call(
-            functools.partial(update_first, n_chunk, width),
-            grid=(n_chunk + n_first,),
+            functools.partial(update_first, n_up, width, middle),
             out_shape=(up_out, up_out, up_out, down_out, down_out, down_out,
                        jax.ShapeDtypeStruct((n_micro * rows, ff), BF16), part_a, part_a),
-            in_specs=[smem, smem, up_block, up_block, up_block, up_chunk, col_a, col_a, col_a, col_a, x_block],
-            out_specs=(up_block, up_block, up_block, col_a, col_a, col_a, hid_block, piece_a, piece_a),
-            scratch_shapes=prod,
-            compiler_params=pltpu.CompilerParams(vmem_limit_bytes=VMEM_MAX),
+            in_specs=[smem, smem, hbm, hbm, hbm, vmem, hbm, hbm, hbm, vmem, hbm],
+            out_specs=(hbm, hbm, hbm, hbm, hbm, hbm, vmem, vmem, vmem),
+            scratch_shapes=scratch(x_next.shape),
+            compiler_params=params,
             cost_estimate=cost(d_model * ff + cut * ff),
             name="update_first",
-        )(clip, learn_rate, w_up, m_up, v_up, mean_up, w_down, m_down, v_down, mean_down, x_all)
+        )(clip, learn_rate, w_up, m_up, v_up, stay(mean_up), w_down, m_down, v_down, stay(mean_down), x_next)
 
         got_a = lax.ppermute(theirs_a, ('model', 'stage'), [(0, 2), (2, 0)])
 
         nw2, nm2, nv2, mine_b, theirs_b = pl.pallas_call(
-            update_second,
-            grid=(n_col - n_first,),
+            functools.partial(update_second, n_up, width, middle, last),
             out_shape=(down_out, down_out, down_out, part_b, part_b),
-            in_specs=[smem, smem, col_b, col_b, col_b, col_b, hid_block, hbm, hbm, hbm],
-            out_specs=(col_b, col_b, col_b, piece_b, piece_b),
-            scratch_shapes=prod,
+            in_specs=[smem, smem, hbm, hbm, hbm, vmem, vmem, hbm, hbm, hbm],
+            out_specs=(hbm, hbm, hbm, vmem, vmem),
+            scratch_shapes=scratch((1, 8, 128)),
             input_output_aliases={7: 0, 8: 1, 9: 2},
-            compiler_params=pltpu.CompilerParams(vmem_limit_bytes=VMEM_MAX),
+            compiler_params=params,
             cost_estimate=cost((d_model - cut) * ff),
             name="update_second",
-        )(clip, learn_rate, w_down, m_down, v_down, mean_down, hid, nw2, nm2, nv2)
+        )(clip, learn_rate, w_down, m_down, v_down, stay(mean_down), hid, nw2, nm2, nv2)
 
         y_next = pl.pallas_call(
             functools.partial(forward_kernel, n_chunk, n_micro, half, width, cut),

time: 729 us -> 715 us (0.981)
  Pallas kernels: 720 us -> 705 us
    pallas_call x2, Pallas kernels: 83.5 us -> 66.6 us  [the longest x1 48.4 us: device_step(): pl.pallas_call(functools.partial(update_first, n_up, width, middle), out_...]
where the time goes in v3:
time: 715 us
  Pallas kernels  705 us (99%)
    pallas_call x1, Pallas kernels, device_step(): pl.pallas_call(functools.partial(grad_kernel, n_chunk, width), out_shape=...  574 us
    pallas_call x1, Pallas kernels, device_step(): pl.pallas_call(functools.partial(forward_kernel, n_chunk, n_micro, half,...  64 us
    pallas_call x1, Pallas kernels, device_step(): pl.pallas_call(functools.partial(update_first, n_up, width, middle), out_...  48.4 us
    pallas_call x1, Pallas kernels, device_step(): pl.pallas_call(functools.partial(update_second, n_up, width, middle, last...  18.3 us
  transfers between devices with their start and end apart: 1, of which 0 were waited for; matrix products, arithmetic and copies ran while one was open for 0% of the time, Pallas kernels for 3%

profile of v3, /device:TPU:0, one launch (start us, length us, event | category | flops | bytes accessed | tf_op | source)
XLA Modules:
  0.0 714.5 jit_solution(14146671737032551450)
XLA Ops:
  1.9 574.1 %grad_exchange.1 = (f32[10,1280,256]{2,1,0:T(8,128)S(1)}, f32[10,256,1280]{2,1,0:T(8,128)S(1)}, f32[8,128]{1,0:T(8,128)}) custom-call(f32[1280,2560]{1,0:T(8,128)} %bitcast.6, f32[2560,1280]{1,0:T(8,128)} %bitcast.5, f32[1280,2560]{1,0:T(8,128)} %bitcast.7, f32[2560,1280]{1,0:T(8,128)} %bitcast.8, bf16[256,1280]{1,0:T(8,128)(2,1)} %bitcast.9, ...), custom_call_target="tpu_custom_call" | custom-call | tf_op jit(solution)/shard_map/grad_exchange/pallas_call | solution.py:447
  576.0 0.0 copy-start.2
  576.0 48.4 %update_first.1 = (f32[1,1280,2560]{2,1,0:T(8,128)}, f32[1,1280,2560]{2,1,0:T(8,128)}, f32[1,1280,2560]{2,1,0:T(8,128)}, f32[1,2560,1280]{2,1,0:T(8,128)}, f32[1...) custom-call(f32[8,128]{1,0:T(8,128)} %get-tuple-element.24.clip, ...), custom_call_target="tpu_custom_call" | custom-call | flops 7549747200 | bytes 117964800 | tf_op jit(solution)/shard_map/update_first/pallas_call | solution.py:498
  624.4 3.0 collective-permute-start
  627.4 0.0 copy-done.2
  627.4 18.3 %update_second.1 = (f32[1,2560,1280]{2,1,0:T(8,128)}, f32[1,2560,1280]{2,1,0:T(8,128)}, f32[1,2560,1280]{2,1,0:T(8,128)}, f32[3,128,640]{2,1,0:T(8,128)S(1)}, f32[3,128,640]{2,1,0:T(8,128)S(1)}) custom-call(f32[8,128]{1,0:T(8,128)S(1)} %copy-done.2, f32[1]{0:T(128)S(6)} %copy.27.rate, ...), custom_call_target="tpu_custom_call", output_to_operand_aliasing={{0}: (7, {}), {1}: (8, {}), {2}: (9, {})} | custom-call | flops 2516582400 | bytes 39321600 | tf_op jit(solution)/shard_map/update_second/pallas_call | solution.py:512
  645.7 0.0 copy-start
  645.7 0.9 copy-done
  646.7 0.0 copy-start.1
  646.7 0.9 copy-done.1
  647.6 0.0 collective-permute-done.got_a
  647.6 64.0 %forward_exchange.1 = bf16[3,256,1280]{2,1,0:T(8,128)(2,1)} custom-call(f32[3,128,640]{2,1,0:T(8,128)} %get-tuple-element.37.mine_a, f32[3,128,640]{2,1,0:T(8,128)} %collective-permute-done.got_a, f32[3,128,640]{2,1,0:T(8,128)} %copy-done, f32[3,128,640]{2,1,0:T(8,128)} %copy-done.1, bf16[3,256,1280]{2,1,0:T(8,128)(2,1)} %x.3, ...), custom_call_target="tpu_custom_call" | custom-call | tf_op jit(solution)/shard_map/forward_exchange/pallas_call | solution.py:524
  711.6 2.9 copy.29
Async XLA Ops:
  576.0 51.4 %copy-start.2 = (f32[8,128]{1,0:T(8,128)S(1)}, f32[8,128]{1,0:T(8,128)}, u32[]{:S(2)}) copy-start(f32[8,128]{1,0:T(8,128)} %get-tuple-element.24.clip) | copy-start | bytes 12292
  624.4 23.2 %collective-permute-start = (f32[3,128,640]{2,1,0:T(8,128)}, f32[3,128,640]{2,1,0:T(8,128)}, u32[]{:S(2)}, u32[]{:S(2)}) collective-permute-start(f32[3,128,640]{2,1,0:T(8,128)} %get-tuple-element.38), channel_id=1, source_target_pairs={{0,4},{4,0},{2,6},{6,2}} | collective-permute-start | bytes 2949128 | tf_op jit(solution)/shard_map/ppermute | solution.py:510
  645.7 1.0 copy-start
  646.7 0.9 copy-start.1

commit v4 on v1

v4 whole, which is shorter than its diff:
```python
import functools

import jax
import jax.numpy as jnp
from jax import lax
from jax.experimental import pallas as pl
from jax.experimental.pallas import tpu as pltpu
from jax.sharding import PartitionSpec as P

ADAM_STEP = 10
BETA_ONE = 0.9
BETA_TWO = 0.95
ADAM_EPS = 1e-8
WEIGHT_DECAY = 0.1
NORM_EPS = 1e-6
ONE_CORR = 1.0 - BETA_ONE ** ADAM_STEP
TWO_CORR = 1.0 - BETA_TWO ** ADAM_STEP
ROOT_EPS = ADAM_EPS * TWO_CORR ** 0.5
ROOT_GAIN = TWO_CORR ** 0.5 / ONE_CORR
TINY = 1.1754944e-38
HUGE = 3.4028235e38
GELU_A = 0.7978845608028654
GELU_B = 0.044715
NT = (((1,), (1,)), ((), ()))
TN = (((0,), (0,)), ((), ()))
MESH = pl.DeviceIdType.MESH
VMEM_MAX = 67_043_328
CHUNK = 128
SLOTS = 8
AHEAD = 5
SPARE = 1 << 20
F32 = jnp.float32
BF16 = jnp.bfloat16


def gelu_parts(z):
    t = jnp.tanh(GELU_A * (z + GELU_B * (z * z * z)))
    return t, z * (0.5 * (1.0 + t))


def gelu_slope(z, t):
    return 0.5 * (1.0 + t) + 0.5 * z * (1.0 - t * t) * (GELU_A * (1.0 + 3.0 * GELU_B * z * z))


def dot(a, b, dims=(((1,), (0,)), ((), ()))):
    return lax.dot_general(a, b, dims, preferred_element_type=F32)


def positions():
    return lax.axis_index("model"), lax.axis_index("data"), lax.axis_index("stage")


def entry_barrier(peers):
    barrier = pltpu.get_barrier_semaphore()
    for peer in peers:
        pl.semaphore_signal(barrier, inc=1, device_id=peer, device_id_type=MESH)
    pl.semaphore_wait(barrier, len(peers))


def remote(src, dst, send, recv, peer):
    return pltpu.make_async_remote_copy(src_ref=src, dst_ref=dst, send_sem=send, recv_sem=recv, device_id=peer, device_id_type=MESH)


def adamw(scale, rate, w, mom, sec, mean):
    grad = scale * mean
    mom_new = BETA_ONE * mom + (1.0 - BETA_ONE) * grad
    sec_new = BETA_TWO * sec + ((1.0 - BETA_TWO) * grad) * grad
    root = sec_new * lax.rsqrt(jnp.minimum(sec_new + TINY, HUGE))
    w_new = w * (1.0 - rate * WEIGHT_DECAY) - (rate * ROOT_GAIN) * (mom_new / (root + ROOT_EPS))
    return w_new, mom_new, sec_new


def grad_kernel(n_chunk, width, w1, w2, g1, g2, m1, v1, m2, v2, acts, dy, x, max_norm, rate,
                gr1, gr2, clip, act_half,
                gs1, gs2, w1b, w2b, gvec, part, got, x_buf, sq1, sq2, sq_out, sq_in,
                w_sem, g_sem, send1, send2, recv1, recv2, part_sem, gvec_sem, sq_send, sq_recv,
                row_sem, f_sem, rs_send, rs_recv):
    m, d, s = positions()
    peer_x = (m, 1 - d, s)
    peer_y = (1 - m, d, s)
    peer_c = (m, d, 1 - s)
    peer_d = (1 - m, d, 1 - s)
    d_model = w1.shape[0]
    is_last = s == 1
    is_first = s == 0

    def loads(j):
        slot = lax.rem(j, 2)
        cols = pl.ds(pl.multiple_of(j * width, width), width)
        return (pltpu.make_async_copy(w1.at[:, cols], w1b.at[slot], w_sem.at[0, slot]),
                pltpu.make_async_copy(w2.at[cols, :], w2b.at[slot], w_sem.at[1, slot]),
                pltpu.make_async_copy(g2.at[cols, :], gs2.at[j], g_sem.at[0, slot]),
                pltpu.make_async_copy(g1.at[:, cols], gs1.at[j], g_sem.at[1, slot]))

    load_dy = pltpu.make_async_copy(dy, gvec, row_sem)
    load_x = pltpu.make_async_copy(x, x_buf, row_sem)

    @pl.when(is_last)
    def _():
        load_dy.start()

    for first in (0, 1):
        for copy in loads(first):
            copy.start()

    @pl.when(is_first)
    def _():
        load_x.start()

    entry_barrier((peer_x, peer_y, peer_c, peer_d))

    hand_over = remote(x_buf.at[0], gvec, gvec_sem.at[0], gvec_sem.at[1], peer_c)
    swap_part = remote(part, got.at[:2], part_sem.at[0], part_sem.at[1], peer_y)

    @pl.when(is_last)
    def _():
        part[...] = jnp.zeros_like(part)
        load_dy.wait()

    @pl.when(is_first)
    def _():
        load_x.wait()
        hand_over.wait_recv()

    def send_two(j):
        return remote(gs2.at[j], gr2.at[j], send2.at[j], recv2.at[j], peer_x)

    def send_one(j):
        return remote(gs1.at[j], gr1.at[j], send1.at[j], recv1.at[j], peer_x)

    @pl.loop(0, n_chunk)
    def _(j):
        slot = lax.rem(j, 2)
        copies = loads(j)
        copies[0].wait()
        up = w1b[slot].astype(BF16)
        rows = acts[...]
        grad = gvec[...]
        z = dot(rows, up)
        t, act = gelu_parts(z)
        hid = act.astype(BF16)
        copies[2].wait()
        gs2[j] += dot(hid, grad, TN)
        send_two(j).start()
        copies[1].wait()
        grad_hid = dot(grad, w2b[slot].astype(BF16), NT)
        grad_pre = (gelu_slope(z, t) * grad_hid).astype(BF16)
        copies[3].wait()
        gs1[j] += dot(rows, grad_pre, TN)
        send_one(j).start()

        @pl.when(is_last)
        def _():
            part[...] += dot(grad_pre, up, NT).reshape(part.shape)

        @pl.when(j + 2 < n_chunk)
        def _():
            for copy in loads(j + 2):
                copy.start()

    @pl.when(is_last)
    def _():
        swap_part.start()
        swap_part.wait()
        total = (part[...] + got[:2]).reshape(gvec.shape)
        x_buf[0] = (gvec[...].astype(F32) + total).astype(BF16)
        hand_over.start()

    n_up = n_chunk // 2
    n_pair = 2 * n_up

    def fetch(p):
        base = lax.rem(p, 3) * 6

        @pl.when(p < n_up)
        def _():
            for q, ref in enumerate((w1, m1, v1)):
                for h in (0, 1):
                    cols = pl.ds(pl.multiple_of((2 * p + h) * width, width), width)
                    pltpu.make_async_copy(ref.at[:, cols], gs1.at[base + 2 * q + h], f_sem.at[base + 2 * q + h]).start()

        @pl.when(p >= n_up)
        def _():
            rows = pl.ds(pl.multiple_of(lax.rem(p - n_up, 2) * d_model, d_model), d_model)
            for q, ref in enumerate((w2, m2, v2)):
                for h in (0, 1):
                    cols = pl.ds(pl.multiple_of((2 * ((p - n_up) // 2) + h) * width, width), width)
                    pltpu.make_async_copy(ref.at[rows, cols], gs1.at[base + 2 * q + h], f_sem.at[base + 2 * q + h]).start()

    def free_and_fetch(lo, hi, p):
        for i in range(lo, hi):
            send_one(i).wait_send()

        @pl.when(is_first)
        def _():
            fetch(jnp.int32(p))

    sq1[...] = jnp.zeros_like(sq1)
    sq2[...] = jnp.zeros_like(sq2)

    @pl.loop(0, n_chunk)
    def _(j):
        send_two(j).wait_recv()
        mean = (gs2[j] + gr2[j]) * 0.5
        gr2[j] = mean
        sq2[...] += jnp.sum((mean * mean).reshape(-1, 8, mean.shape[1]), axis=0)
        send_one(j).wait_recv()
        mean = (gs1[j] + gr1[j]) * 0.5
        gr1[j] = mean
        sq1[...] += jnp.sum((mean * mean).reshape(-1, 8, mean.shape[1]), axis=0)

        @pl.when(j == 10)
        def _():
            free_and_fetch(0, 6, 0)

        @pl.when(j == 15)
        def _():
            free_and_fetch(6, 12, 1)

    sq_out[...] = jnp.full(sq_out.shape, jnp.sum(sq1[...]) + jnp.sum(sq2[...]), F32)
    mine = 2 * m + s
    others = ((peer_y, 2 * (1 - m) + s), (peer_c, 2 * m + 1 - s), (peer_d, 2 * (1 - m) + 1 - s))
    shares = [remote(sq_out, sq_in.at[mine], sq_send.at[k], sq_recv.at[mine], peer) for k, (peer, _) in enumerate(others)]
    for copy in shares:
        copy.start()
    free_and_fetch(12, n_chunk, 2)
    sq_in[mine] = sq_out[...]
    for peer, index in others:
        remote(sq_out, sq_in.at[index], sq_send.at[0], sq_recv.at[index], peer).wait_recv()
    total = (sq_in[0] + sq_in[1]) + (sq_in[2] + sq_in[3])
    clip[...] = jnp.minimum(1.0, max_norm[0] / (jnp.sqrt(total) + NORM_EPS))

    for j in range(n_chunk):
        send_two(j).wait_send()
    for copy in shares:
        copy.wait_send()

    @pl.when(is_last)
    def _():
        hand_over.wait_send()

    @pl.when(is_first)
    def _():
        scale = clip[0, 0]
        step_rate = rate[0]
        n_micro, n_row = x_buf.shape[:2]
        group = 2 * n_micro
        half = n_row // 2
        wide = 2 * width
        n_block = d_model // wide

        def new_weights(base, means):
            parts = [adamw(scale, step_rate, gs1[base + h], gs1[base + 2 + h], gs1[base + 4 + h], means[h])[0].astype(BF16) for h in (0, 1)]
            return jnp.concatenate(parts, axis=1)

        def block_copy(c):
            cols = pl.ds(pl.multiple_of(c * wide, wide), wide)
            return remote(gs2.at[2 * group + n_micro:2 * group + 2 * n_micro, :, cols], got.at[:, :, cols], rs_send.at[c], rs_recv.at[c], peer_y)

        @pl.loop(0, n_pair)
        def _(p):
            base = lax.rem(p, 3) * 6
            for i in range(6):
                pltpu.make_async_copy(w1.at[:, :width], gs1.at[base + i], f_sem.at[base + i]).wait()

            @pl.when(p < n_up)
            def _():
                new = new_weights(base, [gr1[2 * p], gr1[2 * p + 1]])
                act = gelu_parts(dot(x_buf[...].reshape(-1, d_model), new))[1].astype(BF16).astype(F32)
                cols = pl.ds(pl.multiple_of(lax.rem(p, n_block) * wide, wide), wide)
                gs2[pl.ds((p // n_block) * group, group), :, cols] = act.reshape(group, half, wide)

            @pl.when(p >= n_up)
            def _():
                c = (p - n_up) // 2
                upper = lax.rem(p - n_up, 2)
                means = []
                for h in (0, 1):
                    cols = pl.ds(pl.multiple_of((2 * c + h) * width, width), width)
                    means.append(gr2[pl.ds(upper * n_up, n_up), :, cols].reshape(d_model, width))
                new = new_weights(base, means)
                cols = pl.ds(pl.multiple_of(c * wide, wide), wide)
                spot = [(g // n_block, slice(None), slice(g % n_block * wide, g % n_block * wide + wide)) for g in range(group)]
                for lo in range(0, group, n_micro):
                    rows = gs2[pl.ds(upper * group + lo, n_micro)].reshape(-1, d_model).astype(BF16)
                    res = dot(rows, new).reshape(n_micro, half, wide)

                    @pl.when(upper == 0)
                    def _():
                        for g in range(n_micro):
                            part[spot[lo + g]] = res[g]

                    @pl.when(upper == 1)
                    def _():
                        for g in range(n_micro):
                            part[spot[lo + g]] += res[g]

                @pl.when(upper == 1)
                def _():
                    for k in range(n_micro):
                        even, odd = part[spot[2 * k]], part[spot[2 * k + 1]]
                        gs2[2 * group + k, :, cols] = jnp.where(m == 0, even, odd)
                        gs2[2 * group + n_micro + k, :, cols] = jnp.where(m == 0, odd, even)
                    block_copy(c).start()

            @pl.when(p + 3 < n_pair)
            def _():
                fetch(p + 3)

        for c in range(n_block):
            block_copy(c).wait_recv()
            cols = slice(c * wide, (c + 1) * wide)
            for k in range(n_micro):
                rows = x_buf[k, pl.ds(pl.multiple_of(m * half, half), half), cols].astype(F32)
                act_half[k, :, cols] = (rows + (gs2[2 * group + k, :, cols] + got[k, :, cols])).astype(BF16)
        for c in range(n_block):
            block_copy(c).wait_send()


def update_kernel(clip, rate, w1, m1, v1, gb1, w2, m2, v2, gb2, nw1, nm1, nv1, nw2, nm2, nv2, ring, in_sem, out_sem):
    n_up, deep, wide = gb1.shape
    n_slot = ring.shape[1]
    last = 2 * n_up
    block = deep // gb2.shape[1]
    scale = clip[0, 0]
    step_rate = rate[0]

    def place(i):
        col = pl.multiple_of(((i - n_up) // 2) * wide, wide)
        row = pl.multiple_of(lax.rem(i - n_up, 2) * deep, deep)
        return pl.ds(row, deep), pl.ds(col, wide)

    def start(i, fetch):
        slot = lax.rem(i, n_slot)
        sem = in_sem if fetch else out_sem

        def go(k, far):
            near = ring.at[k, slot]
            pair = (far, near) if fetch else (near, far)
            pltpu.make_async_copy(*pair, sem.at[k, slot]).start()

        @pl.when(i < n_up)
        def _():
            cols = pl.ds(pl.multiple_of(i * wide, wide), wide)
            for k, ref in enumerate((w1, m1, v1) if fetch else (nw1, nm1, nv1)):
                go(k, ref.at[0, :, cols])

        @pl.when(i >= n_up)
        def _():
            rows, cols = place(i)
            for k, ref in enumerate((w2, m2, v2) if fetch else (nw2, nm2, nv2)):
                go(k, ref.at[0, rows, cols])

    def finish(i, fetch):
        slot = lax.rem(i, n_slot)
        for k, ref in enumerate((w2, m2, v2) if fetch else (nw2, nm2, nv2)):
            far, near = ref.at[0, :deep, :wide], ring.at[k, slot]
            sem = (in_sem if fetch else out_sem).at[k, slot]
            (pltpu.make_async_copy(far, near, sem) if fetch else pltpu.make_async_copy(near, far, sem)).wait()

    for i in range(AHEAD):
        start(jnp.int32(i), True)

    def step(slot, mean):
        new, mom, sec = adamw(scale, step_rate, ring[0, slot], ring[1, slot], ring[2, slot], mean)
        ring[0, slot] = new
        ring[1, slot] = mom
        ring[2, slot] = sec

    @pl.loop(0, last)
    def _(i):
        slot = lax.rem(i, n_slot)
        finish(i, True)

        @pl.when(i < n_up)
        def _():
            step(slot, gb1[i])

        @pl.when(i >= n_up)
        def _():
            cols = place(i)[1]
            step(slot, gb2[pl.ds(lax.rem(i - n_up, 2) * block, block), :, cols].reshape(deep, wide))

        start(i, False)

        @pl.when(i + AHEAD < last)
        def _():
            @pl.when(i + AHEAD - n_slot >= 0)
            def _():
                finish(i + AHEAD - n_slot, False)
            start(i + AHEAD, True)

    for i in range(last - n_slot, last):
        finish(jnp.int32(i), False)


def forward_kernel(n_chunk, width, from_core, from_diag, nw1, nw2, y,
                   w1, w2, w1f, w2f, act, own_half, peer_half, part, part_in,
                   w_sem, p_send, p_recv, y_send, y_recv, f_send, f_recv, ready):
    m, d, s = positions()
    n_micro, half = own_half.shape[:2]
    peer_y = (1 - m, d, s)
    peer_c = (m, d, 1 - s)

    def loads(j):
        slot = lax.rem(j, 2)
        cols = pl.ds(pl.multiple_of(j * width, width), width)
        return (pltpu.make_async_copy(nw1.at[0, :, cols], w1f.at[slot], w_sem.at[0, slot]),
                pltpu.make_async_copy(nw2.at[0, cols, :], w2f.at[slot], w_sem.at[1, slot]))

    barrier = pltpu.get_barrier_semaphore()

    @pl.when(s == 1)
    def _():
        for first in (0, 1):
            for copy in loads(first):
                copy.start()
        pl.semaphore_signal(barrier, inc=1, device_id=peer_y, device_id_type=MESH)
        pl.semaphore_signal(barrier, inc=1, device_id=peer_c, device_id_type=MESH)

    pl.semaphore_wait(barrier, 1)

    @pl.when(s == 0)
    def _():
        pl.semaphore_signal(ready, inc=1, device_id=peer_c, device_id_type=MESH)

    mine = pl.ds(pl.multiple_of(m * half, half), half)
    theirs = pl.ds(pl.multiple_of((1 - m) * half, half), half)

    def send_part(k):
        return remote(part.at[k, theirs, :], part_in.at[k], p_send.at[k], p_recv.at[k], peer_y)

    def swap_y(k):
        return remote(own_half.at[k], peer_half.at[k], y_send.at[0, k], y_recv.at[0, k], peer_y)

    def give_own(k):
        return remote(own_half.at[k], y.at[k, mine, :], y_send.at[1, k], y_recv.at[1, k], peer_c)

    def pass_on(k):
        return remote(peer_half.at[k], y.at[k, theirs, :], f_send.at[k], f_recv.at[k], peer_c)

    @pl.when(s == 0)
    def _():
        for k in range(n_micro):
            give_own(k).wait_recv()
            pass_on(k).wait_recv()

    @pl.when(s == 1)
    def _():
        act[:, mine, :] = from_core[...]
        act[:, theirs, :] = from_diag[...]

        def chunk(k, j):
            hid = gelu_parts(dot(act[k], w1[j]))[1].astype(BF16)
            part[k] += dot(hid, w2[j])

        def finish(k):
            send_part(k).wait_recv()
            out = act[k, mine, :].astype(F32) + (part[k, mine, :] + part_in[k])
            own_half[k] = out.astype(BF16)
            swap_y(k).start()
            y[k, mine, :] = own_half[k]

        for k in range(n_micro):
            part[k] = jnp.zeros_like(part[k])

            @pl.loop(0, n_chunk)
            def _(j):
                if k == 0:
                    slot = lax.rem(j, 2)
                    copies = loads(j)
                    copies[0].wait()
                    w1[j] = w1f[slot].astype(BF16)
                    copies[1].wait()
                    w2[j] = w2f[slot].astype(BF16)

                    @pl.when(j + 2 < n_chunk)
                    def _():
                        for copy in loads(j + 2):
                            copy.start()
                chunk(k, j)

            send_part(k).start()
            if k > 0:
                finish(k - 1)
        finish(n_micro - 1)
        pl.semaphore_wait(ready, 1)
        for k in range(n_micro):
            give_own(k).start()
        for k in range(n_micro):
            swap_y(k).wait_recv()
            pass_on(k).start()
            y[k, theirs, :] = peer_half[k]
        for k in range(n_micro):
            send_part(k).wait_send()
            swap_y(k).wait_send()
            give_own(k).wait_send()
            pass_on(k).wait_send()


def solution(mesh):
    up_spec = P('stage', None, 'model')
    down_spec = P('stage', 'model', None)
    row_spec = P(None, 'data', None)
    in_specs = (up_spec, down_spec, up_spec, down_spec, up_spec, down_spec, P('data', 'stage', None, 'model'), P('data', 'stage', 'model', None), P('stage', 'data', None), P('data', None), row_spec, P(None), P(None))
    out_specs = (up_spec, down_spec, up_spec, down_spec, up_spec, down_spec, row_spec)

    def device_step(w_up, w_down, m_up, m_down, v_up, v_down, g_up, g_down, acts_last, grad_out, x_next, learn_rate, max_norm):
        d_model, ff = w_up.shape[1:]
        rows = grad_out.shape[0]
        n_micro = x_next.shape[0]
        width = CHUNK
        n_chunk = ff // width
        half = rows // 2
        hbm = pl.BlockSpec(memory_space=pl.ANY)
        vmem = pl.BlockSpec(memory_space=pltpu.VMEM)
        smem = pl.BlockSpec(memory_space=pltpu.SMEM)
        dma = pltpu.SemaphoreType.DMA
        resident = 4 * 2 * d_model * ff
        n_block = d_model // (2 * width)

        mean_up, mean_down, clip, act_half = pl.pallas_call(
            functools.partial(grad_kernel, n_chunk, width),
            out_shape=(pltpu.VMEM((n_chunk, d_model, width), F32),
                       pltpu.VMEM((n_chunk, width, d_model), F32),
                       jax.ShapeDtypeStruct((8, 128), F32),
                       jax.ShapeDtypeStruct((n_micro, half, d_model), BF16)),
            in_specs=[hbm] * 8 + [vmem, hbm, hbm, smem, smem],
            out_specs=(vmem, vmem, vmem, vmem),
            scratch_shapes=[
                pltpu.VMEM((n_chunk, d_model, width), F32),
                pltpu.VMEM((n_chunk, width, d_model), F32),
                pltpu.VMEM((2, d_model, width), F32),
                pltpu.VMEM((2, width, d_model), F32),
                pltpu.VMEM((rows, d_model), BF16),
                pltpu.VMEM((2, half, d_model), F32),
                pltpu.VMEM((n_micro, half, d_model), F32),
                pltpu.VMEM((n_micro, rows, d_model), BF16),
                pltpu.VMEM((8, width), F32),
                pltpu.VMEM((8, d_model), F32),
                pltpu.VMEM((8, 128), F32),
                pltpu.VMEM((4, 8, 128), F32),
                dma((2, 2)), dma((2, 2)),
                dma((n_chunk,)), dma((n_chunk,)), dma((n_chunk,)), dma((n_chunk,)),
                dma((2,)), dma((2,)), dma((3,)), dma((4,)),
                dma(()), dma((18,)), dma((n_block,)), dma((n_block,)),
            ],
            compiler_params=pltpu.CompilerParams(collective_id=0, has_side_effects=True, vmem_limit_bytes=VMEM_MAX - resident - SPARE),
            name="grad_exchange",
        )(w_up[0], w_down[0], g_up[0, 0], g_down[0, 0], m_up[0], v_up[0], m_down[0], v_down[0], acts_last[0], grad_out, x_next, max_norm, learn_rate)

        from_diag = lax.ppermute(act_half, ('model', 'stage'), [(0, 3), (2, 1)])
        from_core = lax.ppermute(act_half, ('model', 'stage'), [(0, 1), (2, 3)])

        def stay(array):
            return pltpu.with_memory_space_constraint(array, pltpu.VMEM)

        up_out = jax.ShapeDtypeStruct(w_up.shape, F32)
        down_out = jax.ShapeDtypeStruct(w_down.shape, F32)
        nw1, nm1, nv1, nw2, nm2, nv2 = pl.pallas_call(
            update_kernel,
            out_shape=(up_out, up_out, up_out, down_out, down_out, down_out),
            in_specs=[smem, smem, hbm, hbm, hbm, vmem, hbm, hbm, hbm, vmem],
            out_specs=(hbm,) * 6,
            scratch_shapes=[pltpu.VMEM((3, SLOTS, d_model, width), F32), dma((3, SLOTS)), dma((3, SLOTS))],
            compiler_params=pltpu.CompilerParams(vmem_limit_bytes=VMEM_MAX - resident - SPARE),
            cost_estimate=pl.CostEstimate(flops=2000 * d_model * ff, bytes_accessed=48 * d_model * ff, transcendentals=4 * d_model * ff),
            name="update",
        )(clip, learn_rate, w_up, m_up, v_up, stay(mean_up), w_down, m_down, v_down, stay(mean_down))

        f_width = 2 * width
        f_chunk = ff // f_width
        y_next = pl.pallas_call(
            functools.partial(forward_kernel, f_chunk, f_width),
            out_shape=jax.ShapeDtypeStruct(x_next.shape, BF16),
            in_specs=[vmem, vmem, hbm, hbm],
            out_specs=vmem,
            scratch_shapes=[
                pltpu.VMEM((f_chunk, d_model, f_width), BF16),
                pltpu.VMEM((f_chunk, f_width, d_model), BF16),
                pltpu.VMEM((2, d_model, f_width), F32),
                pltpu.VMEM((2, f_width, d_model), F32),
                pltpu.VMEM((n_micro, rows, d_model), BF16),
                pltpu.VMEM((n_micro, half, d_model), BF16),
                pltpu.VMEM((n_micro, half, d_model), BF16),
                pltpu.VMEM((n_micro, rows, d_model), F32),
                pltpu.VMEM((n_micro, half, d_model), F32),
                dma((2, 2)), dma((n_micro,)), dma((n_micro,)), dma((2, n_micro)), dma((2, n_micro)), dma((n_micro,)), dma((n_micro,)),
                pltpu.SemaphoreType.REGULAR,
            ],
            compiler_params=pltpu.CompilerParams(collective_id=1, has_side_effects=True, vmem_limit_bytes=VMEM_MAX),
            name="forward_exchange",
        )(from_core, from_diag, nw1, nw2)
        return nw1, nw2, nm1, nm2, nv1, nv2, y_next

    return jax.shard_map(device_step, mesh=mesh, in_specs=in_specs, out_specs=out_specs, check_vma=False)
```

time: 733 us -> 690 us (0.941)
  Pallas kernels: 728 us -> 681 us
    pallas_call x2, Pallas kernels: 154 us -> 65.6 us  [the longest x1 54.4 us: device_step(): pl.pallas_call(update_kernel, out_shape=(up_out, up_out, up_out, down_out...]
    pallas_call x1, Pallas kernels: 574 us -> 615 us  [device_step(): pl.pallas_call(functools.partial(grad_kernel, n_chunk, width), out_shape=...]
  transfers between devices with their start and end apart: 0 -> 2, of which waited for: 0 -> 0; matrix products, arithmetic and copies ran while one was open for 0% -> 0% of each run, Pallas kernels for 0% -> 8%
where the time goes in v4:
time: 690 us
  Pallas kernels  681 us (99%)
    pallas_call x1, Pallas kernels, device_step(): pl.pallas_call(functools.partial(grad_kernel, n_chunk, width), out_shape=...  615 us
    pallas_call x1, Pallas kernels, device_step(): pl.pallas_call(update_kernel, out_shape=(up_out, up_out, up_out, down_out...  54.4 us
  transfers between devices with their start and end apart: 2, of which 0 were waited for; matrix products, arithmetic and copies ran while one was open for 0% of the time, Pallas kernels for 8%

profile of v4, /device:TPU:0, one launch (start us, length us, event | category | flops | bytes accessed | tf_op | source)
XLA Modules:
  0.0 690.0 jit_solution(2709836578967183131)
XLA Ops:
  1.9 615.1 %grad_exchange.1 = (f32[20,1280,128]{2,1,0:T(8,128)S(1)}, f32[20,128,1280]{2,1,0:T(8,128)S(1)}, f32[8,128]{1,0:T(8,128)}, bf16[3,128,1280]{2,1,0:T(8,128)(2,1)}) custom-call(f32[1280,2560]{1,0:T(8,128)} %bitcast.9, f32[2560,1280]{1,0:T(8,128)} %bitcast.10, f32[1280,2560]{1,0:T(8,128)} %bitcast.15, f32[2560,1280]{1,0:T(8,128)} %bitcast.16, ...), custom_call_target="tpu_custom_call" | custom-call | tf_op jit(solution)/shard_map/grad_exchange/pallas_call | solution.py:522
  617.0 2.2 collective-permute-start
  619.2 2.2 collective-permute-start.1
  621.5 54.4 %update.1 = (f32[1,1280,2560]{2,1,0:T(8,128)}, f32[1,1280,2560]{2,1,0:T(8,128)}, f32[1,1280,2560]{2,1,0:T(8,128)}, f32[1,2560,1280]{2,1,0:T(8,128)}, f32[1,2560,1280]{2,1,0:T(8,128)}, /*index=5*/f32[1,2560,1280]{2,1,0:T(8,128)}) custom-call(f32[8,128]{1,0:T(8,128)} %get-tuple-element.17.clip, f32[1]{0:T(128)S(6)} %copy.21.rate, f32[1,1280,2560]{2,1,0:T(8,128)} %w1.1, ...), custom_call_target="tpu_custom_call" | custom-call | flops 6553600000 | bytes 157286400 | tf_op jit(solution)/shard_map/update/pallas_call | solution.py:560
  675.9 0.0 collective-permute-done.from_core
  675.9 0.0 collective-permute-done.1.from_diag
  675.9 11.2 %forward_exchange.1 = bf16[3,256,1280]{2,1,0:T(8,128)(2,1)} custom-call(bf16[3,128,1280]{2,1,0:T(8,128)(2,1)} %collective-permute-done.from_core, bf16[3,128,1280]{2,1,0:T(8,128)(2,1)} %collective-permute-done.1.from_diag, f32[1,1280,2560]{2,1,0:T(8,128)} %get-tuple-element.34.nw1, f32[1,2560,1280]{2,1,0:T(8,128)} %get-tuple-element.35.nw2), custom_call_target="tpu_custom_call" | custom-call | tf_op jit(solution)/shard_map/forward_exchange/pallas_call | solution.py:573
  687.1 2.9 copy.23
Async XLA Ops:
  617.0 58.9 %collective-permute-start = (bf16[3,128,1280]{2,1,0:T(8,128)(2,1)}, bf16[3,128,1280]{2,1,0:T(8,128)(2,1)}, u32[]{:S(2)}, u32[]{:S(2)}) collective-permute-start(bf16[3,128,1280]{2,1,0:T(8,128)(2,1)} %get-tuple-element.26), channel_id=1, source_target_pairs={{0,1},{4,5},{2,3},{6,7}} | collective-permute-start | bytes 2949128 | tf_op jit(solution)/shard_map/ppermute | solution.py:553
  619.2 56.6 %collective-permute-start.1 = (bf16[3,128,1280]{2,1,0:T(8,128)(2,1)}, bf16[3,128,1280]{2,1,0:T(8,128)(2,1)}, u32[]{:S(2)}, u32[]{:S(2)}) collective-permute-start(bf16[3,128,1280]{2,1,0:T(8,128)(2,1)} %get-tuple-element.26), channel_id=1, source_target_pairs={{0,5},{4,1},{2,7},{6,3}} | collective-permute-start | bytes 2949128 | tf_op jit(solution)/shard_map/ppermute | solution.py:552

commit v5 on v4

--- a/solution.py
+++ b/solution.py
@@ -317,7 +317,7 @@
             block_copy(c).wait_send()
 
 
-def update_kernel(clip, rate, w1, m1, v1, gb1, w2, m2, v2, gb2, nw1, nm1, nv1, nw2, nm2, nv2, ring, in_sem, out_sem):
+def update_kernel(clip, rate, w1, m1, v1, gb1, w2, m2, v2, gb2, nw1, nm1, nv1, nw2, nm2, nv2, keep1, keep2, ring, in_sem, out_sem):
     n_up, deep, wide = gb1.shape
     n_slot = ring.shape[1]
     last = 2 * n_up
@@ -366,6 +366,7 @@
         ring[0, slot] = new
         ring[1, slot] = mom
         ring[2, slot] = sec
+        return new
 
     @pl.loop(0, last)
     def _(i):
@@ -374,12 +375,14 @@
 
         @pl.when(i < n_up)
         def _():
-            step(slot, gb1[i])
+            keep1[i] = step(slot, gb1[i])
 
         @pl.when(i >= n_up)
         def _():
             cols = place(i)[1]
-            step(slot, gb2[pl.ds(lax.rem(i - n_up, 2) * block, block), :, cols].reshape(deep, wide))
+            rows = pl.ds(lax.rem(i - n_up, 2) * block, block)
+            new = step(slot, gb2[rows, :, cols].reshape(deep, wide))
+            keep2[rows, :, cols] = new.reshape(block, -1, wide)
 
         start(i, False)
 
@@ -394,27 +397,19 @@
         finish(jnp.int32(i), False)
 
 
-def forward_kernel(n_chunk, width, from_core, from_diag, nw1, nw2, y,
-                   w1, w2, w1f, w2f, act, own_half, peer_half, part, part_in,
-                   w_sem, p_send, p_recv, y_send, y_recv, f_send, f_recv, ready):
+def forward_kernel(from_core, from_diag, new1, new2, y,
+                   w1, w2, act, own_half, peer_half, part, part_in,
+                   p_send, p_recv, y_send, y_recv, f_send, f_recv, ready):
     m, d, s = positions()
     n_micro, half = own_half.shape[:2]
     peer_y = (1 - m, d, s)
     peer_c = (m, d, 1 - s)
 
-    def loads(j):
-        slot = lax.rem(j, 2)
-        cols = pl.ds(pl.multiple_of(j * width, width), width)
-        return (pltpu.make_async_copy(nw1.at[0, :, cols], w1f.at[slot], w_sem.at[0, slot]),
-                pltpu.make_async_copy(nw2.at[0, cols, :], w2f.at[slot], w_sem.at[1, slot]))
-
+    n_chunk = w1.shape[0]
     barrier = pltpu.get_barrier_semaphore()
 
     @pl.when(s == 1)
     def _():
-        for first in (0, 1):
-            for copy in loads(first):
-                copy.start()
         pl.semaphore_signal(barrier, inc=1, device_id=peer_y, device_id_type=MESH)
         pl.semaphore_signal(barrier, inc=1, device_id=peer_c, device_id_type=MESH)
 
@@ -467,17 +462,8 @@
             @pl.loop(0, n_chunk)
             def _(j):
                 if k == 0:
-                    slot = lax.rem(j, 2)
-                    copies = loads(j)
-                    copies[0].wait()
-                    w1[j] = w1f[slot].astype(BF16)
-                    copies[1].wait()
-                    w2[j] = w2f[slot].astype(BF16)
-
-                    @pl.when(j + 2 < n_chunk)
-                    def _():
-                        for copy in loads(j + 2):
-                            copy.start()
+                    w1[j] = jnp.concatenate([new1[2 * j].astype(BF16), new1[2 * j + 1].astype(BF16)], axis=1)
+                    w2[j] = new2[pl.ds(2 * j, 2)].reshape(w2.shape[1:]).astype(BF16)
                 chunk(k, j)
 
             send_part(k).start()
@@ -557,11 +543,13 @@
 
         up_out = jax.ShapeDtypeStruct(w_up.shape, F32)
         down_out = jax.ShapeDtypeStruct(w_down.shape, F32)
-        nw1, nm1, nv1, nw2, nm2, nv2 = pl.pallas_call(
+        nw1, nm1, nv1, nw2, nm2, nv2, new1, new2 = pl.pallas_call(
             update_kernel,
-            out_shape=(up_out, up_out, up_out, down_out, down_out, down_out),
+            out_shape=(up_out, up_out, up_out, down_out, down_out, down_out,
+                       pltpu.VMEM(mean_up.shape, F32), pltpu.VMEM(mean_down.shape, F32)),
             in_specs=[smem, smem, hbm, hbm, hbm, vmem, hbm, hbm, hbm, vmem],
-            out_specs=(hbm,) * 6,
+            out_specs=(hbm,) * 6 + (vmem, vmem),
+            input_output_aliases={5: 6, 9: 7},
             scratch_shapes=[pltpu.VMEM((3, SLOTS, d_model, width), F32), dma((3, SLOTS)), dma((3, SLOTS))],
             compiler_params=pltpu.CompilerParams(vmem_limit_bytes=VMEM_MAX - resident - SPARE),
             cost_estimate=pl.CostEstimate(flops=2000 * d_model * ff, bytes_accessed=48 * d_model * ff, transcendentals=4 * d_model * ff),
@@ -571,26 +559,24 @@
         f_width = 2 * width
         f_chunk = ff // f_width
         y_next = pl.pallas_call(
-            functools.partial(forward_kernel, f_chunk, f_width),
+            forward_kernel,
             out_shape=jax.ShapeDtypeStruct(x_next.shape, BF16),
-            in_specs=[vmem, vmem, hbm, hbm],
+            in_specs=[vmem, vmem, vmem, vmem],
             out_specs=vmem,
             scratch_shapes=[
                 pltpu.VMEM((f_chunk, d_model, f_width), BF16),
                 pltpu.VMEM((f_chunk, f_width, d_model), BF16),
-                pltpu.VMEM((2, d_model, f_width), F32),
-                pltpu.VMEM((2, f_width, d_model), F32),
                 pltpu.VMEM((n_micro, rows, d_model), BF16),
                 pltpu.VMEM((n_micro, half, d_model), BF16),
                 pltpu.VMEM((n_micro, half, d_model), BF16),
                 pltpu.VMEM((n_micro, rows, d_model), F32),
                 pltpu.VMEM((n_micro, half, d_model), F32),
-                dma((2, 2)), dma((n_micro,)), dma((n_micro,)), dma((2, n_micro)), dma((2, n_micro)), dma((n_micro,)), dma((n_micro,)),
+                dma((n_micro,)), dma((n_micro,)), dma((2, n_micro)), dma((2, n_micro)), dma((n_micro,)), dma((n_micro,)),
                 pltpu.SemaphoreType.REGULAR,
             ],
-            compiler_params=pltpu.CompilerParams(collective_id=1, has_side_effects=True, vmem_limit_bytes=VMEM_MAX),
+            compiler_params=pltpu.CompilerParams(collective_id=1, has_side_effects=True, vmem_limit_bytes=VMEM_MAX - resident - SPARE),
             name="forward_exchange",
-        )(from_core, from_diag, nw1, nw2)
+        )(from_core, from_diag, stay(new1), stay(new2))
         return nw1, nw2, nm1, nm2, nv1, nv2, y_next
 
     return jax.shard_map(device_step, mesh=mesh, in_specs=in_specs, out_specs=out_specs, check_vma=False)

time: 690 us -> 688 us (level)
  no operation moved by 1% of the time
where the time goes in v5:
time: 688 us
  Pallas kernels  678 us (99%)
    pallas_call x1, Pallas kernels, device_step(): pl.pallas_call(functools.partial(grad_kernel, n_chunk, width), out_shape=...  615 us
    pallas_call x1, Pallas kernels, device_step(): pl.pallas_call(update_kernel, out_shape=(up_out, up_out, up_out, down_out...  54.3 us
  transfers between devices with their start and end apart: 2, of which 0 were waited for; matrix products, arithmetic and copies ran while one was open for 0% of the time, Pallas kernels for 8%

profile of v5, /device:TPU:0, one launch (start us, length us, event | category | flops | bytes accessed | tf_op | source)
XLA Modules:
  0.0 687.6 jit_solution(12387609442805556403)
XLA Ops:
  1.9 615.1 %grad_exchange.1 = (f32[20,1280,128]{2,1,0:T(8,128)S(1)}, f32[20,128,1280]{2,1,0:T(8,128)S(1)}, f32[8,128]{1,0:T(8,128)}, bf16[3,128,1280]{2,1,0:T(8,128)(2,1)}) custom-call(f32[1280,2560]{1,0:T(8,128)} %bitcast.9, f32[2560,1280]{1,0:T(8,128)} %bitcast.10, f32[1280,2560]{1,0:T(8,128)} %bitcast.15, f32[2560,1280]{1,0:T(8,128)} %bitcast.16, ...), custom_call_target="tpu_custom_call" | custom-call | tf_op jit(solution)/shard_map/grad_exchange/pallas_call | solution.py:508
  617.0 1.4 collective-permute-start
  618.4 2.3 collective-permute-start.1
  620.6 54.3 %update.1 = (f32[1,1280,2560]{2,1,0:T(8,128)}, f32[1,1280,2560]{2,1,0:T(8,128)}, f32[1,1280,2560]{2,1,0:T(8,128)}, f32[1,2560,1280]{2,1,0:T(8,128)}, f32[1,2560,...) custom-call(f32[8,128]{1,0:T(8,128)} %get-tuple-element.19.clip, ...), custom_call_target="tpu_custom_call", output_to_operand_aliasing={{6}: (5, {}), {7}: (9, {})} | custom-call | flops 6553600000 | bytes 157286400 | tf_op jit(solution)/shard_map/update/pallas_call | solution.py:546
  675.0 0.0 collective-permute-done.from_core
  675.0 0.0 copy-start
  675.0 0.0 collective-permute-done.1.from_diag
  675.0 0.9 copy-done
  675.9 8.7 %forward_exchange.1 = bf16[3,256,1280]{2,1,0:T(8,128)(2,1)} custom-call(bf16[3,128,1280]{2,1,0:T(8,128)(2,1)} %copy-done, bf16[3,128,1280]{2,1,0:T(8,128)(2,1)} %collective-permute-done.1.from_diag, f32[20,1280,128]{2,1,0:T(8,128)S(1)} %get-tuple-element.29.new1, f32[20,128,1280]{2,1,0:T(8,128)S(1)} %get-tuple-element.30.new2), custom_call_target="tpu_custom_call" | custom-call | tf_op jit(solution)/shard_map/forward_exchange/pallas_call | solution.py:561
  684.6 2.9 copy.27
Async XLA Ops:
  617.0 58.0 %collective-permute-start = (bf16[3,128,1280]{2,1,0:T(8,128)(2,1)}, bf16[3,128,1280]{2,1,0:T(8,128)(2,1)S(1)}, u32[]{:S(2)}, u32[]{:S(2)}) collective-permute-start(bf16[3,128,1280]{2,1,0:T(8,128)(2,1)} %get-tuple-element.28), channel_id=1, source_target_pairs={{0,1},{4,5},{2,3},{6,7}} | collective-permute-start | bytes 2949128 | tf_op jit(solution)/shard_map/ppermute | solution.py:539
  618.4 56.6 %collective-permute-start.1 = (bf16[3,128,1280]{2,1,0:T(8,128)(2,1)}, bf16[3,128,1280]{2,1,0:T(8,128)(2,1)}, u32[]{:S(2)}, u32[]{:S(2)}) collective-permute-start(bf16[3,128,1280]{2,1,0:T(8,128)(2,1)} %get-tuple-element.28), channel_id=1, source_target_pairs={{0,5},{4,1},{2,7},{6,3}} | collective-permute-start | bytes 2949128 | tf_op jit(solution)/shard_map/ppermute | solution.py:538
  675.0 0.9 copy-start

commit v6 on v5

--- a/solution.py
+++ b/solution.py
@@ -72,9 +72,9 @@
 
 def grad_kernel(n_chunk, width, w1, w2, g1, g2, m1, v1, m2, v2, acts, dy, x, max_norm, rate,
                 gr1, gr2, clip, act_half,
-                gs1, gs2, w1b, w2b, gvec, part, got, x_buf, sq1, sq2, sq_out, sq_in,
+                gs1, gs2, w1b, w2b, part, got, x_buf, even_buf, odd_buf, sq1, sq2, sq_out, sq_in,
                 w_sem, g_sem, send1, send2, recv1, recv2, part_sem, gvec_sem, sq_send, sq_recv,
-                row_sem, f_sem, rs_send, rs_recv):
+                row_sem, act_sem, f_sem, rs_send, rs_recv):
     m, d, s = positions()
     peer_x = (m, 1 - d, s)
     peer_y = (1 - m, d, s)
@@ -92,8 +92,12 @@
                 pltpu.make_async_copy(g2.at[cols, :], gs2.at[j], g_sem.at[0, slot]),
                 pltpu.make_async_copy(g1.at[:, cols], gs1.at[j], g_sem.at[1, slot]))
 
+    acts_buf, gvec = x_buf.at[2:4], x_buf.at[4:6]
+    load_acts = pltpu.make_async_copy(acts, acts_buf, act_sem)
     load_dy = pltpu.make_async_copy(dy, gvec, row_sem)
     load_x = pltpu.make_async_copy(x, x_buf, row_sem)
+
+    load_acts.start()
 
     @pl.when(is_last)
     def _():
@@ -103,13 +107,9 @@
         for copy in loads(first):
             copy.start()
 
-    @pl.when(is_first)
-    def _():
-        load_x.start()
-
     entry_barrier((peer_x, peer_y, peer_c, peer_d))
 
-    hand_over = remote(x_buf.at[0], gvec, gvec_sem.at[0], gvec_sem.at[1], peer_c)
+    hand_over = remote(x_buf.at[:2], gvec, gvec_sem.at[0], gvec_sem.at[1], peer_c)
     swap_part = remote(part, got.at[:2], part_sem.at[0], part_sem.at[1], peer_y)
 
     @pl.when(is_last)
@@ -119,8 +119,9 @@
 
     @pl.when(is_first)
     def _():
-        load_x.wait()
         hand_over.wait_recv()
+
+    load_acts.wait()
 
     def send_two(j):
         return remote(gs2.at[j], gr2.at[j], send2.at[j], recv2.at[j], peer_x)
@@ -134,8 +135,8 @@
         copies = loads(j)
         copies[0].wait()
         up = w1b[slot].astype(BF16)
-        rows = acts[...]
-        grad = gvec[...]
+        rows = acts_buf[...].reshape(-1, d_model)
+        grad = gvec[...].reshape(-1, d_model)
         z = dot(rows, up)
         t, act = gelu_parts(z)
         hid = act.astype(BF16)
@@ -162,9 +163,12 @@
     def _():
         swap_part.start()
         swap_part.wait()
-        total = (part[...] + got[:2]).reshape(gvec.shape)
-        x_buf[0] = (gvec[...].astype(F32) + total).astype(BF16)
+        x_buf[:2] = (gvec[...].astype(F32) + (part[...] + got[:2])).astype(BF16)
         hand_over.start()
+
+    @pl.when(is_first)
+    def _():
+        load_x.start()
 
     n_up = n_chunk // 2
     n_pair = 2 * n_up
@@ -243,78 +247,139 @@
     def _():
         scale = clip[0, 0]
         step_rate = rate[0]
-        n_micro, n_row = x_buf.shape[:2]
-        group = 2 * n_micro
-        half = n_row // 2
+        group, half = x_buf.shape[:2]
+        n_micro = group // 2
+        third = group // 2
+        deep = d_model // 2
         wide = 2 * width
         n_block = d_model // wide
 
-        def new_weights(base, means):
-            parts = [adamw(scale, step_rate, gs1[base + h], gs1[base + 2 + h], gs1[base + 4 + h], means[h])[0].astype(BF16) for h in (0, 1)]
-            return jnp.concatenate(parts, axis=1)
+        def arrive(p):
+            base = lax.rem(p, 3) * 6
+            for i in range(6):
+                pltpu.make_async_copy(w1.at[:, :width], gs1.at[base + i], f_sem.at[base + i]).wait()
+
+        def new_weights(p, t, buf, means):
+            base = lax.rem(p, 3) * 6
+            some = pl.ds(pl.multiple_of(t * deep, deep), deep)
+            for h in (0, 1):
+                new = adamw(scale, step_rate, gs1[base + h, some], gs1[base + 2 + h, some], gs1[base + 4 + h, some], means[h])[0]
+                buf[some, h * width:(h + 1) * width] = new.astype(BF16)
+
+        def up_means(p, t):
+            some = pl.ds(pl.multiple_of(t * deep, deep), deep)
+            return [gr1[2 * p, some], gr1[2 * p + 1, some]]
+
+        def down_means(p, t, upper):
+            means = []
+            for h in (0, 1):
+                cols = pl.ds(pl.multiple_of((2 * ((p - n_up) // 2) + h) * width, width), width)
+                means.append(gr2[pl.ds(upper * n_up + t * (n_up // 2), n_up // 2), :, cols].reshape(deep, width))
+            return means
+
+        def up_product(p, t, buf):
+            rows = x_buf[pl.ds(t * third, third)].reshape(-1, d_model)
+            act = gelu_parts(dot(rows, buf[...]))[1].astype(BF16).astype(F32)
+            cols = pl.ds(pl.multiple_of(lax.rem(p, n_block) * wide, wide), wide)
+            gs2[pl.ds((p // n_block) * group + t * third, third), :, cols] = act.reshape(third, half, wide)
+
+        def down_product(p, t, buf, upper):
+            rows = gs2[pl.ds(upper * group + t * third, third)].reshape(-1, d_model).astype(BF16)
+            res = dot(rows, buf[...]).reshape(third, half, wide)
+            for g in range(third):
+                spot = slice(g * wide, (g + 1) * wide)
+                if upper:
+                    part[t, :, spot] += res[g]
+                else:
+                    part[t, :, spot] = res[g]
+
+        def give_block(c):
+            cols = pl.ds(pl.multiple_of(c * wide, wide), wide)
+            for k in range(n_micro):
+                even, odd = [part[g // third, :, g % third * wide:(g % third + 1) * wide] for g in (2 * k, 2 * k + 1)]
+                gs2[2 * group + k, :, cols] = jnp.where(m == 0, even, odd)
+                gs2[2 * group + n_micro + k, :, cols] = jnp.where(m == 0, odd, even)
+            block_copy(c).start()
 
         def block_copy(c):
             cols = pl.ds(pl.multiple_of(c * wide, wide), wide)
             return remote(gs2.at[2 * group + n_micro:2 * group + 2 * n_micro, :, cols], got.at[:, :, cols], rs_send.at[c], rs_recv.at[c], peer_y)
 
-        @pl.loop(0, n_pair)
-        def _(p):
-            base = lax.rem(p, 3) * 6
-            for i in range(6):
-                pltpu.make_async_copy(w1.at[:, :width], gs1.at[base + i], f_sem.at[base + i]).wait()
-
-            @pl.when(p < n_up)
+        def ahead(p):
+            if isinstance(p, int):
+                if p < n_pair:
+                    fetch(jnp.int32(p))
+                return
+
+            @pl.when(p < n_pair)
             def _():
-                new = new_weights(base, [gr1[2 * p], gr1[2 * p + 1]])
-                act = gelu_parts(dot(x_buf[...].reshape(-1, d_model), new))[1].astype(BF16).astype(F32)
-                cols = pl.ds(pl.multiple_of(lax.rem(p, n_block) * wide, wide), wide)
-                gs2[pl.ds((p // n_block) * group, group), :, cols] = act.reshape(group, half, wide)
-
-            @pl.when(p >= n_up)
-            def _():
-                c = (p - n_up) // 2
-                upper = lax.rem(p - n_up, 2)
-                means = []
-                for h in (0, 1):
-                    cols = pl.ds(pl.multiple_of((2 * c + h) * width, width), width)
-                    means.append(gr2[pl.ds(upper * n_up, n_up), :, cols].reshape(d_model, width))
-                new = new_weights(base, means)
-                cols = pl.ds(pl.multiple_of(c * wide, wide), wide)
-                spot = [(g // n_block, slice(None), slice(g % n_block * wide, g % n_block * wide + wide)) for g in range(group)]
-                for lo in range(0, group, n_micro):
-                    rows = gs2[pl.ds(upper * group + lo, n_micro)].reshape(-1, d_model).astype(BF16)
-                    res = dot(rows, new).reshape(n_micro, half, wide)
-
-                    @pl.when(upper == 0)
-                    def _():
-                        for g in range(n_micro):
-                            part[spot[lo + g]] = res[g]
-
-                    @pl.when(upper == 1)
-                    def _():
-                        for g in range(n_micro):
-                            part[spot[lo + g]] += res[g]
-
-                @pl.when(upper == 1)
-                def _():
-                    for k in range(n_micro):
-                        even, odd = part[spot[2 * k]], part[spot[2 * k + 1]]
-                        gs2[2 * group + k, :, cols] = jnp.where(m == 0, even, odd)
-                        gs2[2 * group + n_micro + k, :, cols] = jnp.where(m == 0, odd, even)
-                    block_copy(c).start()
-
-            @pl.when(p + 3 < n_pair)
-            def _():
-                fetch(p + 3)
+                fetch(p)
+
+        bufs = (even_buf, odd_buf)
+
+        def up_step(p, odd, down):
+            arrive(p + 1)
+
+            @pl.loop(0, 2)
+            def _(t):
+                up_product(p, t, bufs[odd])
+                new_weights(p + 1, t, bufs[1 - odd], down_means(p + 1, t, 0) if down else up_means(p + 1, t))
+
+            ahead(p + 4)
+
+        def down_step(p, odd):
+            arrive(p + 1)
+
+            @pl.loop(0, 2)
+            def _(t):
+                down_product(p, t, bufs[odd], odd)
+                new_weights(p + 1, t, bufs[1 - odd], down_means(p + 1, t, 1 - odd))
+
+            ahead(p + 4)
+            if odd:
+                give_block((p - n_up) // 2)
+
+        load_x.wait()
+        arrive(0)
+
+        @pl.loop(0, 2)
+        def _(t):
+            new_weights(0, t, even_buf, up_means(0, t))
+
+        ahead(3)
+
+        @pl.loop(0, n_up // 2 - 1)
+        def _(i):
+            up_step(2 * i, 0, False)
+            up_step(2 * i + 1, 1, False)
+
+        up_step(n_up - 2, 0, False)
+        up_step(n_up - 1, 1, True)
+
+        @pl.loop(n_up // 2, n_pair // 2 - 1)
+        def _(i):
+            down_step(2 * i, 0)
+            down_step(2 * i + 1, 1)
+
+        down_step(n_pair - 2, 0)
+
+        @pl.loop(0, 2)
+        def _(t):
+            down_product(n_pair - 1, t, odd_buf, 1)
+
+        give_block(n_block - 1)
 
         for c in range(n_block):
             block_copy(c).wait_recv()
             cols = slice(c * wide, (c + 1) * wide)
             for k in range(n_micro):
-                rows = x_buf[k, pl.ds(pl.multiple_of(m * half, half), half), cols].astype(F32)
-                act_half[k, :, cols] = (rows + (gs2[2 * group + k, :, cols] + got[k, :, cols])).astype(BF16)
+                rows = x_buf[2 * k + m, :, cols].astype(F32)
+                x_buf[k, :, cols] = (rows + (gs2[2 * group + k, :, cols] + got[k, :, cols])).astype(BF16)
+        store = pltpu.make_async_copy(x_buf.at[:n_micro], act_half, row_sem)
+        store.start()
         for c in range(n_block):
             block_copy(c).wait_send()
+        store.wait()
 
 
 def update_kernel(clip, rate, w1, m1, v1, gb1, w2, m2, v2, gb2, nw1, nm1, nv1, nw2, nm2, nv2, keep1, keep2, ring, in_sem, out_sem):
@@ -398,14 +463,14 @@
 
 
 def forward_kernel(from_core, from_diag, new1, new2, y,
-                   w1, w2, act, own_half, peer_half, part, part_in,
-                   p_send, p_recv, y_send, y_recv, f_send, f_recv, ready):
+                   w1, w2, hid, act, own_half, peer_half, part, part_in,
+                   p_send, p_recv, y_send, y_recv, g_send, g_recv, f_send, f_recv, ready):
     m, d, s = positions()
-    n_micro, half = own_half.shape[:2]
+    n_micro, half, d_model = own_half.shape
+    n_chunk, _, width = w1.shape
+    n_block = d_model // width
     peer_y = (1 - m, d, s)
     peer_c = (m, d, 1 - s)
-
-    n_chunk = w1.shape[0]
     barrier = pltpu.get_barrier_semaphore()
 
     @pl.when(s == 1)
@@ -422,14 +487,17 @@
     mine = pl.ds(pl.multiple_of(m * half, half), half)
     theirs = pl.ds(pl.multiple_of((1 - m) * half, half), half)
 
-    def send_part(k):
-        return remote(part.at[k, theirs, :], part_in.at[k], p_send.at[k], p_recv.at[k], peer_y)
-
-    def swap_y(k):
-        return remote(own_half.at[k], peer_half.at[k], y_send.at[0, k], y_recv.at[0, k], peer_y)
+    def span(c):
+        return pl.ds(pl.multiple_of(c * width, width), width)
+
+    def send_part(k, c):
+        return remote(part.at[k, theirs, span(c)], part_in.at[k, :, span(c)], p_send.at[k, c], p_recv.at[k, c], peer_y)
+
+    def swap_y(k, c):
+        return remote(own_half.at[k, :, span(c)], peer_half.at[k, :, span(c)], y_send.at[k, c], y_recv.at[k, c], peer_y)
 
     def give_own(k):
-        return remote(own_half.at[k], y.at[k, mine, :], y_send.at[1, k], y_recv.at[1, k], peer_c)
+        return remote(own_half.at[k], y.at[k, mine, :], g_send.at[k], g_recv.at[k], peer_c)
 
     def pass_on(k):
         return remote(peer_half.at[k], y.at[k, theirs, :], f_send.at[k], f_recv.at[k], peer_c)
@@ -445,41 +513,45 @@
         act[:, mine, :] = from_core[...]
         act[:, theirs, :] = from_diag[...]
 
-        def chunk(k, j):
-            hid = gelu_parts(dot(act[k], w1[j]))[1].astype(BF16)
-            part[k] += dot(hid, w2[j])
-
-        def finish(k):
-            send_part(k).wait_recv()
-            out = act[k, mine, :].astype(F32) + (part[k, mine, :] + part_in[k])
-            own_half[k] = out.astype(BF16)
-            swap_y(k).start()
-            y[k, mine, :] = own_half[k]
-
         for k in range(n_micro):
-            part[k] = jnp.zeros_like(part[k])
-
             @pl.loop(0, n_chunk)
             def _(j):
                 if k == 0:
                     w1[j] = jnp.concatenate([new1[2 * j].astype(BF16), new1[2 * j + 1].astype(BF16)], axis=1)
-                    w2[j] = new2[pl.ds(2 * j, 2)].reshape(w2.shape[1:]).astype(BF16)
-                chunk(k, j)
-
-            send_part(k).start()
-            if k > 0:
-                finish(k - 1)
-        finish(n_micro - 1)
+                hid[:, span(j)] = gelu_parts(dot(act[k], w1[j]))[1].astype(BF16)
+
+            @pl.loop(0, n_block)
+            def _(c):
+                if k == 0:
+                    w2[:, span(c)] = new2[:, :, span(c)].reshape(-1, width).astype(BF16)
+                part[k, :, span(c)] = dot(hid[...], w2[:, span(c)])
+                send_part(k, c).start()
+
+        for k in range(n_micro):
+            @pl.loop(0, n_block)
+            def _(c):
+                send_part(k, c).wait_recv()
+                out = act[k, mine, span(c)].astype(F32) + (part[k, mine, span(c)] + part_in[k, :, span(c)])
+                own_half[k, :, span(c)] = out.astype(BF16)
+                swap_y(k, c).start()
+
         pl.semaphore_wait(ready, 1)
         for k in range(n_micro):
             give_own(k).start()
+            y[k, mine, :] = own_half[k]
         for k in range(n_micro):
-            swap_y(k).wait_recv()
+            @pl.loop(0, n_block)
+            def _(c):
+                swap_y(k, c).wait_recv()
+
             pass_on(k).start()
             y[k, theirs, :] = peer_half[k]
         for k in range(n_micro):
-            send_part(k).wait_send()
-            swap_y(k).wait_send()
+            @pl.loop(0, n_block)
+            def _(c):
+                send_part(k, c).wait_send()
+                swap_y(k, c).wait_send()
+
             give_own(k).wait_send()
             pass_on(k).wait_send()
 
@@ -511,17 +583,18 @@
                        pltpu.VMEM((n_chunk, width, d_model), F32),
                        jax.ShapeDtypeStruct((8, 128), F32),
                        jax.ShapeDtypeStruct((n_micro, half, d_model), BF16)),
-            in_specs=[hbm] * 8 + [vmem, hbm, hbm, smem, smem],
-            out_specs=(vmem, vmem, vmem, vmem),
+            in_specs=[hbm] * 11 + [smem, smem],
+            out_specs=(vmem, vmem, vmem, hbm),
             scratch_shapes=[
                 pltpu.VMEM((n_chunk, d_model, width), F32),
                 pltpu.VMEM((n_chunk, width, d_model), F32),
                 pltpu.VMEM((2, d_model, width), F32),
                 pltpu.VMEM((2, width, d_model), F32),
-                pltpu.VMEM((rows, d_model), BF16),
                 pltpu.VMEM((2, half, d_model), F32),
                 pltpu.VMEM((n_micro, half, d_model), F32),
-                pltpu.VMEM((n_micro, rows, d_model), BF16),
+                pltpu.VMEM((2 * n_micro, half, d_model), BF16),
+                pltpu.VMEM((d_model, 2 * width), BF16),
+                pltpu.VMEM((d_model, 2 * width), BF16),
                 pltpu.VMEM((8, width), F32),
                 pltpu.VMEM((8, d_model), F32),
                 pltpu.VMEM((8, 128), F32),
@@ -529,11 +602,11 @@
                 dma((2, 2)), dma((2, 2)),
                 dma((n_chunk,)), dma((n_chunk,)), dma((n_chunk,)), dma((n_chunk,)),
                 dma((2,)), dma((2,)), dma((3,)), dma((4,)),
-                dma(()), dma((18,)), dma((n_block,)), dma((n_block,)),
+                dma(()), dma(()), dma((18,)), dma((n_block,)), dma((n_block,)),
             ],
             compiler_params=pltpu.CompilerParams(collective_id=0, has_side_effects=True, vmem_limit_bytes=VMEM_MAX - resident - SPARE),
             name="grad_exchange",
-        )(w_up[0], w_down[0], g_up[0, 0], g_down[0, 0], m_up[0], v_up[0], m_down[0], v_down[0], acts_last[0], grad_out, x_next, max_norm, learn_rate)
+        )(w_up[0], w_down[0], g_up[0, 0], g_down[0, 0], m_up[0], v_up[0], m_down[0], v_down[0], acts_last.reshape(2, half, d_model), grad_out.reshape(2, half, d_model), x_next.reshape(2 * n_micro, half, d_model), max_norm, learn_rate)
 
         from_diag = lax.ppermute(act_half, ('model', 'stage'), [(0, 3), (2, 1)])
         from_core = lax.ppermute(act_half, ('model', 'stage'), [(0, 1), (2, 3)])
@@ -565,13 +638,15 @@
             out_specs=vmem,
             scratch_shapes=[
                 pltpu.VMEM((f_chunk, d_model, f_width), BF16),
-                pltpu.VMEM((f_chunk, f_width, d_model), BF16),
+                pltpu.VMEM((ff, d_model), BF16),
+                pltpu.VMEM((rows, ff), BF16),
                 pltpu.VMEM((n_micro, rows, d_model), BF16),
                 pltpu.VMEM((n_micro, half, d_model), BF16),
                 pltpu.VMEM((n_micro, half, d_model), BF16),
                 pltpu.VMEM((n_micro, rows, d_model), F32),
                 pltpu.VMEM((n_micro, half, d_model), F32),
-                dma((n_micro,)), dma((n_micro,)), dma((2, n_micro)), dma((2, n_micro)), dma((n_micro,)), dma((n_micro,)),
+                dma((n_micro, n_block)), dma((n_micro, n_block)), dma((n_micro, n_block)), dma((n_micro, n_block)),
+                dma((n_micro,)), dma((n_micro,)), dma((n_micro,)), dma((n_micro,)),
                 pltpu.SemaphoreType.REGULAR,
             ],
             compiler_params=pltpu.CompilerParams(collective_id=1, has_side_effects=True, vmem_limit_bytes=VMEM_MAX - resident - SPARE),

time: 688 us -> 694 us (level)
    pallas_call x1, Pallas kernels: 615 us -> 622 us  [device_step(): pl.pallas_call(functools.partial(grad_kernel, n_chunk, width), out_shape=...]
where the time goes in v6:
time: 694 us; the launch traced here: 693 us
  Pallas kernels  684 us (99%)
    pallas_call x1, Pallas kernels, device_step(): pl.pallas_call(functools.partial(grad_kernel, n_chunk, width), out_shape=...  622 us
    pallas_call x1, Pallas kernels, device_step(): pl.pallas_call(update_kernel, out_shape=(up_out, up_out, up_out, down_out...  54.3 us
  transfers between devices with their start and end apart: 2, of which 0 were waited for; matrix products, arithmetic and copies ran while one was open for 0% of the time, Pallas kernels for 8%

profile of v6, /device:TPU:0, one launch (start us, length us, event | category | flops | bytes accessed | tf_op | source)
XLA Modules:
  0.0 693.3 jit_solution(2628252796033771233)
XLA Ops:
  1.9 622.1 %grad_exchange.1 = (f32[20,1280,128]{2,1,0:T(8,128)S(1)}, f32[20,128,1280]{2,1,0:T(8,128)S(1)}, f32[8,128]{1,0:T(8,128)}, bf16[3,128,1280]{2,1,0:T(8,128)(2,1)}) custom-call(f32[1280,2560]{1,0:T(8,128)} %bitcast.11, f32[2560,1280]{1,0:T(8,128)} %bitcast.12, f32[1280,2560]{1,0:T(8,128)} %bitcast.17, f32[2560,1280]{1,0:T(8,128)} %bitcast.18, ...), custom_call_target="tpu_custom_call" | custom-call | tf_op jit(solution)/shard_map/grad_exchange/pallas_call | solution.py:580
  624.0 1.4 collective-permute-start
  625.4 2.3 collective-permute-start.1
  627.6 54.3 %update.1 = (f32[1,1280,2560]{2,1,0:T(8,128)}, f32[1,1280,2560]{2,1,0:T(8,128)}, f32[1,1280,2560]{2,1,0:T(8,128)}, f32[1,2560,1280]{2,1,0:T(8,128)}, f32[1,2560,...) custom-call(f32[8,128]{1,0:T(8,128)} %get-tuple-element.19.clip, ...), custom_call_target="tpu_custom_call", output_to_operand_aliasing={{6}: (5, {}), {7}: (9, {})} | custom-call | flops 6553600000 | bytes 157286400 | tf_op jit(solution)/shard_map/update/pallas_call | solution.py:619
  682.0 0.0 collective-permute-done.from_core
  682.0 0.0 copy-start
  682.0 0.0 collective-permute-done.1.from_diag
  682.0 0.9 copy-done
  682.9 7.4 %forward_exchange.1 = bf16[3,256,1280]{2,1,0:T(8,128)(2,1)} custom-call(bf16[3,128,1280]{2,1,0:T(8,128)(2,1)} %copy-done, bf16[3,128,1280]{2,1,0:T(8,128)(2,1)} %collective-permute-done.1.from_diag, f32[20,1280,128]{2,1,0:T(8,128)S(1)} %get-tuple-element.29.new1, f32[20,128,1280]{2,1,0:T(8,128)S(1)} %get-tuple-element.30.new2), custom_call_target="tpu_custom_call" | custom-call | tf_op jit(solution)/shard_map/forward_exchange/pallas_call | solution.py:634
  690.4 2.9 copy.27
Async XLA Ops:
  624.0 58.0 %collective-permute-start = (bf16[3,128,1280]{2,1,0:T(8,128)(2,1)}, bf16[3,128,1280]{2,1,0:T(8,128)(2,1)S(1)}, u32[]{:S(2)}, u32[]{:S(2)}) collective-permute-start(bf16[3,128,1280]{2,1,0:T(8,128)(2,1)} %get-tuple-element.28), channel_id=1, source_target_pairs={{0,1},{4,5},{2,3},{6,7}} | collective-permute-start | bytes 2949128 | tf_op jit(solution)/shard_map/ppermute | solution.py:612
  625.4 56.6 %collective-permute-start.1 = (bf16[3,128,1280]{2,1,0:T(8,128)(2,1)}, bf16[3,128,1280]{2,1,0:T(8,128)(2,1)}, u32[]{:S(2)}, u32[]{:S(2)}) collective-permute-start(bf16[3,128,1280]{2,1,0:T(8,128)(2,1)} %get-tuple-element.28), channel_id=1, source_target_pairs={{0,5},{4,1},{2,7},{6,3}} | collective-permute-start | bytes 2949128 | tf_op jit(solution)/shard_map/ppermute | solution.py:611
  682.0 0.9 copy-start

commit v7 on v6

--- a/solution.py
+++ b/solution.py
@@ -28,7 +28,7 @@
 CHUNK = 128
 SLOTS = 8
 AHEAD = 5
-SPARE = 1 << 20
+SPARE = 5 << 19
 F32 = jnp.float32
 BF16 = jnp.bfloat16
 
@@ -72,7 +72,7 @@
 
 def grad_kernel(n_chunk, width, w1, w2, g1, g2, m1, v1, m2, v2, acts, dy, x, max_norm, rate,
                 gr1, gr2, clip, act_half,
-                gs1, gs2, w1b, w2b, part, got, x_buf, even_buf, odd_buf, sq1, sq2, sq_out, sq_in,
+                gs1, gs2, w1b, w2b, part, got, x_buf, sq1, sq2, sq_out, sq_in,
                 w_sem, g_sem, send1, send2, recv1, recv2, part_sem, gvec_sem, sq_send, sq_recv,
                 row_sem, act_sem, f_sem, rs_send, rs_recv):
     m, d, s = positions()
@@ -250,7 +250,6 @@
         group, half = x_buf.shape[:2]
         n_micro = group // 2
         third = group // 2
-        deep = d_model // 2
         wide = 2 * width
         n_block = d_model // wide
 
@@ -259,39 +258,32 @@
             for i in range(6):
                 pltpu.make_async_copy(w1.at[:, :width], gs1.at[base + i], f_sem.at[base + i]).wait()
 
-        def new_weights(p, t, buf, means):
+        def new_weights(p, means):
             base = lax.rem(p, 3) * 6
-            some = pl.ds(pl.multiple_of(t * deep, deep), deep)
-            for h in (0, 1):
-                new = adamw(scale, step_rate, gs1[base + h, some], gs1[base + 2 + h, some], gs1[base + 4 + h, some], means[h])[0]
-                buf[some, h * width:(h + 1) * width] = new.astype(BF16)
-
-        def up_means(p, t):
-            some = pl.ds(pl.multiple_of(t * deep, deep), deep)
-            return [gr1[2 * p, some], gr1[2 * p + 1, some]]
-
-        def down_means(p, t, upper):
+            parts = [adamw(scale, step_rate, gs1[base + h], gs1[base + 2 + h], gs1[base + 4 + h], means[h])[0].astype(BF16) for h in (0, 1)]
+            return jnp.concatenate(parts, axis=1)
+
+        def up_pair(p):
+            new = new_weights(p, [gr1[2 * p], gr1[2 * p + 1]])
+            act = gelu_parts(dot(x_buf[...].reshape(-1, d_model), new))[1].astype(BF16).astype(F32)
+            cols = pl.ds(pl.multiple_of(lax.rem(p, n_block) * wide, wide), wide)
+            gs2[pl.ds((p // n_block) * group, group), :, cols] = act.reshape(group, half, wide)
+
+        def down_pair(p, upper):
             means = []
             for h in (0, 1):
                 cols = pl.ds(pl.multiple_of((2 * ((p - n_up) // 2) + h) * width, width), width)
-                means.append(gr2[pl.ds(upper * n_up + t * (n_up // 2), n_up // 2), :, cols].reshape(deep, width))
-            return means
-
-        def up_product(p, t, buf):
-            rows = x_buf[pl.ds(t * third, third)].reshape(-1, d_model)
-            act = gelu_parts(dot(rows, buf[...]))[1].astype(BF16).astype(F32)
-            cols = pl.ds(pl.multiple_of(lax.rem(p, n_block) * wide, wide), wide)
-            gs2[pl.ds((p // n_block) * group + t * third, third), :, cols] = act.reshape(third, half, wide)
-
-        def down_product(p, t, buf, upper):
-            rows = gs2[pl.ds(upper * group + t * third, third)].reshape(-1, d_model).astype(BF16)
-            res = dot(rows, buf[...]).reshape(third, half, wide)
-            for g in range(third):
-                spot = slice(g * wide, (g + 1) * wide)
-                if upper:
-                    part[t, :, spot] += res[g]
-                else:
-                    part[t, :, spot] = res[g]
+                means.append(gr2[upper * n_up:(upper + 1) * n_up, :, cols].reshape(d_model, width))
+            new = new_weights(p, means)
+            for lo in range(0, group, third):
+                rows = gs2[upper * group + lo:upper * group + lo + third].reshape(-1, d_model).astype(BF16)
+                res = dot(rows, new).reshape(third, half, wide)
+                for g in range(third):
+                    spot = slice(g * wide, (g + 1) * wide)
+                    if upper:
+                        part[lo // third, :, spot] += res[g]
+                    else:
+                        part[lo // third, :, spot] = res[g]
 
         def give_block(c):
             cols = pl.ds(pl.multiple_of(c * wide, wide), wide)
@@ -306,68 +298,26 @@
             return remote(gs2.at[2 * group + n_micro:2 * group + 2 * n_micro, :, cols], got.at[:, :, cols], rs_send.at[c], rs_recv.at[c], peer_y)
 
         def ahead(p):
-            if isinstance(p, int):
-                if p < n_pair:
-                    fetch(jnp.int32(p))
-                return
-
             @pl.when(p < n_pair)
             def _():
                 fetch(p)
 
-        bufs = (even_buf, odd_buf)
-
-        def up_step(p, odd, down):
-            arrive(p + 1)
-
-            @pl.loop(0, 2)
-            def _(t):
-                up_product(p, t, bufs[odd])
-                new_weights(p + 1, t, bufs[1 - odd], down_means(p + 1, t, 0) if down else up_means(p + 1, t))
-
-            ahead(p + 4)
-
-        def down_step(p, odd):
-            arrive(p + 1)
-
-            @pl.loop(0, 2)
-            def _(t):
-                down_product(p, t, bufs[odd], odd)
-                new_weights(p + 1, t, bufs[1 - odd], down_means(p + 1, t, 1 - odd))
-
-            ahead(p + 4)
-            if odd:
-                give_block((p - n_up) // 2)
-
         load_x.wait()
-        arrive(0)
-
-        @pl.loop(0, 2)
-        def _(t):
-            new_weights(0, t, even_buf, up_means(0, t))
-
-        ahead(3)
-
-        @pl.loop(0, n_up // 2 - 1)
-        def _(i):
-            up_step(2 * i, 0, False)
-            up_step(2 * i + 1, 1, False)
-
-        up_step(n_up - 2, 0, False)
-        up_step(n_up - 1, 1, True)
-
-        @pl.loop(n_up // 2, n_pair // 2 - 1)
-        def _(i):
-            down_step(2 * i, 0)
-            down_step(2 * i + 1, 1)
-
-        down_step(n_pair - 2, 0)
-
-        @pl.loop(0, 2)
-        def _(t):
-            down_product(n_pair - 1, t, odd_buf, 1)
-
-        give_block(n_block - 1)
+
+        @pl.loop(0, n_up)
+        def _(p):
+            arrive(p)
+            up_pair(p)
+            ahead(p + 3)
+
+        @pl.loop(0, n_block)
+        def _(c):
+            for upper in (0, 1):
+                p = n_up + 2 * c + upper
+                arrive(p)
+                down_pair(p, upper)
+                ahead(p + 3)
+            give_block(c)
 
         for c in range(n_block):
             block_copy(c).wait_recv()
@@ -593,8 +543,6 @@
                 pltpu.VMEM((2, half, d_model), F32),
                 pltpu.VMEM((n_micro, half, d_model), F32),
                 pltpu.VMEM((2 * n_micro, half, d_model), BF16),
-                pltpu.VMEM((d_model, 2 * width), BF16),
-                pltpu.VMEM((d_model, 2 * width), BF16),
                 pltpu.VMEM((8, width), F32),
                 pltpu.VMEM((8, d_model), F32),
                 pltpu.VMEM((8, 128), F32),
@@ -633,7 +581,7 @@
         f_chunk = ff // f_width
         y_next = pl.pallas_call(
             forward_kernel,
-            out_shape=jax.ShapeDtypeStruct(x_next.shape, BF16),
+            out_shape=pltpu.VMEM(x_next.shape, BF16),
             in_specs=[vmem, vmem, vmem, vmem],
             out_specs=vmem,
             scratch_shapes=[

time: 694 us -> 682 us (0.983)
  Pallas kernels: 684 us -> 674 us
    pallas_call x1, Pallas kernels: 622 us -> 614 us  [device_step(): pl.pallas_call(functools.partial(grad_kernel, n_chunk, width), out_shape=...]
where the time goes in v7:
time: 682 us; the launch traced here: 681 us
  Pallas kernels  674 us (99%)
    pallas_call x1, Pallas kernels, device_step(): pl.pallas_call(functools.partial(grad_kernel, n_chunk, width), out_shape=...  614 us
    pallas_call x1, Pallas kernels, device_step(): pl.pallas_call(update_kernel, out_shape=(up_out, up_out, up_out, down_out...  54.4 us
  transfers between devices with their start and end apart: 2, of which 0 were waited for; matrix products, arithmetic and copies ran while one was open for 0% of the time, Pallas kernels for 8%

profile of v7, /device:TPU:0, one launch (start us, length us, event | category | flops | bytes accessed | tf_op | source)
XLA Modules:
  0.0 681.4 jit_solution(8910297997503619908)
XLA Ops:
  1.9 613.7 %grad_exchange.1 = (f32[20,1280,128]{2,1,0:T(8,128)S(1)}, f32[20,128,1280]{2,1,0:T(8,128)S(1)}, f32[8,128]{1,0:T(8,128)}, bf16[3,128,1280]{2,1,0:T(8,128)(2,1)}) custom-call(f32[1280,2560]{1,0:T(8,128)} %bitcast.11, f32[2560,1280]{1,0:T(8,128)} %bitcast.12, f32[1280,2560]{1,0:T(8,128)} %bitcast.17, f32[2560,1280]{1,0:T(8,128)} %bitcast.18, ...), custom_call_target="tpu_custom_call" | custom-call | tf_op jit(solution)/shard_map/grad_exchange/pallas_call | solution.py:530
  615.6 1.4 collective-permute-start
  617.0 1.4 collective-permute-start.1
  618.4 54.4 %update.1 = (f32[1,1280,2560]{2,1,0:T(8,128)}, f32[1,1280,2560]{2,1,0:T(8,128)}, f32[1,1280,2560]{2,1,0:T(8,128)}, f32[1,2560,1280]{2,1,0:T(8,128)}, f32[1,2560,...) custom-call(f32[8,128]{1,0:T(8,128)} %get-tuple-element.19.clip, ...), custom_call_target="tpu_custom_call", output_to_operand_aliasing={{6}: (5, {}), {7}: (9, {})} | custom-call | flops 6553600000 | bytes 157286400 | tf_op jit(solution)/shard_map/update/pallas_call | solution.py:567
  672.7 0.0 collective-permute-done.from_core
  672.7 0.0 copy-start
  672.7 0.0 collective-permute-done.1.from_diag
  672.8 0.0 copy-start.1
  672.8 0.9 copy-done
  673.7 0.3 copy-done.1
  674.0 6.1 forward_exchange.1
  680.2 1.3 copy.25
Async XLA Ops:
  615.6 57.1 %collective-permute-start = (bf16[3,128,1280]{2,1,0:T(8,128)(2,1)}, bf16[3,128,1280]{2,1,0:T(8,128)(2,1)S(1)}, u32[]{:S(2)}, u32[]{:S(2)}) collective-permute-start(bf16[3,128,1280]{2,1,0:T(8,128)(2,1)} %get-tuple-element.28), channel_id=1, source_target_pairs={{0,1},{4,5},{2,3},{6,7}} | collective-permute-start | bytes 2949128 | tf_op jit(solution)/shard_map/ppermute | solution.py:560
  617.0 55.7 %collective-permute-start.1 = (bf16[3,128,1280]{2,1,0:T(8,128)(2,1)}, bf16[3,128,1280]{2,1,0:T(8,128)(2,1)S(1)}, u32[]{:S(2)}, u32[]{:S(2)}) collective-permute-start(bf16[3,128,1280]{2,1,0:T(8,128)(2,1)} %get-tuple-element.28), channel_id=1, source_target_pairs={{0,5},{4,1},{2,7},{6,3}} | collective-permute-start | bytes 2949128 | tf_op jit(solution)/shard_map/ppermute | solution.py:559
  672.7 0.9 copy-start
  672.8 1.3 copy-start.1

commit v8 on v7

--- a/solution.py
+++ b/solution.py
@@ -71,8 +71,8 @@
 
 
 def grad_kernel(n_chunk, width, w1, w2, g1, g2, m1, v1, m2, v2, acts, dy, x, max_norm, rate,
-                gr1, gr2, clip, act_half,
-                gs1, gs2, w1b, w2b, part, got, x_buf, sq1, sq2, sq_out, sq_in,
+                gr1, gr2, gs1, clip, act_half,
+                gs2, w1b, w2b, part, got, x_buf, sq1, sq2, sq_out, sq_in,
                 w_sem, g_sem, send1, send2, recv1, recv2, part_sem, gvec_sem, sq_send, sq_recv,
                 row_sem, act_sem, f_sem, rs_send, rs_recv):
     m, d, s = positions()
@@ -103,11 +103,11 @@
     def _():
         load_dy.start()
 
-    for first in (0, 1):
-        for copy in loads(first):
-            copy.start()
-
+    for copy in loads(0):
+        copy.start()
     entry_barrier((peer_x, peer_y, peer_c, peer_d))
+    for copy in loads(1):
+        copy.start()
 
     hand_over = remote(x_buf.at[:2], gvec, gvec_sem.at[0], gvec_sem.at[1], peer_c)
     swap_part = remote(part, got.at[:2], part_sem.at[0], part_sem.at[1], peer_y)
@@ -191,13 +191,16 @@
                     cols = pl.ds(pl.multiple_of((2 * ((p - n_up) // 2) + h) * width, width), width)
                     pltpu.make_async_copy(ref.at[rows, cols], gs1.at[base + 2 * q + h], f_sem.at[base + 2 * q + h]).start()
 
+    def arrive(p):
+        base = lax.rem(p, 3) * 6
+        for i in range(6):
+            pltpu.make_async_copy(w1.at[:, :width], gs1.at[base + i], f_sem.at[base + i]).wait()
+
     def free_and_fetch(lo, hi, p):
         for i in range(lo, hi):
             send_one(i).wait_send()
 
-        @pl.when(is_first)
-        def _():
-            fetch(jnp.int32(p))
+        fetch(p)
 
     sq1[...] = jnp.zeros_like(sq1)
     sq2[...] = jnp.zeros_like(sq2)
@@ -215,11 +218,11 @@
 
         @pl.when(j == 10)
         def _():
-            free_and_fetch(0, 6, 0)
+            free_and_fetch(0, 6, 18 * s)
 
         @pl.when(j == 15)
         def _():
-            free_and_fetch(6, 12, 1)
+            free_and_fetch(6, 12, 1 + 18 * s)
 
     sq_out[...] = jnp.full(sq_out.shape, jnp.sum(sq1[...]) + jnp.sum(sq2[...]), F32)
     mine = 2 * m + s
@@ -227,7 +230,7 @@
     shares = [remote(sq_out, sq_in.at[mine], sq_send.at[k], sq_recv.at[mine], peer) for k, (peer, _) in enumerate(others)]
     for copy in shares:
         copy.start()
-    free_and_fetch(12, n_chunk, 2)
+    free_and_fetch(12, n_chunk, 2 + 15 * s)
     sq_in[mine] = sq_out[...]
     for peer, index in others:
         remote(sq_out, sq_in.at[index], sq_send.at[0], sq_recv.at[index], peer).wait_recv()
@@ -242,6 +245,8 @@
     @pl.when(is_last)
     def _():
         hand_over.wait_send()
+        for p in (18, 19, 17):
+            arrive(jnp.int32(p))
 
     @pl.when(is_first)
     def _():
@@ -252,11 +257,6 @@
         third = group // 2
         wide = 2 * width
         n_block = d_model // wide
-
-        def arrive(p):
-            base = lax.rem(p, 3) * 6
-            for i in range(6):
-                pltpu.make_async_copy(w1.at[:, :width], gs1.at[base + i], f_sem.at[base + i]).wait()
 
         def new_weights(p, means):
             base = lax.rem(p, 3) * 6
@@ -332,15 +332,17 @@
         store.wait()
 
 
-def update_kernel(clip, rate, w1, m1, v1, gb1, w2, m2, v2, gb2, nw1, nm1, nv1, nw2, nm2, nv2, keep1, keep2, ring, in_sem, out_sem):
+def update_kernel(clip, rate, w1, m1, v1, gb1, w2, m2, v2, gb2, held, nw1, nm1, nv1, nw2, nm2, nv2, keep1, keep2, held_out, ring, in_sem, out_sem, held_sem):
     n_up, deep, wide = gb1.shape
     n_slot = ring.shape[1]
-    last = 2 * n_up
+    near = [(place, h) for place in range(3) for h in (0, 1)]
+    last = 2 * n_up - len(near)
     block = deep // gb2.shape[1]
     scale = clip[0, 0]
     step_rate = rate[0]
 
     def place(i):
+        i = i + i // (last - 1)
         col = pl.multiple_of(((i - n_up) // 2) * wide, wide)
         row = pl.multiple_of(lax.rem(i - n_up, 2) * deep, deep)
         return pl.ds(row, deep), pl.ds(col, wide)
@@ -350,8 +352,8 @@
         sem = in_sem if fetch else out_sem
 
         def go(k, far):
-            near = ring.at[k, slot]
-            pair = (far, near) if fetch else (near, far)
+            here = ring.at[k, slot]
+            pair = (far, here) if fetch else (here, far)
             pltpu.make_async_copy(*pair, sem.at[k, slot]).start()
 
         @pl.when(i < n_up)
@@ -369,9 +371,9 @@
     def finish(i, fetch):
         slot = lax.rem(i, n_slot)
         for k, ref in enumerate((w2, m2, v2) if fetch else (nw2, nm2, nv2)):
-            far, near = ref.at[0, :deep, :wide], ring.at[k, slot]
+            far, here = ref.at[0, :deep, :wide], ring.at[k, slot]
             sem = (in_sem if fetch else out_sem).at[k, slot]
-            (pltpu.make_async_copy(far, near, sem) if fetch else pltpu.make_async_copy(near, far, sem)).wait()
+            (pltpu.make_async_copy(far, here, sem) if fetch else pltpu.make_async_copy(here, far, sem)).wait()
 
     for i in range(AHEAD):
         start(jnp.int32(i), True)
@@ -383,6 +385,24 @@
         ring[2, slot] = sec
         return new
 
+    def held_copies(place, h):
+        col, upper = {2: (6, 1), 0: (8, 0), 1: (8, 1)}[place]
+        rows, cols = slice(upper * deep, (upper + 1) * deep), slice((col + h) * wide, (col + h + 1) * wide)
+        return upper, cols, [pltpu.make_async_copy(held_out.at[6 * place + 2 * k + h], ref.at[0, rows, cols], held_sem.at[6 * place + 2 * k + h])
+                             for k, ref in enumerate((nw2, nm2, nv2))]
+
+    for spot, h in near:
+        upper, cols, copies = held_copies(spot, h)
+        rows = slice(upper * block, (upper + 1) * block)
+        base = 6 * spot + h
+        new, mom, sec = adamw(scale, step_rate, held[base], held[base + 2], held[base + 4], gb2[rows, :, cols].reshape(deep, wide))
+        held_out[base] = new
+        held_out[base + 2] = mom
+        held_out[base + 4] = sec
+        keep2[rows, :, cols] = new.reshape(block, -1, wide)
+        for copy in copies:
+            copy.start()
+
     @pl.loop(0, last)
     def _(i):
         slot = lax.rem(i, n_slot)
@@ -395,7 +415,7 @@
         @pl.when(i >= n_up)
         def _():
             cols = place(i)[1]
-            rows = pl.ds(lax.rem(i - n_up, 2) * block, block)
+            rows = pl.ds(lax.rem(i + i // (last - 1) - n_up, 2) * block, block)
             new = step(slot, gb2[rows, :, cols].reshape(deep, wide))
             keep2[rows, :, cols] = new.reshape(block, -1, wide)
 
@@ -410,21 +430,30 @@
 
     for i in range(last - n_slot, last):
         finish(jnp.int32(i), False)
+    for spot, h in near:
+        for copy in held_copies(spot, h)[2]:
+            copy.wait()
 
 
 def forward_kernel(from_core, from_diag, new1, new2, y,
-                   w1, w2, hid, act, own_half, peer_half, part, part_in,
-                   p_send, p_recv, y_send, y_recv, g_send, g_recv, f_send, f_recv, ready):
+                   hid, act, own_half, peer_half, part, part_in,
+                   in_sem, p_send, p_recv, y_send, y_recv, g_send, g_recv, f_send, f_recv, ready):
     m, d, s = positions()
     n_micro, half, d_model = own_half.shape
-    n_chunk, _, width = w1.shape
-    n_block = d_model // width
+    width = 2 * new1.shape[2]
+    n_chunk, n_block = new1.shape[0] // 2, d_model // width
     peer_y = (1 - m, d, s)
     peer_c = (m, d, 1 - s)
     barrier = pltpu.get_barrier_semaphore()
+    mine = pl.ds(pl.multiple_of(m * half, half), half)
+    theirs = pl.ds(pl.multiple_of((1 - m) * half, half), half)
+    rows_in = (pltpu.make_async_copy(from_core, act.at[:, mine, :], in_sem.at[0]),
+               pltpu.make_async_copy(from_diag, act.at[:, theirs, :], in_sem.at[1]))
 
     @pl.when(s == 1)
     def _():
+        for copy in rows_in:
+            copy.start()
         pl.semaphore_signal(barrier, inc=1, device_id=peer_y, device_id_type=MESH)
         pl.semaphore_signal(barrier, inc=1, device_id=peer_c, device_id_type=MESH)
 
@@ -433,9 +462,6 @@
     @pl.when(s == 0)
     def _():
         pl.semaphore_signal(ready, inc=1, device_id=peer_c, device_id_type=MESH)
-
-    mine = pl.ds(pl.multiple_of(m * half, half), half)
-    theirs = pl.ds(pl.multiple_of((1 - m) * half, half), half)
 
     def span(c):
         return pl.ds(pl.multiple_of(c * width, width), width)
@@ -460,21 +486,19 @@
 
     @pl.when(s == 1)
     def _():
-        act[:, mine, :] = from_core[...]
-        act[:, theirs, :] = from_diag[...]
+        for copy in rows_in:
+            copy.wait()
 
         for k in range(n_micro):
             @pl.loop(0, n_chunk)
             def _(j):
-                if k == 0:
-                    w1[j] = jnp.concatenate([new1[2 * j].astype(BF16), new1[2 * j + 1].astype(BF16)], axis=1)
-                hid[:, span(j)] = gelu_parts(dot(act[k], w1[j]))[1].astype(BF16)
+                up = jnp.concatenate([new1[2 * j].astype(BF16), new1[2 * j + 1].astype(BF16)], axis=1)
+                hid[:, span(j)] = gelu_parts(dot(act[k], up))[1].astype(BF16)
 
             @pl.loop(0, n_block)
             def _(c):
-                if k == 0:
-                    w2[:, span(c)] = new2[:, :, span(c)].reshape(-1, width).astype(BF16)
-                part[k, :, span(c)] = dot(hid[...], w2[:, span(c)])
+                down = new2[:, :, span(c)].reshape(-1, width).astype(BF16)
+                part[k, :, span(c)] = dot(hid[...], down)
                 send_part(k, c).start()
 
         for k in range(n_micro):
@@ -524,19 +548,19 @@
         vmem = pl.BlockSpec(memory_space=pltpu.VMEM)
         smem = pl.BlockSpec(memory_space=pltpu.SMEM)
         dma = pltpu.SemaphoreType.DMA
-        resident = 4 * 2 * d_model * ff
+        resident = 4 * 3 * d_model * ff
         n_block = d_model // (2 * width)
 
-        mean_up, mean_down, clip, act_half = pl.pallas_call(
+        mean_up, mean_down, held, clip, act_half = pl.pallas_call(
             functools.partial(grad_kernel, n_chunk, width),
             out_shape=(pltpu.VMEM((n_chunk, d_model, width), F32),
                        pltpu.VMEM((n_chunk, width, d_model), F32),
+                       pltpu.VMEM((n_chunk, d_model, width), F32),
                        jax.ShapeDtypeStruct((8, 128), F32),
                        jax.ShapeDtypeStruct((n_micro, half, d_model), BF16)),
             in_specs=[hbm] * 11 + [smem, smem],
-            out_specs=(vmem, vmem, vmem, hbm),
+            out_specs=(vmem, vmem, vmem, vmem, hbm),
             scratch_shapes=[
-                pltpu.VMEM((n_chunk, d_model, width), F32),
                 pltpu.VMEM((n_chunk, width, d_model), F32),
                 pltpu.VMEM((2, d_model, width), F32),
                 pltpu.VMEM((2, width, d_model), F32),
@@ -564,36 +588,32 @@
 
         up_out = jax.ShapeDtypeStruct(w_up.shape, F32)
         down_out = jax.ShapeDtypeStruct(w_down.shape, F32)
-        nw1, nm1, nv1, nw2, nm2, nv2, new1, new2 = pl.pallas_call(
+        nw1, nm1, nv1, nw2, nm2, nv2, new1, new2, _ = pl.pallas_call(
             update_kernel,
             out_shape=(up_out, up_out, up_out, down_out, down_out, down_out,
-                       pltpu.VMEM(mean_up.shape, F32), pltpu.VMEM(mean_down.shape, F32)),
-            in_specs=[smem, smem, hbm, hbm, hbm, vmem, hbm, hbm, hbm, vmem],
-            out_specs=(hbm,) * 6 + (vmem, vmem),
-            input_output_aliases={5: 6, 9: 7},
-            scratch_shapes=[pltpu.VMEM((3, SLOTS, d_model, width), F32), dma((3, SLOTS)), dma((3, SLOTS))],
+                       pltpu.VMEM(mean_up.shape, F32), pltpu.VMEM(mean_down.shape, F32), pltpu.VMEM(held.shape, F32)),
+            in_specs=[smem, smem, hbm, hbm, hbm, vmem, hbm, hbm, hbm, vmem, vmem],
+            out_specs=(hbm,) * 6 + (vmem, vmem, vmem),
+            input_output_aliases={5: 6, 9: 7, 10: 8},
+            scratch_shapes=[pltpu.VMEM((3, SLOTS, d_model, width), F32), dma((3, SLOTS)), dma((3, SLOTS)), dma((18,))],
             compiler_params=pltpu.CompilerParams(vmem_limit_bytes=VMEM_MAX - resident - SPARE),
             cost_estimate=pl.CostEstimate(flops=2000 * d_model * ff, bytes_accessed=48 * d_model * ff, transcendentals=4 * d_model * ff),
             name="update",
-        )(clip, learn_rate, w_up, m_up, v_up, stay(mean_up), w_down, m_down, v_down, stay(mean_down))
-
-        f_width = 2 * width
-        f_chunk = ff // f_width
+        )(clip, learn_rate, w_up, m_up, v_up, stay(mean_up), w_down, m_down, v_down, stay(mean_down), stay(held))
+
         y_next = pl.pallas_call(
             forward_kernel,
             out_shape=pltpu.VMEM(x_next.shape, BF16),
-            in_specs=[vmem, vmem, vmem, vmem],
+            in_specs=[hbm, hbm, vmem, vmem],
             out_specs=vmem,
             scratch_shapes=[
-                pltpu.VMEM((f_chunk, d_model, f_width), BF16),
-                pltpu.VMEM((ff, d_model), BF16),
                 pltpu.VMEM((rows, ff), BF16),
                 pltpu.VMEM((n_micro, rows, d_model), BF16),
                 pltpu.VMEM((n_micro, half, d_model), BF16),
                 pltpu.VMEM((n_micro, half, d_model), BF16),
                 pltpu.VMEM((n_micro, rows, d_model), F32),
                 pltpu.VMEM((n_micro, half, d_model), F32),
-                dma((n_micro, n_block)), dma((n_micro, n_block)), dma((n_micro, n_block)), dma((n_micro, n_block)),
+                dma((2,)), dma((n_micro, n_block)), dma((n_micro, n_block)), dma((n_micro, n_block)), dma((n_micro, n_block)),
                 dma((n_micro,)), dma((n_micro,)), dma((n_micro,)), dma((n_micro,)),
                 pltpu.SemaphoreType.REGULAR,
             ],

time: 682 us -> 677 us (level)
  no operation moved by 1% of the time
where the time goes in v8:
time: 677 us; the launch traced here: 676 us
  Pallas kernels  670 us (99%)
    pallas_call x1, Pallas kernels, device_step(): pl.pallas_call(functools.partial(grad_kernel, n_chunk, width), out_shape=...  613 us
    pallas_call x1, Pallas kernels, device_step(): pl.pallas_call(update_kernel, out_shape=(up_out, up_out, up_out, down_out...  52.6 us
  transfers between devices with their start and end apart: 2, of which 0 were waited for; matrix products, arithmetic and copies ran while one was open for 0% of the time, Pallas kernels for 8%

profile of v8, /device:TPU:0, one launch (start us, length us, event | category | flops | bytes accessed | tf_op | source)
XLA Modules:
  0.0 676.4 jit_solution(10431557726414214796)
XLA Ops:
  1.9 613.0 %grad_exchange.1 = (f32[20,1280,128]{2,1,0:T(8,128)S(1)}, f32[20,128,1280]{2,1,0:T(8,128)S(1)}, f32[20,1280,128]{2,1,0:T(8,128)S(1)}, f32[8,128]{1,0:T(8,128)}, bf16[3,128,1280]{2,1,0:T(8,128)(2,1)}) custom-call(f32[1280,2560]{1,0:T(8,128)} %bitcast.11, f32[2560,1280]{1,0:T(8,128)} %bitcast.12, f32[1280,2560]{1,0:T(8,128)} %bitcast.17, ...), custom_call_target="tpu_custom_call" | custom-call | tf_op jit(solution)/shard_map/grad_exchange/pallas_call | solution.py:554
  614.9 1.4 collective-permute-start
  616.3 1.5 collective-permute-start.1
  617.8 52.6 %update.1 = (f32[1,1280,2560]{2,1,0:T(8,128)}, f32[1,1280,2560]{2,1,0:T(8,128)}, f32[1,1280,2560]{2,1,0:T(8,128)}, f32[1,2560,1280]{2,1,0:T(8,128)}, f32[1,2560,...) custom-call(f32[8,128]{1,0:T(8,128)} %get-tuple-element.20.clip, ...), custom_call_target="tpu_custom_call", output_to_operand_aliasing={{6}: (5, {}), {7}: (9, {}), {8}: (10, {})} | custom-call | flops 6553600000 | bytes 157286400 | tf_op jit(solution)/shard_map/update/pallas_call | solution.py:591
  670.5 0.0 collective-permute-done.from_core
  670.5 0.0 collective-permute-done.1.from_diag
  670.5 4.7 forward_exchange.1
  675.2 1.3 copy.27
Async XLA Ops:
  614.9 55.5 %collective-permute-start = (bf16[3,128,1280]{2,1,0:T(8,128)(2,1)}, bf16[3,128,1280]{2,1,0:T(8,128)(2,1)S(1)}, u32[]{:S(2)}, u32[]{:S(2)}) collective-permute-start(bf16[3,128,1280]{2,1,0:T(8,128)(2,1)} %get-tuple-element.30), channel_id=1, source_target_pairs={{0,1},{4,5},{2,3},{6,7}} | collective-permute-start | bytes 2949128 | tf_op jit(solution)/shard_map/ppermute | solution.py:584
  616.3 54.2 %collective-permute-start.1 = (bf16[3,128,1280]{2,1,0:T(8,128)(2,1)}, bf16[3,128,1280]{2,1,0:T(8,128)(2,1)S(1)}, u32[]{:S(2)}, u32[]{:S(2)}) collective-permute-start(bf16[3,128,1280]{2,1,0:T(8,128)(2,1)} %get-tuple-element.30), channel_id=1, source_target_pairs={{0,5},{4,1},{2,7},{6,3}} | collective-permute-start | bytes 2949128 | tf_op jit(solution)/shard_map/ppermute | solution.py:583

commit v9 on v8

--- a/solution.py
+++ b/solution.py
@@ -6,6 +6,7 @@
 from jax.experimental import pallas as pl
 from jax.experimental.pallas import tpu as pltpu
 from jax.sharding import PartitionSpec as P
+
 
 ADAM_STEP = 10
 BETA_ONE = 0.9
@@ -332,58 +333,63 @@
         store.wait()
 
 
-def update_kernel(clip, rate, w1, m1, v1, gb1, w2, m2, v2, gb2, held, nw1, nm1, nv1, nw2, nm2, nv2, keep1, keep2, held_out, ring, in_sem, out_sem, held_sem):
-    n_up, deep, wide = gb1.shape
-    n_slot = ring.shape[1]
-    near = [(place, h) for place in range(3) for h in (0, 1)]
-    last = 2 * n_up - len(near)
-    block = deep // gb2.shape[1]
+def update_kernel(clip, rate, w1, m1, v1, gb1, w2, m2, v2, gb2, held, nw1, nm1, nv1, nw2, nm2, nv2, keep1, keep2, held_out,
+                  ring, in_sem, out_sem, held_sem):
+    _, deep, wide = gb1.shape
+    n_slot, tall, span = ring.shape[1:]
+    block = deep // tall
+    per_row = w1.shape[2] // span
+    n_up = per_row * (deep // tall)
+    n_down = w2.shape[1] // tall
+    last = n_up + n_down
     scale = clip[0, 0]
     step_rate = rate[0]
-
-    def place(i):
-        i = i + i // (last - 1)
-        col = pl.multiple_of(((i - n_up) // 2) * wide, wide)
-        row = pl.multiple_of(lax.rem(i - n_up, 2) * deep, deep)
-        return pl.ds(row, deep), pl.ds(col, wide)
-
-    def start(i, fetch):
+    kinds = ((0, n_up, span), (n_up, n_up + n_down // 2, 8 * wide), (n_up + n_down // 2, last, 6 * wide))
+
+    def copies(i, kind, fetch):
         slot = lax.rem(i, n_slot)
         sem = in_sem if fetch else out_sem
-
-        def go(k, far):
-            here = ring.at[k, slot]
-            pair = (far, here) if fetch else (here, far)
-            pltpu.make_async_copy(*pair, sem.at[k, slot]).start()
-
-        @pl.when(i < n_up)
-        def _():
-            cols = pl.ds(pl.multiple_of(i * wide, wide), wide)
-            for k, ref in enumerate((w1, m1, v1) if fetch else (nw1, nm1, nv1)):
-                go(k, ref.at[0, :, cols])
-
-        @pl.when(i >= n_up)
-        def _():
-            rows, cols = place(i)
-            for k, ref in enumerate((w2, m2, v2) if fetch else (nw2, nm2, nv2)):
-                go(k, ref.at[0, rows, cols])
+        cols = kinds[kind][2]
+        if kind == 0:
+            refs = (w1, m1, v1) if fetch else (nw1, nm1, nv1)
+            where = (0, pl.ds(pl.multiple_of(i // per_row * tall, tall), tall), pl.ds(pl.multiple_of(lax.rem(i, per_row) * span, span), span))
+        else:
+            refs = (w2, m2, v2) if fetch else (nw2, nm2, nv2)
+            where = (0, pl.ds(pl.multiple_of((i - n_up) * tall, tall), tall), slice(0, cols))
+        out = []
+        for k, ref in enumerate(refs):
+            pair = (ref.at[where], ring.at[k, slot, :, :cols])
+            out.append(pltpu.make_async_copy(*(pair if fetch else pair[::-1]), sem.at[k, slot]))
+        return out
+
+    def each(i, act):
+        if isinstance(i, int):
+            kind = [n for n, (lo, hi, _) in enumerate(kinds) if lo <= i < hi][0]
+            act(jnp.int32(i), kind)
+            return
+        for kind, (lo, hi, _) in enumerate(kinds):
+            @pl.when((i >= lo) & (i < hi))
+            def _():
+                act(i, kind)
+
+    def start(i, fetch):
+        def act(i, kind):
+            for copy in copies(i, kind, fetch):
+                copy.start()
+
+        each(i, act)
 
     def finish(i, fetch):
-        slot = lax.rem(i, n_slot)
-        for k, ref in enumerate((w2, m2, v2) if fetch else (nw2, nm2, nv2)):
-            far, here = ref.at[0, :deep, :wide], ring.at[k, slot]
-            sem = (in_sem if fetch else out_sem).at[k, slot]
-            (pltpu.make_async_copy(far, here, sem) if fetch else pltpu.make_async_copy(here, far, sem)).wait()
+        def act(i, kind):
+            for copy in copies(i, kind, fetch):
+                copy.wait()
+
+        each(i, act)
 
     for i in range(AHEAD):
-        start(jnp.int32(i), True)
-
-    def step(slot, mean):
-        new, mom, sec = adamw(scale, step_rate, ring[0, slot], ring[1, slot], ring[2, slot], mean)
-        ring[0, slot] = new
-        ring[1, slot] = mom
-        ring[2, slot] = sec
-        return new
+        start(i, True)
+
+    near = [(place, h) for place in range(3) for h in (0, 1)]
 
     def held_copies(place, h):
         col, upper = {2: (6, 1), 0: (8, 0), 1: (8, 1)}[place]
@@ -392,7 +398,7 @@
                              for k, ref in enumerate((nw2, nm2, nv2))]
 
     for spot, h in near:
-        upper, cols, copies = held_copies(spot, h)
+        upper, cols, moves = held_copies(spot, h)
         rows = slice(upper * block, (upper + 1) * block)
         base = 6 * spot + h
         new, mom, sec = adamw(scale, step_rate, held[base], held[base + 2], held[base + 4], gb2[rows, :, cols].reshape(deep, wide))
@@ -400,25 +406,31 @@
         held_out[base + 2] = mom
         held_out[base + 4] = sec
         keep2[rows, :, cols] = new.reshape(block, -1, wide)
-        for copy in copies:
+        for copy in moves:
             copy.start()
+
+    def step(slot, cols, mean):
+        new, mom, sec = adamw(scale, step_rate, ring[0, slot, :, cols], ring[1, slot, :, cols], ring[2, slot, :, cols], mean)
+        ring[0, slot, :, cols] = new
+        ring[1, slot, :, cols] = mom
+        ring[2, slot, :, cols] = sec
+        return new
+
+    def compute(i, kind):
+        slot = lax.rem(i, n_slot)
+        if kind == 0:
+            rows = pl.ds(pl.multiple_of(i // per_row * tall, tall), tall)
+            for t in range(span // wide):
+                col = lax.rem(i, per_row) * (span // wide) + t
+                keep1[col, rows] = step(slot, slice(t * wide, (t + 1) * wide), gb1[col, rows])
+        else:
+            cols = slice(0, kinds[kind][2])
+            keep2[i - n_up, :, cols] = step(slot, cols, gb2[i - n_up, :, cols])
 
     @pl.loop(0, last)
     def _(i):
-        slot = lax.rem(i, n_slot)
         finish(i, True)
-
-        @pl.when(i < n_up)
-        def _():
-            keep1[i] = step(slot, gb1[i])
-
-        @pl.when(i >= n_up)
-        def _():
-            cols = place(i)[1]
-            rows = pl.ds(lax.rem(i + i // (last - 1) - n_up, 2) * block, block)
-            new = step(slot, gb2[rows, :, cols].reshape(deep, wide))
-            keep2[rows, :, cols] = new.reshape(block, -1, wide)
-
+        each(i, compute)
         start(i, False)
 
         @pl.when(i + AHEAD < last)
@@ -426,10 +438,11 @@
             @pl.when(i + AHEAD - n_slot >= 0)
             def _():
                 finish(i + AHEAD - n_slot, False)
+
             start(i + AHEAD, True)
 
     for i in range(last - n_slot, last):
-        finish(jnp.int32(i), False)
+        finish(i, False)
     for spot, h in near:
         for copy in held_copies(spot, h)[2]:
             copy.wait()
@@ -595,7 +608,7 @@
             in_specs=[smem, smem, hbm, hbm, hbm, vmem, hbm, hbm, hbm, vmem, vmem],
             out_specs=(hbm,) * 6 + (vmem, vmem, vmem),
             input_output_aliases={5: 6, 9: 7, 10: 8},
-            scratch_shapes=[pltpu.VMEM((3, SLOTS, d_model, width), F32), dma((3, SLOTS)), dma((3, SLOTS)), dma((18,))],
+            scratch_shapes=[pltpu.VMEM((3, SLOTS, width, d_model), F32), dma((3, SLOTS)), dma((3, SLOTS)), dma((18,))],
             compiler_params=pltpu.CompilerParams(vmem_limit_bytes=VMEM_MAX - resident - SPARE),
             cost_estimate=pl.CostEstimate(flops=2000 * d_model * ff, bytes_accessed=48 * d_model * ff, transcendentals=4 * d_model * ff),
             name="update",

time: 677 us -> 675 us (level)
  no operation moved by 1% of the time
where the time goes in v9:
time: 675 us
  Pallas kernels  669 us (99%)
    pallas_call x1, Pallas kernels, device_step(): pl.pallas_call(functools.partial(grad_kernel, n_chunk, width), out_shape=...  613 us
    pallas_call x1, Pallas kernels, device_step(): pl.pallas_call(update_kernel, out_shape=(up_out, up_out, up_out, down_out...  51.2 us
  transfers between devices with their start and end apart: 2, of which 0 were waited for; matrix products, arithmetic and copies ran while one was open for 0% of the time, Pallas kernels for 8%

profile of v9, /device:TPU:0, one launch (start us, length us, event | category | flops | bytes accessed | tf_op | source)
XLA Modules:
  0.0 674.9 jit_solution(870949293455958674)
XLA Ops:
  1.9 612.9 %grad_exchange.1 = (f32[20,1280,128]{2,1,0:T(8,128)S(1)}, f32[20,128,1280]{2,1,0:T(8,128)S(1)}, f32[20,1280,128]{2,1,0:T(8,128)S(1)}, f32[8,128]{1,0:T(8,128)}, bf16[3,128,1280]{2,1,0:T(8,128)(2,1)}) custom-call(f32[1280,2560]{1,0:T(8,128)} %bitcast.11, f32[2560,1280]{1,0:T(8,128)} %bitcast.12, f32[1280,2560]{1,0:T(8,128)} %bitcast.17, ...), custom_call_target="tpu_custom_call" | custom-call | tf_op jit(solution)/shard_map/grad_exchange/pallas_call | solution.py:567
  614.9 1.4 collective-permute-start
  616.2 1.5 collective-permute-start.1
  617.8 51.2 %update.1 = (f32[1,1280,2560]{2,1,0:T(8,128)}, f32[1,1280,2560]{2,1,0:T(8,128)}, f32[1,1280,2560]{2,1,0:T(8,128)}, f32[1,2560,1280]{2,1,0:T(8,128)}, f32[1,2560,...) custom-call(f32[8,128]{1,0:T(8,128)} %get-tuple-element.20.clip, ...), custom_call_target="tpu_custom_call", output_to_operand_aliasing={{6}: (5, {}), {7}: (9, {}), {8}: (10, {})} | custom-call | flops 6553600000 | bytes 157286400 | tf_op jit(solution)/shard_map/update/pallas_call | solution.py:604
  669.0 0.0 collective-permute-done.from_core
  669.0 0.0 collective-permute-done.1.from_diag
  669.0 4.7 forward_exchange.1
  673.6 1.3 copy.27
Async XLA Ops:
  614.9 54.1 %collective-permute-start = (bf16[3,128,1280]{2,1,0:T(8,128)(2,1)}, bf16[3,128,1280]{2,1,0:T(8,128)(2,1)S(1)}, u32[]{:S(2)}, u32[]{:S(2)}) collective-permute-start(bf16[3,128,1280]{2,1,0:T(8,128)(2,1)} %get-tuple-element.30), channel_id=1, source_target_pairs={{0,1},{4,5},{2,3},{6,7}} | collective-permute-start | bytes 2949128 | tf_op jit(solution)/shard_map/ppermute | solution.py:597
  616.2 52.7 %collective-permute-start.1 = (bf16[3,128,1280]{2,1,0:T(8,128)(2,1)}, bf16[3,128,1280]{2,1,0:T(8,128)(2,1)S(1)}, u32[]{:S(2)}, u32[]{:S(2)}) collective-permute-start(bf16[3,128,1280]{2,1,0:T(8,128)(2,1)} %get-tuple-element.30), channel_id=1, source_target_pairs={{0,5},{4,1},{2,7},{6,3}} | collective-permute-start | bytes 2949128 | tf_op jit(solution)/shard_map/ppermute | solution.py:596

commit v10 on v9

--- a/solution.py
+++ b/solution.py
@@ -75,7 +75,7 @@
                 gr1, gr2, gs1, clip, act_half,
                 gs2, w1b, w2b, part, got, x_buf, sq1, sq2, sq_out, sq_in,
                 w_sem, g_sem, send1, send2, recv1, recv2, part_sem, gvec_sem, sq_send, sq_recv,
-                row_sem, act_sem, f_sem, rs_send, rs_recv):
+                row_sem, act_sem, f_sem, rs_send, rs_recv, out_sem):
     m, d, s = positions()
     peer_x = (m, 1 - d, s)
     peer_y = (1 - m, d, s)
@@ -186,10 +186,10 @@
 
         @pl.when(p >= n_up)
         def _():
-            rows = pl.ds(pl.multiple_of(lax.rem(p - n_up, 2) * d_model, d_model), d_model)
+            cols = pl.ds(pl.multiple_of((p - n_up) * width, width), width)
             for q, ref in enumerate((w2, m2, v2)):
                 for h in (0, 1):
-                    cols = pl.ds(pl.multiple_of((2 * ((p - n_up) // 2) + h) * width, width), width)
+                    rows = pl.ds(h * d_model, d_model)
                     pltpu.make_async_copy(ref.at[rows, cols], gs1.at[base + 2 * q + h], f_sem.at[base + 2 * q + h]).start()
 
     def arrive(p):
@@ -257,46 +257,33 @@
         n_micro = group // 2
         third = group // 2
         wide = 2 * width
-        n_block = d_model // wide
+        n_block = d_model // width
 
         def new_weights(p, means):
             base = lax.rem(p, 3) * 6
-            parts = [adamw(scale, step_rate, gs1[base + h], gs1[base + 2 + h], gs1[base + 4 + h], means[h])[0].astype(BF16) for h in (0, 1)]
-            return jnp.concatenate(parts, axis=1)
+            return [adamw(scale, step_rate, gs1[base + h], gs1[base + 2 + h], gs1[base + 4 + h], means[h])[0].astype(BF16) for h in (0, 1)]
 
         def up_pair(p):
-            new = new_weights(p, [gr1[2 * p], gr1[2 * p + 1]])
+            new = jnp.concatenate(new_weights(p, [gr1[2 * p], gr1[2 * p + 1]]), axis=1)
             act = gelu_parts(dot(x_buf[...].reshape(-1, d_model), new))[1].astype(BF16).astype(F32)
-            cols = pl.ds(pl.multiple_of(lax.rem(p, n_block) * wide, wide), wide)
-            gs2[pl.ds((p // n_block) * group, group), :, cols] = act.reshape(group, half, wide)
-
-        def down_pair(p, upper):
-            means = []
-            for h in (0, 1):
-                cols = pl.ds(pl.multiple_of((2 * ((p - n_up) // 2) + h) * width, width), width)
-                means.append(gr2[upper * n_up:(upper + 1) * n_up, :, cols].reshape(d_model, width))
-            new = new_weights(p, means)
+            cols = pl.ds(pl.multiple_of(lax.rem(p, n_up // 2) * wide, wide), wide)
+            gs2[pl.ds((p // (n_up // 2)) * group, group), :, cols] = act.reshape(group, half, wide)
+
+        def block(c):
+            return pl.ds(pl.multiple_of(c * width, width), width)
+
+        def down_pair(c):
+            new = new_weights(n_up + c, [gr2[h * n_up:(h + 1) * n_up, :, block(c)].reshape(d_model, width) for h in (0, 1)])
             for lo in range(0, group, third):
-                rows = gs2[upper * group + lo:upper * group + lo + third].reshape(-1, d_model).astype(BF16)
-                res = dot(rows, new).reshape(third, half, wide)
-                for g in range(third):
-                    spot = slice(g * wide, (g + 1) * wide)
-                    if upper:
-                        part[lo // third, :, spot] += res[g]
-                    else:
-                        part[lo // third, :, spot] = res[g]
-
-        def give_block(c):
-            cols = pl.ds(pl.multiple_of(c * wide, wide), wide)
-            for k in range(n_micro):
-                even, odd = [part[g // third, :, g % third * wide:(g % third + 1) * wide] for g in (2 * k, 2 * k + 1)]
-                gs2[2 * group + k, :, cols] = jnp.where(m == 0, even, odd)
-                gs2[2 * group + n_micro + k, :, cols] = jnp.where(m == 0, odd, even)
+                low, high = [dot(gs2[h * group + lo:h * group + lo + third].reshape(-1, d_model).astype(BF16), new[h]) for h in (0, 1)]
+                res = (low + high).reshape(third, half, width)
+                for g in range(lo, lo + third):
+                    other = m if g % 2 == 0 else 1 - m
+                    gs2[2 * group + g // 2 + n_micro * other, :, block(c)] = res[g - lo]
             block_copy(c).start()
 
         def block_copy(c):
-            cols = pl.ds(pl.multiple_of(c * wide, wide), wide)
-            return remote(gs2.at[2 * group + n_micro:2 * group + 2 * n_micro, :, cols], got.at[:, :, cols], rs_send.at[c], rs_recv.at[c], peer_y)
+            return remote(gs2.at[2 * group + n_micro:2 * group + 2 * n_micro, :, block(c)], got.at[:, :, block(c)], rs_send.at[c], rs_recv.at[c], peer_y)
 
         def ahead(p):
             @pl.when(p < n_pair)
@@ -313,24 +300,25 @@
 
         @pl.loop(0, n_block)
         def _(c):
-            for upper in (0, 1):
-                p = n_up + 2 * c + upper
-                arrive(p)
-                down_pair(p, upper)
-                ahead(p + 3)
-            give_block(c)
-
-        for c in range(n_block):
+            arrive(n_up + c)
+            down_pair(c)
+            ahead(n_up + c + 3)
+
+        def store(c):
+            return pltpu.make_async_copy(x_buf.at[:n_micro, :, block(c)], act_half.at[:, :, block(c)], out_sem.at[c])
+
+        @pl.loop(0, n_block)
+        def _(c):
             block_copy(c).wait_recv()
-            cols = slice(c * wide, (c + 1) * wide)
             for k in range(n_micro):
-                rows = x_buf[2 * k + m, :, cols].astype(F32)
-                x_buf[k, :, cols] = (rows + (gs2[2 * group + k, :, cols] + got[k, :, cols])).astype(BF16)
-        store = pltpu.make_async_copy(x_buf.at[:n_micro], act_half, row_sem)
-        store.start()
-        for c in range(n_block):
+                rows = x_buf[2 * k + m, :, block(c)].astype(F32)
+                x_buf[k, :, block(c)] = (rows + (gs2[2 * group + k, :, block(c)] + got[k, :, block(c)])).astype(BF16)
+            store(c).start()
+
+        @pl.loop(0, n_block)
+        def _(c):
             block_copy(c).wait_send()
-        store.wait()
+            store(c).wait()
 
 
 def update_kernel(clip, rate, w1, m1, v1, gb1, w2, m2, v2, gb2, held, nw1, nm1, nv1, nw2, nm2, nv2, keep1, keep2, held_out,
@@ -344,7 +332,9 @@
     last = n_up + n_down
     scale = clip[0, 0]
     step_rate = rate[0]
-    kinds = ((0, n_up, span), (n_up, n_up + n_down // 2, 8 * wide), (n_up + n_down // 2, last, 6 * wide))
+    n_held = 3
+    first_held = span // wide - n_held
+    kinds = ((0, n_up, span), (n_up, last, first_held * wide))
 
     def copies(i, kind, fetch):
         slot = lax.rem(i, n_slot)
@@ -389,17 +379,17 @@
     for i in range(AHEAD):
         start(i, True)
 
-    near = [(place, h) for place in range(3) for h in (0, 1)]
-
-    def held_copies(place, h):
-        col, upper = {2: (6, 1), 0: (8, 0), 1: (8, 1)}[place]
-        rows, cols = slice(upper * deep, (upper + 1) * deep), slice((col + h) * wide, (col + h + 1) * wide)
-        return upper, cols, [pltpu.make_async_copy(held_out.at[6 * place + 2 * k + h], ref.at[0, rows, cols], held_sem.at[6 * place + 2 * k + h])
-                             for k, ref in enumerate((nw2, nm2, nv2))]
+    near = [(spot, h) for spot in range(n_held) for h in (0, 1)]
+
+    def held_copies(spot, h):
+        col = first_held + (spot + 1) % n_held
+        rows, cols = slice(h * deep, (h + 1) * deep), slice(col * wide, (col + 1) * wide)
+        return cols, [pltpu.make_async_copy(held_out.at[6 * spot + 2 * k + h], ref.at[0, rows, cols], held_sem.at[6 * spot + 2 * k + h])
+                      for k, ref in enumerate((nw2, nm2, nv2))]
 
     for spot, h in near:
-        upper, cols, moves = held_copies(spot, h)
-        rows = slice(upper * block, (upper + 1) * block)
+        cols, moves = held_copies(spot, h)
+        rows = slice(h * block, (h + 1) * block)
         base = 6 * spot + h
         new, mom, sec = adamw(scale, step_rate, held[base], held[base + 2], held[base + 4], gb2[rows, :, cols].reshape(deep, wide))
         held_out[base] = new
@@ -444,7 +434,7 @@
     for i in range(last - n_slot, last):
         finish(i, False)
     for spot, h in near:
-        for copy in held_copies(spot, h)[2]:
+        for copy in held_copies(spot, h)[1]:
             copy.wait()
 
 
@@ -587,7 +577,7 @@
                 dma((2, 2)), dma((2, 2)),
                 dma((n_chunk,)), dma((n_chunk,)), dma((n_chunk,)), dma((n_chunk,)),
                 dma((2,)), dma((2,)), dma((3,)), dma((4,)),
-                dma(()), dma(()), dma((18,)), dma((n_block,)), dma((n_block,)),
+                dma(()), dma(()), dma((18,)), dma((2 * n_block,)), dma((2 * n_block,)), dma((2 * n_block,)),
             ],
             compiler_params=pltpu.CompilerParams(collective_id=0, has_side_effects=True, vmem_limit_bytes=VMEM_MAX - resident - SPARE),
             name="grad_exchange",

time: 675 us -> 678 us (level)
  no operation moved by 1% of the time
where the time goes in v10:
time: 678 us; the launch traced here: 677 us
  Pallas kernels  671 us (99%)
    pallas_call x1, Pallas kernels, device_step(): pl.pallas_call(functools.partial(grad_kernel, n_chunk, width), out_shape=...  615 us
    pallas_call x1, Pallas kernels, device_step(): pl.pallas_call(update_kernel, out_shape=(up_out, up_out, up_out, down_out...  51.2 us
  transfers between devices with their start and end apart: 2, of which 0 were waited for; matrix products, arithmetic and copies ran while one was open for 0% of the time, Pallas kernels for 8%

profile of v10, /device:TPU:0, one launch (start us, length us, event | category | flops | bytes accessed | tf_op | source)
XLA Modules:
  0.0 677.4 jit_solution(2087650111388712690)
XLA Ops:
  1.9 615.4 %grad_exchange.1 = (f32[20,1280,128]{2,1,0:T(8,128)S(1)}, f32[20,128,1280]{2,1,0:T(8,128)S(1)}, f32[20,1280,128]{2,1,0:T(8,128)S(1)}, f32[8,128]{1,0:T(8,128)}, bf16[3,128,1280]{2,1,0:T(8,128)(2,1)}) custom-call(f32[1280,2560]{1,0:T(8,128)} %bitcast.11, f32[2560,1280]{1,0:T(8,128)} %bitcast.12, f32[1280,2560]{1,0:T(8,128)} %bitcast.17, ...), custom_call_target="tpu_custom_call" | custom-call | tf_op jit(solution)/shard_map/grad_exchange/pallas_call | solution.py:557
  617.3 1.4 collective-permute-start
  618.7 1.5 collective-permute-start.1
  620.2 51.2 %update.1 = (f32[1,1280,2560]{2,1,0:T(8,128)}, f32[1,1280,2560]{2,1,0:T(8,128)}, f32[1,1280,2560]{2,1,0:T(8,128)}, f32[1,2560,1280]{2,1,0:T(8,128)}, f32[1,2560,...) custom-call(f32[8,128]{1,0:T(8,128)} %get-tuple-element.20.clip, ...), custom_call_target="tpu_custom_call", output_to_operand_aliasing={{6}: (5, {}), {7}: (9, {}), {8}: (10, {})} | custom-call | flops 6553600000 | bytes 157286400 | tf_op jit(solution)/shard_map/update/pallas_call | solution.py:594
  671.4 0.0 collective-permute-done.from_core
  671.5 0.0 collective-permute-done.1.from_diag
  671.5 4.7 forward_exchange.1
  676.1 1.3 copy.27
Async XLA Ops:
  617.3 54.1 %collective-permute-start = (bf16[3,128,1280]{2,1,0:T(8,128)(2,1)}, bf16[3,128,1280]{2,1,0:T(8,128)(2,1)S(1)}, u32[]{:S(2)}, u32[]{:S(2)}) collective-permute-start(bf16[3,128,1280]{2,1,0:T(8,128)(2,1)} %get-tuple-element.30), channel_id=1, source_target_pairs={{0,1},{4,5},{2,3},{6,7}} | collective-permute-start | bytes 2949128 | tf_op jit(solution)/shard_map/ppermute | solution.py:587
  618.7 52.8 %collective-permute-start.1 = (bf16[3,128,1280]{2,1,0:T(8,128)(2,1)}, bf16[3,128,1280]{2,1,0:T(8,128)(2,1)S(1)}, u32[]{:S(2)}, u32[]{:S(2)}) collective-permute-start(bf16[3,128,1280]{2,1,0:T(8,128)(2,1)} %get-tuple-element.30), channel_id=1, source_target_pairs={{0,5},{4,1},{2,7},{6,3}} | collective-permute-start | bytes 2949128 | tf_op jit(solution)/shard_map/ppermute | solution.py:586
